TPU v7x, 32 devices: a whole 2x2x4 slice. The times are simulated.
32 devices in a mesh: samples: 8 (over z, y), snps: 4 (over x, core).
Axes of the slice: x: 2, y: 2, z: 4, core: 2. Of those that a mesh axis runs over, the one named last changes fastest.
Arguments:
- genotype: int32 [4096, 1536], P('samples', 'snps'), may hold values from 0 to 2
- mask: int32 [4096, 1536], P('samples', 'snps'), may hold values 0 or 1
Outputs:
- blocks: float32 [4096, 2560], P('samples', 'snps')
All inputs are finite; a program needn't handle non-finite values. No bound on the sum of `mask` on one device may be relied on, other than what follows from the above.
Results may differ from a plain program's by a relative error of at most 0.0014.
Values may be sent and summed in bfloat16 or wider, within the bound.
No kernel may reach another device: no remote copies, remote signals or barrier semaphores. Data moves between devices by JAX's collectives and lax.ppermute only.
A program may use at most 128 MiB of HBM per device.

v0:
```python
import jax
import jax.numpy as jnp
from jax import lax
from jax.sharding import PartitionSpec as P


def passed_along(value, axis, steps):
    count = lax.axis_size(axis)
    pairs = [(source, (source + steps) % count) for source in range(count)]
    return lax.ppermute(value, axis, pairs)


def standardize(dosage, observed_mask, allele_sum, observed_sum):
    frequency = (allele_sum + 1.0) / (2.0 * observed_sum + 2.0)
    scaled = (
        observed_mask * (dosage - 2.0 * frequency) / jnp.sqrt(2.0 * frequency * (1.0 - frequency))
    )
    return scaled.astype(jnp.bfloat16)


def cross_block(own_rows, other_rows):
    return lax.dot_general(
        own_rows, other_rows, (((1,), (1,)), ((), ())), preferred_element_type=jnp.float32
    )


def place_block(target, block, offset):
    column = jnp.asarray(offset, jnp.int32) * block.shape[1]
    return lax.dynamic_update_slice(target, block, (jnp.int32(0), column))


def per_device(genotype, mask):
    dosage = genotype.astype(jnp.float32)
    observed_mask = mask.astype(jnp.float32)
    allele_sum, observed_sum = lax.psum(
        (jnp.sum(dosage * observed_mask, axis=0), jnp.sum(observed_mask, axis=0)), "samples"
    )
    standard = standardize(dosage, observed_mask, allele_sum, observed_sum)
    circle_size = lax.axis_size("samples")
    snp_parts = lax.axis_size("snps")
    block_rows = standard.shape[0]
    offsets = circle_size // 2 + 1
    snp_total = standard.shape[1] * snp_parts
    strip = jnp.zeros((block_rows, offsets * block_rows), jnp.float32)
    strip = place_block(strip, cross_block(standard, standard), 0)

    def advance(turn_index, carry):
        strip_now, holding = carry
        for second in range(2):
            holding = passed_along(holding, "samples", -1)
            strip_now = place_block(
                strip_now, cross_block(standard, holding), 2 * turn_index + second + 1
            )
        return (strip_now, holding)

    strip, holding_last = lax.fori_loop(0, circle_size // 4, advance, (strip, standard))
    summed = lax.psum_scatter(strip, "snps", scatter_dimension=1, tiled=True)
    return summed / snp_total


def solution(mesh):
    return jax.shard_map(
        per_device,
        mesh=mesh,
        in_specs=(P("samples", "snps"), P("samples", "snps")),
        out_specs=P("samples", "snps"),
        check_vma=False,
    )
```

profile of v0, /device:TPU:0, one launch (start us, length us, event | category | flops | bytes accessed | tf_op | source)
XLA Modules:
  0.0 140.4 jit_solution(3592213365028404441)
XLA Ops:
  6.5 0.0 reduce-scatter.2.cloned.1.call-start
  6.5 1.5 %multiply_reduce_fusion = (f32[384]{0:T(512)S(1)}, f32[384]{0:T(512)S(1)}) fusion(s32[512,384]{1,0:T(8,128)} %param.4, s32[512,384]{1,0:T(8,128)} %param.5), kind=kLoop, calls=%fused_computation.3 | loop fusion | flops 982272 | bytes 1575936 | tf_op jit(solution)/shard_map/reduce_sum | solution.py:36
  8.1 23.1 %all-reduce.1 = (f32[384]{0:T(512)S(1)}, f32[384]{0:T(512)S(1)}) all-reduce(f32[384]{0:T(512)S(1)} %get-tuple-element.117, f32[384]{0:T(512)S(1)} %get-tuple-element.116), channel_id=1, replica_groups=mesh['samples'=8,'snps'=4] {'samples'}, use_global_device_ids=true, to_apply=%region_3.0 | all-reduce | flops 768 | bytes 6144 | tf_op jit(solution)/shard_map/psum | solution.py:35
  31.2 1.5 %divide_convert_fusion = bf16[512,384]{1,0:T(8,128)(2,1)S(1)} fusion(s32[512,384]{1,0:T(8,128)} %param.4, s32[512,384]{1,0:T(8,128)} %param.5, f32[384]{0:T(512)S(1)} %multiply_sqrt_fusion, f32[384]{0:T(512)S(1)} %get-tuple-element.128), kind=kLoop, calls=%fused_computation.2 | loop fusion | flops 1179648 | bytes 1969152 | tf_op jit(solution)/shard_map/convert_element_type | solution.py:18
  32.8 0.5 fusion
  33.3 3.0 %dynamic_update_slice.23 = f32[512,2560]{1,0:T(8,128)} pad(f32[512,512]{1,0:T(8,128)S(1)} %fusion, f32[]{:T(128)} %constant.62.clone.1), padding=0_0x0_2048 | pad | bytes 6291460 | tf_op jit(solution)/shard_map/dynamic_update_slice | solution.py:29
  36.3 42.4 %while.17 = (s32[]{:T(128)}, f32[512,2560]{1,0:T(8,128)}, bf16[512,384]{1,0:T(8,128)(2,1)S(1)}, bf16[512,384]{1,0:T(8,128)(2,1)S(1)}, s32[]{:T(128)}, /*index=5*/s32[]{:T(128)}, s32[]{:T(128)}, s32[]{:T(128)}, s32[]{:T(128)}) while((s32[]{:T(128)}, f32[512,2560]{1,0:T(8,128)}, bf16[512,384]{1,0:T(8,128)(2,1)S(1)}, ...), condition=%wide.region_5.0_spmd, body=%wide.region_4.0_spmd.sunk | while | flops 402653184 | bytes 6816053 | solution.py:56
  36.3 0.0 collective-permute-start
  36.3 10.2 %collective-permute-done = bf16[512,384]{1,0:T(8,128)(2,1)S(1)} collective-permute-done((bf16[512,384]{1,0:T(8,128)(2,1)S(1)}, bf16[512,384]{1,0:T(8,128)(2,1)S(1)}, u32[]{:S(2)}, u32[]{:S(2)}) %collective-permute-start) | collective-permute-done | bytes 393248 | tf_op jit(solution)/shard_map/while/body/eval_jaxpr/ppermute | solution.py:10
  46.5 0.2 collective-permute-start.1
  46.7 1.5 %convolution_dynamic-update-slice_fusion.4 = f32[512,2560]{1,0:T(8,128)} fusion(f32[512,2560]{1,0:T(8,128)} %get-tuple-element.165, s32[]{:T(128)S(6)} %select_n.22, bf16[512,384]{1,0:T(8,128)(2,1)S(1)} %get-tuple-element.176, bf16[512,384]{1,0:T(8,128)(2,1)S(1)} %collective-permute-done), kind=kOutput, calls=%fused_computation.1.clone.1 | convolution fusion | flops 201326592 | bytes 1835012 | tf_op jit(solution)/shard_map/while/body/eval_jaxpr/dot_general | solution.py:22
  48.3 8.2 %collective-permute-done.1 = bf16[512,384]{1,0:T(8,128)(2,1)S(1)} collective-permute-done((bf16[512,384]{1,0:T(8,128)(2,1)S(1)}, bf16[512,384]{1,0:T(8,128)(2,1)S(1)}, u32[]{:S(2)}, u32[]{:S(2)}) %collective-permute-start.1) | collective-permute-done | bytes 393248 | tf_op jit(solution)/shard_map/while/body/eval_jaxpr/ppermute | solution.py:10
  56.4 1.5 %convolution_dynamic-update-slice_fusion.5 = f32[512,2560]{1,0:T(8,128)} fusion(f32[512,2560]{1,0:T(8,128)} %convolution_dynamic-update-slice_fusion.4, s32[]{:T(128)S(6)} %select_n.23, bf16[512,384]{1,0:T(8,128)(2,1)S(1)} %get-tuple-element.176, bf16[512,384]{1,0:T(8,128)(2,1)S(1)} %collective-permute-done.1), kind=kOutput, calls=%fused_computation.clone.1 | convolution fusion | flops 201326592 | bytes 1835012 | tf_op jit(solution)/shard_map/while/body/eval_jaxpr/dot_general | solution.py:22
  57.9 0.8 collective-permute-start
  58.7 10.6 %collective-permute-done = bf16[512,384]{1,0:T(8,128)(2,1)S(1)} collective-permute-done((bf16[512,384]{1,0:T(8,128)(2,1)S(1)}, bf16[512,384]{1,0:T(8,128)(2,1)S(1)}, u32[]{:S(2)}, u32[]{:S(2)}) %collective-permute-start) | collective-permute-done | bytes 393248 | tf_op jit(solution)/shard_map/while/body/eval_jaxpr/ppermute | solution.py:10
  69.4 1.6 %collective-permute-start.1 = (bf16[512,384]{1,0:T(8,128)(2,1)S(1)}, bf16[512,384]{1,0:T(8,128)(2,1)S(1)}, u32[]{:S(2)}, u32[]{:S(2)}) collective-permute-start(bf16[512,384]{1,0:T(8,128)(2,1)S(1)} %collective-permute-done), channel_id=1, source_target_pairs={{0,28},{4,0},{8,4},{12,8},{16,12},{20,16},{24,20},{28,24},{1,29},{... | collective-permute-start | bytes 1179656 | tf_op jit(solution)/shard_map/while/body/eval_jaxpr/ppermute | solution.py:10
  71.0 1.5 %convolution_dynamic-update-slice_fusion.4 = f32[512,2560]{1,0:T(8,128)} fusion(f32[512,2560]{1,0:T(8,128)} %get-tuple-element.165, s32[]{:T(128)S(6)} %select_n.22, bf16[512,384]{1,0:T(8,128)(2,1)S(1)} %get-tuple-element.176, bf16[512,384]{1,0:T(8,128)(2,1)S(1)} %collective-permute-done), kind=kOutput, calls=%fused_computation.1.clone.1 | convolution fusion | flops 201326592 | bytes 1835012 | tf_op jit(solution)/shard_map/while/body/eval_jaxpr/dot_general | solution.py:22
  72.5 4.6 %collective-permute-done.1 = bf16[512,384]{1,0:T(8,128)(2,1)S(1)} collective-permute-done((bf16[512,384]{1,0:T(8,128)(2,1)S(1)}, bf16[512,384]{1,0:T(8,128)(2,1)S(1)}, u32[]{:S(2)}, u32[]{:S(2)}) %collective-permute-start.1) | collective-permute-done | bytes 393248 | tf_op jit(solution)/shard_map/while/body/eval_jaxpr/ppermute | solution.py:10
  77.1 1.5 %convolution_dynamic-update-slice_fusion.5 = f32[512,2560]{1,0:T(8,128)} fusion(f32[512,2560]{1,0:T(8,128)} %convolution_dynamic-update-slice_fusion.4, s32[]{:T(128)S(6)} %select_n.23, bf16[512,384]{1,0:T(8,128)(2,1)S(1)} %get-tuple-element.176, bf16[512,384]{1,0:T(8,128)(2,1)S(1)} %collective-permute-done.1), kind=kOutput, calls=%fused_computation.clone.1 | convolution fusion | flops 201326592 | bytes 1835012 | tf_op jit(solution)/shard_map/while/body/eval_jaxpr/dot_general | solution.py:22
  78.6 0.0 reduce-scatter.2.cloned.1.call-update
  78.6 52.4 %reduce-scatter.2.cloned.1.call-done = f32[512,640]{1,0:T(8,128)} async-done(((f32[512,2560]{1,0:T(8,128)}), f32[512,640]{1,0:T(8,128)}) %reduce-scatter.2.cloned.1.call-update) | async-done | bytes 1310736 | tf_op jit(solution)/shard_map/reduce_scatter | solution.py:57
  131.0 2.5 %broadcast_multiply_fusion = f32[512,640]{1,0:T(8,128)} fusion(f32[512,640]{1,0:T(8,128)} %reduce-scatter.2.cloned.1.call-done), kind=kLoop, calls=%fused_computation.5 | loop fusion | flops 327680 | bytes 2621440 | tf_op jit(solution)/shard_map/div | solution.py:58
  (3 shorter events, 0.1 us)
Async XLA Ops:
  6.5 124.5 %reduce-scatter.2.cloned.1.call-start = ((), (), s32[]{:S(2)}) async-start(), calls=%async_computation.1 | async-start | bytes 6553600 | tf_op jit(solution)/shard_map/reduce_scatter | solution.py:57
  36.3 10.3 %collective-permute-start = (bf16[512,384]{1,0:T(8,128)(2,1)S(1)}, bf16[512,384]{1,0:T(8,128)(2,1)S(1)}, u32[]{:S(2)}, u32[]{:S(2)}) collective-permute-start(bf16[512,384]{1,0:T(8,128)(2,1)S(1)} %get-tuple-element.166), channel_id=1, source_target_pairs={{0,28},{4,0},{8,4},{12,8},{16,12},{20,16},{24,20},{28,24},{1,29},{... | collective-permute-start | bytes 1179656 | tf_op jit(solution)/shard_map/while/body/eval_jaxpr/ppermute | solution.py:10
  46.5 9.9 %collective-permute-start.1 = (bf16[512,384]{1,0:T(8,128)(2,1)S(1)}, bf16[512,384]{1,0:T(8,128)(2,1)S(1)}, u32[]{:S(2)}, u32[]{:S(2)}) collective-permute-start(bf16[512,384]{1,0:T(8,128)(2,1)S(1)} %collective-permute-done), channel_id=1, source_target_pairs={{0,28},{4,0},{8,4},{12,8},{16,12},{20,16},{24,20},{28,24},{1,29},{... | collective-permute-start | bytes 1179656 | tf_op jit(solution)/shard_map/while/body/eval_jaxpr/ppermute | solution.py:10
  57.9 11.4 %collective-permute-start = (bf16[512,384]{1,0:T(8,128)(2,1)S(1)}, bf16[512,384]{1,0:T(8,128)(2,1)S(1)}, u32[]{:S(2)}, u32[]{:S(2)}) collective-permute-start(bf16[512,384]{1,0:T(8,128)(2,1)S(1)} %get-tuple-element.166), channel_id=1, source_target_pairs={{0,28},{4,0},{8,4},{12,8},{16,12},{20,16},{24,20},{28,24},{1,29},{... | collective-permute-start | bytes 1179656 | tf_op jit(solution)/shard_map/while/body/eval_jaxpr/ppermute | solution.py:10
  69.4 7.8 %collective-permute-start.1 = (bf16[512,384]{1,0:T(8,128)(2,1)S(1)}, bf16[512,384]{1,0:T(8,128)(2,1)S(1)}, u32[]{:S(2)}, u32[]{:S(2)}) collective-permute-start(bf16[512,384]{1,0:T(8,128)(2,1)S(1)} %collective-permute-done), channel_id=1, source_target_pairs={{0,28},{4,0},{8,4},{12,8},{16,12},{20,16},{24,20},{28,24},{1,29},{... | collective-permute-start | bytes 1179656 | tf_op jit(solution)/shard_map/while/body/eval_jaxpr/ppermute | solution.py:10
Sparse Core Ops, SparseCore 0:
  78.8 52.2 reduce-scatter.1
where the time goes:
time: 141 us; the launch traced here: 140 us
  waiting for transfers between devices  86.1 us (61%)
  blocking collectives  23.1 us (16%)
  between operations  13.4 us (10%)
  matrix products  6.47 us (5%)
  other arithmetic  5.56 us (4%)
  local copies, waits for them, and re-layouts  3.03 us (2%)
  starting transfers between devices  2.67 us (2%)
    reduce_scatter x1, waiting for transfers between devices, per_device(): summed = lax.psum_scatter(strip, 'snps', scatter_dimension=1, tiled=True)  52.4 us
    ppermute x4, waiting for transfers between devices, passed_along(): return lax.ppermute(value, axis, pairs)  33.7 us
    psum x1, blocking collectives, per_device(): lax.psum((jnp.sum(dosage * observed_mask, axis=0), jnp.sum(observed_mask,...  23.1 us
    dot_general x5, matrix products, cross_block(): lax.dot_general(own_rows, other_rows, (((1,), (1,)), ((), ())), preferred...  6.47 us
    dynamic_update_slice x1, local copies, waits for them, and re-layouts, place_block(): return lax.dynamic_update_slice(target, block, (jnp.int32(0), column))  2.98 us
  transfers between devices with their start and end apart: 5, of which 5 were waited for; matrix products, arithmetic and copies ran while one was open for 2% of the time, Pallas kernels for 0%

commit v1 on v0

v1 whole, which is shorter than its diff:
```python
import functools
import math

import jax
import jax.numpy as jnp
from jax import lax
from jax.experimental import pallas as pl
from jax.experimental.pallas import tpu as pltpu
from jax.sharding import PartitionSpec as P


def send(value, axis, route):
    count = lax.axis_size(axis)
    pairs = [(source, route(source)) for source in range(count)]
    return lax.ppermute(value, axis, [pair for pair in pairs if pair[1] is not None])


def swap_core(value):
    return send(value, "snps", lambda s: s ^ 1)


def arrival(piece):
    k, half = piece
    return k + 0.5 * half + (1.6 if k % 2 else 0.0)


def strips(samples):
    whole_count = (samples + 2) // 4
    result = []
    for strip in range(4):
        first = strip * (samples + 2) // 4
        begin = first + strip % 2
        wholes = [divmod(begin + n, 2) for n in range(whole_count)]
        cut = divmod(first if strip % 2 else first + whole_count, 2)
        result.append((sorted(wholes, key=arrival), wholes, cut))
    return result


def call_kernel(body, shapes, operands, specs, flops, moved, **more):
    return pl.pallas_call(
        body,
        out_shape=shapes,
        in_specs=specs,
        compiler_params=pltpu.CompilerParams(vmem_limit_bytes=24 * 2**20),
        cost_estimate=pl.CostEstimate(flops=flops, bytes_accessed=moved, transcendentals=0),
        **more,
    )(*operands)


VMEM = pl.BlockSpec(memory_space=pltpu.VMEM)
SMEM = pl.BlockSpec(memory_space=pltpu.SMEM)
ANY = pl.BlockSpec(memory_space=pl.ANY)


def encode_body(genotype_ref, mask_ref, whole_ref, first_ref, second_ref, sums_ref):
    half = pl.program_id(0)
    mask = mask_ref[...]
    dosage = mask * genotype_ref[...]
    calls = (dosage + mask).astype(jnp.float32).astype(jnp.bfloat16)
    whole_ref[...] = calls

    @pl.when(half == 0)
    def _():
        first_ref[...] = calls
        sums_ref[...] = jnp.zeros_like(sums_ref)

    @pl.when(half == 1)
    def _():
        second_ref[...] = calls

    sums_ref[0:1, :] += jnp.sum(dosage.astype(jnp.float32), axis=0, keepdims=True)
    sums_ref[1:2, :] += jnp.sum(mask.astype(jnp.float32), axis=0, keepdims=True)


def encode(genotype, mask):
    rows, columns = genotype.shape
    half = rows // 2
    calls = lambda n: jax.ShapeDtypeStruct((n, columns), jnp.bfloat16)
    block = pl.BlockSpec((half, columns), lambda i: (i, 0))
    fixed = lambda n: pl.BlockSpec((n, columns), lambda i: (0, 0))
    return pl.pallas_call(
        encode_body,
        name="encode",
        grid=(2,),
        out_shape=(calls(rows), calls(half), calls(half), jax.ShapeDtypeStruct((2, columns), jnp.float32)),
        in_specs=[block, block],
        out_specs=(block, fixed(half), fixed(half), fixed(2)),
        compiler_params=pltpu.CompilerParams(vmem_limit_bytes=16 * 2**20),
    )(genotype, mask)


def factors(sums):
    frequency = (sums[0:1] + 1.0) / (2.0 * sums[1:2] + 2.0)
    return 1.0 + 2.0 * frequency, 1.0 / jnp.sqrt(2.0 * frequency * (1.0 - frequency))


def standardized(calls, shift, scale):
    wide = calls.astype(jnp.float32)
    return jnp.where(wide > 0.0, (wide - shift) * scale, 0.0).astype(jnp.bfloat16)


def left_body(calls_ref, other_ref, sums_ref, other_sums_ref, left_ref, shift_ref, scale_ref):
    part = calls_ref.shape[1]
    for n, (rows_ref, counts_ref) in enumerate(((calls_ref, sums_ref), (other_ref, other_sums_ref))):
        shift, scale = factors(counts_ref[...])
        shift_ref[:, pl.ds(n * part, part)] = shift
        scale_ref[:, pl.ds(n * part, part)] = scale
        left_ref[:, pl.ds(n * part, part)] = standardized(rows_ref[...], shift, scale)


def fill_right(choice, parity, cases, refs, shift_ref, scale_ref, right_ref):
    part = refs[0].shape[1]
    for strip, by_parity in enumerate(cases):
        for odd, (at, begin) in enumerate(by_parity):
            same = by_parity[0] == by_parity[1]
            if odd and same:
                continue
            wanted = choice == strip if same else (choice == strip) & (parity == odd)

            @pl.when(wanted)
            def _(at=at, begin=begin):
                for n in range(2):
                    columns = pl.ds(n * part, part)
                    right_ref[:, columns] = standardized(
                        refs[at + n][pl.ds(begin, right_ref.shape[0]), :],
                        shift_ref[:, columns], scale_ref[:, columns],
                    )


def multiply(left, right):
    return lax.dot_general(
        left, right, (((1,), (1,)), ((), ())), preferred_element_type=jnp.float32
    )


def theirs_body(cases, down, where_ref, left_ref, shift_ref, scale_ref, *rest):
    *refs, out_ref, right_ref = rest
    fill_right(where_ref[0], where_ref[1], cases, refs, shift_ref, scale_ref, right_ref)
    out_ref[...] = multiply(left_ref[...], right_ref[...]) * down


def ours_body(cases, places, up, first, where_ref, left_ref, shift_ref, scale_ref, got_ref, *rest):
    *refs, out_ref, right_ref, total_ref, sem = rest
    if not first:
        refs = refs[:-1]
    fill_right(where_ref[0], where_ref[1], cases, refs, shift_ref, scale_ref, right_ref)
    ours = multiply(left_ref[...], right_ref[...])
    total_ref[...] = ours * up[0] + got_ref[...] * up[1]
    width = total_ref.shape[1]
    for strip, begin in enumerate(places):

        @pl.when(where_ref[0] == strip)
        def _(begin=begin):
            copy = pltpu.make_async_copy(total_ref, out_ref.at[:, pl.ds(begin, width)], sem)
            copy.start()
            copy.wait()


def per_device(genotype, mask):
    samples = lax.axis_size("samples")
    parts = lax.axis_size("snps")
    assert samples % 4 == 0 and samples & (samples - 1) == 0 and parts == 4
    rows, snp_part = genotype.shape
    snp_total = snp_part * parts
    turns = samples // 4
    half_rows = rows // 2
    width = rows * (samples // 2 + 1) // parts

    calls, first, second, sums = encode(genotype, mask)

    along = lambda s: (s - 2) % samples
    line = [[first, second]]
    for _ in range(1, turns + 1):
        line.append([send(line[-1][h], "samples", along) for h in range(2)])
    beside = send(calls, "samples", lambda s: s - 1 if s % 2 else None)
    side = [None]
    for t in range(1, turns):
        side.append([send(line[t][h], "samples", lambda s: s ^ 1) for h in range(2)])
    side.append([send(line[turns][h], "samples", lambda s: None if s % 2 else s + 1) for h in range(2)])

    for bit in range(samples.bit_length() - 1):
        sums = sums + send(sums, "samples", lambda s, step=1 << bit: s ^ step)
    other_sums = swap_core(sums)

    both = {("own", None): (calls, swap_core(calls)), ("y", 0): (beside, swap_core(beside))}
    for t in range(1, turns + 1):
        for h in range(2):
            both["z", t, h] = (line[t][h], swap_core(line[t][h]))
            both["y", t, h] = (side[t][h], swap_core(side[t][h]))

    def source(k, h, odd):
        if k == 0:
            return ("own", None), h * half_rows
        if k % 2 == 0:
            return ("z", k // 2, h), 0
        if k == 1 and not odd:
            return ("y", 0), h * half_rows
        return ("y", (k + odd) // 2, h), 0

    part = snp_part
    line_shape = jax.ShapeDtypeStruct((1, 2 * part), jnp.float32)
    left, shift, scale = call_kernel(
        left_body,
        (jax.ShapeDtypeStruct((rows, 2 * part), jnp.bfloat16), line_shape, line_shape),
        (*both["own", None], sums, other_sums), [VMEM] * 4, 10 * rows * part, 4 * rows * part,
        out_specs=(VMEM, VMEM, VMEM),
    )

    device = lax.axis_index("snps").astype(jnp.int32)
    parity = (lax.axis_index("samples") % 2).astype(jnp.int32)
    table = strips(samples)
    bound = snp_total / 2 * 4 * (samples * rows + 1) / 3
    down = 2.0 ** -math.ceil(math.log2(bound / 32768.0))
    count = len(table[0][0])
    quarter = half_rows // 2

    def gather(n):
        keys, cases, places = [], [], []
        for strip, (by_arrival, natural, cut) in enumerate(table):
            piece = by_arrival[n] if n < count else cut
            by_parity = []
            for odd in range(2):
                key, begin = source(*piece, odd)
                if key not in keys:
                    keys.append(key)
                if n == count and strip % 2:
                    begin += quarter
                by_parity.append((2 * keys.index(key), begin))
            cases.append(tuple(by_parity))
            if n < count:
                places.append(natural.index(piece) * half_rows + (strip % 2) * quarter)
            else:
                places.append(0 if strip % 2 else count * half_rows)
        return [array for key in keys for array in both[key]], tuple(cases), tuple(places)

    out = None
    pieces = []
    for n in range(count + 1):
        arrays, cases, places = gather(n)
        columns = half_rows if n < count else quarter
        flops = 2 * rows * 2 * part * columns
        right = pltpu.VMEM((columns, 2 * part), jnp.bfloat16)
        theirs = call_kernel(
            functools.partial(theirs_body, cases, down),
            jax.ShapeDtypeStruct((rows, columns), jnp.float32),
            (jnp.stack([device ^ 2, parity]), left, shift, scale, *arrays),
            [SMEM] + [VMEM] * (3 + len(arrays)), flops, 2 * rows * columns,
            out_specs=VMEM, scratch_shapes=[right],
        )
        got = send(theirs.astype(jnp.float16), "snps", lambda s: s ^ 2)
        pieces.append((arrays, cases, places, columns, flops, right, got))
    for n, (arrays, cases, places, columns, flops, right, got) in enumerate(pieces):
        last = () if out is None else (out,)
        operands = (jnp.stack([device, parity]), left, shift, scale, got.astype(jnp.float32), *arrays, *last)
        out = call_kernel(
            functools.partial(ours_body, cases, places, (1.0 / snp_total, 1.0 / (down * snp_total)), n == 0),
            jax.ShapeDtypeStruct((rows, width), jnp.float32), operands,
            [SMEM] + [VMEM] * (4 + len(arrays)) + [ANY] * len(last), flops, 4 * rows * columns,
            out_specs=ANY,
            scratch_shapes=[right, pltpu.VMEM((rows, columns), jnp.float32), pltpu.SemaphoreType.DMA],
            input_output_aliases={len(operands) - 1: 0} if last else {},
        )
    return out


def solution(mesh):
    return jax.shard_map(
        per_device,
        mesh=mesh,
        in_specs=(P("samples", "snps"), P("samples", "snps")),
        out_specs=P("samples", "snps"),
        check_vma=False,
    )
```

time: 141 us -> 77.9 us (0.55)
  waiting for transfers between devices: 86.1 us -> 34.4 us
  starting transfers between devices: 2.67 us -> 27.9 us
  blocking collectives: 23.1 us -> 0 us
  between operations: 13.4 us -> 0.19 us
  Pallas kernels: 0 us -> 10.9 us
  matrix products: 6.47 us -> 0 us
  other arithmetic: 5.56 us -> 0.35 us
    reduce_scatter x1 -> x0, waiting for transfers between devices: 52.4 us -> none  [per_device(): summed = lax.psum_scatter(strip, 'snps', scatter_dimension=1, tiled=True)]
    ppermute x4 -> x26, starting transfers between devices: 2.66 us -> 27.9 us  [send(): lax.ppermute(value, axis, [pair for pair in pairs if pair[1] is not None])]
    psum x1 -> x0, blocking collectives: 23.1 us -> none  [per_device(): lax.psum((jnp.sum(dosage * observed_mask, axis=0), jnp.sum(observed_mask,...]
    pallas_call x0 -> x8, Pallas kernels: none -> 10.9 us  [the longest x7 10.6 us: call_kernel(): pl.pallas_call(body, out_shape=shapes, in_specs=specs, compiler_params=pl...]
    dot_general x5 -> x0, matrix products: 6.47 us -> none  [cross_block(): lax.dot_general(own_rows, other_rows, (((1,), (1,)), ((), ())), preferred...]
    unnamed x1 -> x8, local copies, waits for them, and re-layouts: 0.04 us -> 3.86 us
    dynamic_update_slice x1 -> x0, local copies, waits for them, and re-layouts: 2.98 us -> none  [place_block(): return lax.dynamic_update_slice(target, block, (jnp.int32(0), column))]
    div x1 -> x0, other arithmetic: 2.48 us -> none  [per_device(): return summed / snp_total]
  transfers between devices with their start and end apart: 5 -> 26, of which waited for: 5 -> 11; matrix products, arithmetic and copies ran while one was open for 2% -> 0% of each run, Pallas kernels for 0% -> 8%
where the time goes in v1:
time: 77.9 us; the launch traced here: 77.5 us
  waiting for transfers between devices  34.4 us (44%)
  starting transfers between devices  27.9 us (36%)
  Pallas kernels  10.9 us (14%)
  local copies, waits for them, and re-layouts  3.86 us (5%)
    ppermute x26, waiting for transfers between devices, send(): lax.ppermute(value, axis, [pair for pair in pairs if pair[1] is not None])  34.4 us
    ppermute x26, starting transfers between devices, send(): lax.ppermute(value, axis, [pair for pair in pairs if pair[1] is not None])  27.9 us
    pallas_call x7, Pallas kernels, call_kernel(): pl.pallas_call(body, out_shape=shapes, in_specs=specs, compiler_params=pl...  10.6 us
    unnamed x8, local copies, waits for them, and re-layouts  3.86 us
  transfers between devices with their start and end apart: 26, of which 11 were waited for; matrix products, arithmetic and copies ran while one was open for 0% of the time, Pallas kernels for 8%

profile of v1, /device:TPU:0, one launch (start us, length us, event | category | flops | bytes accessed | tf_op | source)
XLA Modules:
  0.0 77.5 jit_solution(7551926773808792067)
XLA Ops:
  0.0 1.1 %copy-done.2 = s32[512,384]{1,0:T(8,128)S(1)} copy-done((s32[512,384]{1,0:T(8,128)S(1)}, s32[512,384]{1,0:T(8,128)}, u32[]{:S(2)}) %copy-start.2) | copy-done | bytes 786456
  1.1 1.1 %copy-done.3 = s32[512,384]{1,0:T(8,128)S(1)} copy-done((s32[512,384]{1,0:T(8,128)S(1)}, s32[512,384]{1,0:T(8,128)}, u32[]{:S(2)}) %copy-start.3) | copy-done | bytes 786456
  2.3 0.4 encode.1
  2.6 0.6 collective-permute-start
  3.2 4.7 %collective-permute-start.7 = (bf16[256,384]{1,0:T(8,128)(2,1)S(1)}, bf16[256,384]{1,0:T(8,128)(2,1)S(1)}, u32[]{:S(2)}, u32[]{:S(2)}) collective-permute-start(bf16[256,384]{1,0:T(8,128)(2,1)S(1)} %get-tuple-element.17), channel_id=1, source_target_pairs={{0,24},{4,28},{8,0},{12,4},{16,8},{20,12},{24,16},{28,20},{1,25},{... | collective-permute-start | bytes 589832 | tf_op jit(solution)/shard_map/ppermute | solution.py:15
  7.8 0.4 collective-permute-start.10
  8.3 1.3 %collective-permute-start.5 = (bf16[512,384]{1,0:T(8,128)(2,1)S(1)}, bf16[512,384]{1,0:T(8,128)(2,1)S(1)}, u32[]{:S(2)}, u32[]{:S(2)}) collective-permute-start(bf16[512,384]{1,0:T(8,128)(2,1)S(1)} %get-tuple-element.12.calls_ref.rest_0_), channel_id=1, source_target_pairs={{4,0},{12,8},{20,16},{28,24},{5,1},{13,9},{21,17},{29,25},{6,2},{1... | collective-permute-start | bytes 1179656 | tf_op jit(solution)/shard_map/ppermute | solution.py:15
  9.6 3.6 %collective-permute-done.7.rest_2_ = bf16[256,384]{1,0:T(8,128)(2,1)S(1)} collective-permute-done((bf16[256,384]{1,0:T(8,128)(2,1)S(1)}, bf16[256,384]{1,0:T(8,128)(2,1)S(1)}, u32[]{:S(2)}, u32[]{:S(2)}) %collective-permute-start.7) | collective-permute-done | bytes 196640 | tf_op jit(solution)/shard_map/ppermute | solution.py:15
  13.1 4.3 %collective-permute-start.17 = (bf16[256,384]{1,0:T(8,128)(2,1)S(1)}, bf16[256,384]{1,0:T(8,128)(2,1)S(1)}, u32[]{:S(2)}, u32[]{:S(2)}) collective-permute-start(bf16[256,384]{1,0:T(8,128)(2,1)S(1)} %collective-permute-done.7.rest_2_), channel_id=1, source_target_pairs={{0,24},{4,28},{8,0},{12,4},{16,8},{20,12},{24,16},{28,20},{1,25},{... | collective-permute-start | bytes 589832 | tf_op jit(solution)/shard_map/ppermute | solution.py:15
  17.4 1.5 %collective-permute-start.1 = (f32[2,384]{1,0:T(2,128)S(1)}, f32[2,384]{1,0:T(2,128)S(1)}, u32[]{:S(2)}, u32[]{:S(2)}) collective-permute-start(f32[2,384]{1,0:T(2,128)S(1)} %get-tuple-element.13), channel_id=1, source_target_pairs={{0,4},{4,0},{8,12},{12,8},{16,20},{20,16},{24,28},{28,24},{1,5},{5... | collective-permute-start | bytes 9224 | tf_op jit(solution)/shard_map/ppermute | solution.py:15
  18.9 2.2 %collective-permute-done.1 = f32[2,384]{1,0:T(2,128)S(1)} collective-permute-done((f32[2,384]{1,0:T(2,128)S(1)}, f32[2,384]{1,0:T(2,128)S(1)}, u32[]{:S(2)}, u32[]{:S(2)}) %collective-permute-start.1) | collective-permute-done | bytes 3104 | tf_op jit(solution)/shard_map/ppermute | solution.py:15
  21.1 1.6 %collective-permute-start.2 = (f32[2,384]{1,0:T(2,128)S(1)}, f32[2,384]{1,0:T(2,128)S(1)}, u32[]{:S(2)}, u32[]{:S(2)}) collective-permute-start(f32[2,384]{1,0:T(2,128)S(1)} %add.14), channel_id=1, source_target_pairs={{0,8},{4,12},{8,0},{12,4},{16,24},{20,28},{24,16},{28,20},{1,9},{5... | collective-permute-start | bytes 9224 | tf_op jit(solution)/shard_map/ppermute | solution.py:15
  22.7 2.0 %collective-permute-done.2 = f32[2,384]{1,0:T(2,128)S(1)} collective-permute-done((f32[2,384]{1,0:T(2,128)S(1)}, f32[2,384]{1,0:T(2,128)S(1)}, u32[]{:S(2)}, u32[]{:S(2)}) %collective-permute-start.2) | collective-permute-done | bytes 3104 | tf_op jit(solution)/shard_map/ppermute | solution.py:15
  24.7 0.0 collective-permute-start.3
  24.8 4.5 %collective-permute-done.3 = f32[2,384]{1,0:T(2,128)S(1)} collective-permute-done((f32[2,384]{1,0:T(2,128)S(1)}, f32[2,384]{1,0:T(2,128)S(1)}, u32[]{:S(2)}, u32[]{:S(2)}) %collective-permute-start.3) | collective-permute-done | bytes 3104 | tf_op jit(solution)/shard_map/ppermute | solution.py:15
  29.2 0.0 collective-permute-start.4
  29.2 1.2 %collective-permute-done.4.other_sums_ref = f32[2,384]{1,0:T(2,128)S(1)} collective-permute-done((f32[2,384]{1,0:T(2,128)S(1)}, f32[2,384]{1,0:T(2,128)S(1)}, u32[]{:S(2)}, u32[]{:S(2)}) %collective-permute-start.4) | collective-permute-done | bytes 3104 | tf_op jit(solution)/shard_map/ppermute | solution.py:15
  30.4 0.2 collective-permute-start.22
  30.6 0.0 collective-permute-done.10.rest_4_
  30.6 0.3 collective-permute-start.23
  30.9 0.0 collective-permute-done.other_ref.rest_1_
  30.9 1.4 %collective-permute-start.11 = (bf16[256,384]{1,0:T(8,128)(2,1)S(1)}, bf16[256,384]{1,0:T(8,128)(2,1)S(1)}, u32[]{:S(2)}, u32[]{:S(2)}) collective-permute-start(bf16[256,384]{1,0:T(8,128)(2,1)S(1)} %collective-permute-done.10.rest_4_), channel_id=1, source_target_pairs={{0,4},{4,0},{8,12},{12,8},{16,20},{20,16},{24,28},{28,24},{1,5},{5... | collective-permute-start | bytes 589832 | tf_op jit(solution)/shard_map/ppermute | solution.py:15
  32.3 0.0 collective-permute-done.17.rest_6_
  32.3 0.6 collective-permute-start.8
  33.0 0.0 collective-permute-done.22.rest_3_
  33.0 1.0 %collective-permute-start.13 = (bf16[256,384]{1,0:T(8,128)(2,1)S(1)}, bf16[256,384]{1,0:T(8,128)(2,1)}, u32[]{:S(2)}, u32[]{:S(2)}) collective-permute-start(bf16[256,384]{1,0:T(8,128)(2,1)S(1)} %collective-permute-done.10.rest_4_), channel_id=1, source_target_pairs={{0,24},{4,28},{8,0},{12,4},{16,8},{20,12},{24,16},{28,20},{1,25},{... | collective-permute-start | bytes 589832 | tf_op jit(solution)/shard_map/ppermute | solution.py:15
  34.0 0.0 collective-permute-done.23.rest_5_
  34.0 0.0 collective-permute-start.24
  34.0 0.0 collective-permute-done.5.rest_0_.rest_2_
  34.0 0.5 collective-permute-start.6
  34.5 4.2 %collective-permute-done.11.rest_4_ = bf16[256,384]{1,0:T(8,128)(2,1)S(1)} collective-permute-done((bf16[256,384]{1,0:T(8,128)(2,1)S(1)}, bf16[256,384]{1,0:T(8,128)(2,1)S(1)}, u32[]{:S(2)}, u32[]{:S(2)}) %collective-permute-start.11) | collective-permute-done | bytes 196640 | tf_op jit(solution)/shard_map/ppermute | solution.py:15
  38.7 0.0 collective-permute-start.12
  38.7 3.4 %collective-permute-done.8.rest_2_.rest_6_ = bf16[256,384]{1,0:T(8,128)(2,1)S(1)} collective-permute-done((bf16[256,384]{1,0:T(8,128)(2,1)S(1)}, bf16[256,384]{1,0:T(8,128)(2,1)S(1)}, u32[]{:S(2)}, u32[]{:S(2)}) %collective-permute-start.8) | collective-permute-done | bytes 196640 | tf_op jit(solution)/shard_map/ppermute | solution.py:15
  42.1 4.0 %collective-permute-start.18 = (bf16[256,384]{1,0:T(8,128)(2,1)S(1)}, bf16[256,384]{1,0:T(8,128)(2,1)}, u32[]{:S(2)}, u32[]{:S(2)}) collective-permute-start(bf16[256,384]{1,0:T(8,128)(2,1)S(1)} %collective-permute-done.17.rest_6_), channel_id=1, source_target_pairs={{0,4},{8,12},{16,20},{24,28},{1,5},{9,13},{17,21},{25,29},{2,6},{1... | collective-permute-start | bytes 589832 | tf_op jit(solution)/shard_map/ppermute | solution.py:15
  46.1 0.0 collective-permute-done.13.rest_10_
  46.1 1.3 %collective-permute-start.14 = (bf16[256,384]{1,0:T(8,128)(2,1)}, bf16[256,384]{1,0:T(8,128)(2,1)S(1)}, u32[]{:S(2)}, u32[]{:S(2)}) collective-permute-start(bf16[256,384]{1,0:T(8,128)(2,1)} %collective-permute-done.13.rest_10_), channel_id=1, source_target_pairs={{0,4},{8,12},{16,20},{24,28},{1,5},{9,13},{17,21},{25,29},{2,6},{1... | collective-permute-start | bytes 589832 | tf_op jit(solution)/shard_map/ppermute | solution.py:15
  47.4 0.0 collective-permute-done.24.rest_7_
  47.4 0.0 copy-start
  47.4 0.7 copy-done
  48.1 0.0 collective-permute-done.12.rest_5_
  48.1 0.5 collective-permute-start.20
  48.6 2.1 %collective-permute-done.18.rest_8_ = bf16[256,384]{1,0:T(8,128)(2,1)} collective-permute-done((bf16[256,384]{1,0:T(8,128)(2,1)S(1)}, bf16[256,384]{1,0:T(8,128)(2,1)}, u32[]{:S(2)}, u32[]{:S(2)}) %collective-permute-start.18) | collective-permute-done | bytes 196640 | tf_op jit(solution)/shard_map/ppermute | solution.py:15
  50.7 2.7 %collective-permute-done.14.rest_6_ = bf16[256,384]{1,0:T(8,128)(2,1)S(1)} collective-permute-done((bf16[256,384]{1,0:T(8,128)(2,1)}, bf16[256,384]{1,0:T(8,128)(2,1)S(1)}, u32[]{:S(2)}, u32[]{:S(2)}) %collective-permute-start.14) | collective-permute-done | bytes 196640 | tf_op jit(solution)/shard_map/ppermute | solution.py:15
  53.3 0.0 collective-permute-start.15
  53.3 0.1 pad_add_fusion.1.where_ref
  53.4 0.3 shard_map.28
  53.8 0.0 copy-start.1
  53.8 0.9 %copy-done.1 = bf16[256,384]{1,0:T(8,128)(2,1)S(1)} copy-done((bf16[256,384]{1,0:T(8,128)(2,1)S(1)}, bf16[256,384]{1,0:T(8,128)(2,1)}, u32[]{:S(2)}) %copy-start.1) | copy-done | bytes 196632
  54.7 1.1 %shard_map.31 = f32[512,256]{1,0:T(8,128)S(1)} custom-call(s32[2]{0:T(128)S(1)} %pad_add_fusion.1.where_ref, bf16[512,768]{1,0:T(8,128)(2,1)S(1)} %get-tuple-element.14.left_ref, f32[1,768]{1,0:T(1,128)S(1)} %get-tuple-element.15.shift_ref, f32[1,768]{1,0:T(1,128)S(1)} %get-tuple-element.16.scale_ref, ...), custom_call_target="tpu_custom_call" | custom-call | flops 201326592 | bytes 262144 | tf_op jit(solution)/shard_map/pallas_call | solution.py:40
  55.9 0.0 collective-permute-done.9.rest_3_.rest_7_
  55.9 1.6 %collective-permute-start.25 = (f16[512,256]{1,0:T(8,128)(2,1)S(1)}, f16[512,256]{1,0:T(8,128)(2,1)S(1)}, u32[]{:S(2)}, u32[]{:S(2)}) collective-permute-start(f16[512,256]{1,0:T(8,128)(2,1)S(1)} %convert_element_type.22), channel_id=1, source_target_pairs={{0,2},{1,3},{2,0},{3,1},{4,6},{5,7},{6,4},{7,5},{8,10},{9,11},{10,... | collective-permute-start | bytes 786440 | tf_op jit(solution)/shard_map/ppermute | solution.py:15
  57.4 0.0 collective-permute-done.6.rest_1_.rest_3_
  57.4 0.0 collective-permute-done.19.rest_9_
  57.4 1.8 %shard_map.30 = f32[512,256]{1,0:T(8,128)S(1)} custom-call(s32[2]{0:T(128)S(1)} %pad_add_fusion.1.where_ref, bf16[512,768]{1,0:T(8,128)(2,1)S(1)} %get-tuple-element.14.left_ref, f32[1,768]{1,0:T(1,128)S(1)} %get-tuple-element.15.shift_ref, f32[1,768]{1,0:T(1,128)S(1)} %get-tuple-element.16.scale_ref, ...), custom_call_target="tpu_custom_call" | custom-call | flops 201326592 | bytes 262144 | tf_op jit(solution)/shard_map/pallas_call | solution.py:40
  59.3 0.6 collective-permute-start.21
  59.9 1.0 %shard_map.29 = f32[512,128]{1,0:T(8,128)S(1)} custom-call(s32[2]{0:T(128)S(1)} %pad_add_fusion.1.where_ref, bf16[512,768]{1,0:T(8,128)(2,1)S(1)} %get-tuple-element.14.left_ref, f32[1,768]{1,0:T(1,128)S(1)} %get-tuple-element.15.shift_ref, f32[1,768]{1,0:T(1,128)S(1)} %get-tuple-element.16.scale_ref, ...), custom_call_target="tpu_custom_call" | custom-call | flops 100663296 | bytes 131072 | tf_op jit(solution)/shard_map/pallas_call | solution.py:40
  61.0 1.6 %collective-permute-start.16 = (f16[512,128]{1,0:T(8,128)(2,1)S(1)}, f16[512,128]{1,0:T(8,128)(2,1)S(1)}, u32[]{:S(2)}, u32[]{:S(2)}) collective-permute-start(f16[512,128]{1,0:T(8,128)(2,1)S(1)} %convert_element_type.18), channel_id=1, source_target_pairs={{0,2},{1,3},{2,0},{3,1},{4,6},{5,7},{6,4},{7,5},{8,10},{9,11},{10,... | collective-permute-start | bytes 393224 | tf_op jit(solution)/shard_map/ppermute | solution.py:15
  62.5 0.1 pad_add_fusion.where_ref
  62.6 2.5 %collective-permute-done.25 = f16[512,256]{1,0:T(8,128)(2,1)S(1)} collective-permute-done((f16[512,256]{1,0:T(8,128)(2,1)S(1)}, f16[512,256]{1,0:T(8,128)(2,1)S(1)}, u32[]{:S(2)}, u32[]{:S(2)}) %collective-permute-start.25) | collective-permute-done | bytes 262176 | tf_op jit(solution)/shard_map/ppermute | solution.py:15
  65.2 1.9 %shard_map.32.rest_12_ = f32[512,640]{1,0:T(8,128)} custom-call(s32[2]{0:T(128)S(1)} %pad_add_fusion.where_ref, bf16[512,768]{1,0:T(8,128)(2,1)S(1)} %get-tuple-element.14.left_ref, f32[1,768]{1,0:T(1,128)S(1)} %get-tuple-element.15.shift_ref, f32[1,768]{1,0:T(1,128)S(1)} %get-tuple-element.16.scale_ref, f32[512,256]{1,0:T(8,128)S(1)} %convert_element_type.23.got_ref, ...), custom_call_target="tpu_custom_call" | custom-call | flops 201326592 | bytes 524288 | tf_op jit(solution)/shard_map/pallas_call | solution.py:40
  67.1 6.0 %collective-permute-done.16 = f16[512,128]{1,0:T(8,128)(2,1)S(1)} collective-permute-done((f16[512,128]{1,0:T(8,128)(2,1)S(1)}, f16[512,128]{1,0:T(8,128)(2,1)S(1)}, u32[]{:S(2)}, u32[]{:S(2)}) %collective-permute-start.16) | collective-permute-done | bytes 131104 | tf_op jit(solution)/shard_map/ppermute | solution.py:15
  73.1 0.0 collective-permute-done.21
  73.2 2.6 %shard_map.33.rest_8_ = f32[512,640]{1,0:T(8,128)} custom-call(s32[2]{0:T(128)S(1)} %pad_add_fusion.where_ref, bf16[512,768]{1,0:T(8,128)(2,1)S(1)} %get-tuple-element.14.left_ref, f32[1,768]{1,0:T(1,128)S(1)} %get-tuple-element.15.shift_ref, f32[1,768]{1,0:T(1,128)S(1)} %get-tuple-element.16.scale_ref, ...), custom_call_target="tpu_custom_call", output_to_operand_aliasing={{}: (17, {})} | custom-call | flops 201326592 | bytes 524288 | tf_op jit(solution)/shard_map/pallas_call | solution.py:40
  75.8 1.7 %shard_map.34 = f32[512,640]{1,0:T(8,128)} custom-call(s32[2]{0:T(128)S(1)} %pad_add_fusion.where_ref, bf16[512,768]{1,0:T(8,128)(2,1)S(1)} %get-tuple-element.14.left_ref, f32[1,768]{1,0:T(1,128)S(1)} %get-tuple-element.15.shift_ref, f32[1,768]{1,0:T(1,128)S(1)} %get-tuple-element.16.scale_ref, ...), custom_call_target="tpu_custom_call", output_to_operand_aliasing={{}: (13, {})} | custom-call | flops 100663296 | bytes 262144 | tf_op jit(solution)/shard_map/pallas_call | solution.py:40
  (15 shorter events, 0.2 us)
Async XLA Ops:
  0.0 1.1 %copy-start.2 = (s32[512,384]{1,0:T(8,128)S(1)}, s32[512,384]{1,0:T(8,128)}, u32[]{:S(2)}) copy-start(s32[512,384]{1,0:T(8,128)} %genotype_ref.1) | copy-start | bytes 2359300
  1.1 1.1 %copy-start.3 = (s32[512,384]{1,0:T(8,128)S(1)}, s32[512,384]{1,0:T(8,128)}, u32[]{:S(2)}) copy-start(s32[512,384]{1,0:T(8,128)} %mask_ref.1) | copy-start | bytes 2359300
  2.6 28.3 %collective-permute-start = (bf16[512,384]{1,0:T(8,128)(2,1)S(1)}, bf16[512,384]{1,0:T(8,128)(2,1)S(1)}, u32[]{:S(2)}, u32[]{:S(2)}) collective-permute-start(bf16[512,384]{1,0:T(8,128)(2,1)S(1)} %get-tuple-element.12.calls_ref.rest_0_), channel_id=1, source_target_pairs={{0,1},{1,0},{2,3},{3,2},{4,5},{5,4},{6,7},{7,6},{8,9},{9,8},{10,11... | collective-permute-start | bytes 1179656 | tf_op jit(solution)/shard_map/ppermute | solution.py:15
  3.2 9.9 %collective-permute-start.7 = (bf16[256,384]{1,0:T(8,128)(2,1)S(1)}, bf16[256,384]{1,0:T(8,128)(2,1)S(1)}, u32[]{:S(2)}, u32[]{:S(2)}) collective-permute-start(bf16[256,384]{1,0:T(8,128)(2,1)S(1)} %get-tuple-element.17), channel_id=1, source_target_pairs={{0,24},{4,28},{8,0},{12,4},{16,8},{20,12},{24,16},{28,20},{1,25},{... | collective-permute-start | bytes 589832 | tf_op jit(solution)/shard_map/ppermute | solution.py:15
  7.8 22.7 %collective-permute-start.10 = (bf16[256,384]{1,0:T(8,128)(2,1)S(1)}, bf16[256,384]{1,0:T(8,128)(2,1)S(1)}, u32[]{:S(2)}, u32[]{:S(2)}) collective-permute-start(bf16[256,384]{1,0:T(8,128)(2,1)S(1)} %get-tuple-element.18), channel_id=1, source_target_pairs={{0,24},{4,28},{8,0},{12,4},{16,8},{20,12},{24,16},{28,20},{1,25},{... | collective-permute-start | bytes 589832 | tf_op jit(solution)/shard_map/ppermute | solution.py:15
  8.3 25.7 %collective-permute-start.5 = (bf16[512,384]{1,0:T(8,128)(2,1)S(1)}, bf16[512,384]{1,0:T(8,128)(2,1)S(1)}, u32[]{:S(2)}, u32[]{:S(2)}) collective-permute-start(bf16[512,384]{1,0:T(8,128)(2,1)S(1)} %get-tuple-element.12.calls_ref.rest_0_), channel_id=1, source_target_pairs={{4,0},{12,8},{20,16},{28,24},{5,1},{13,9},{21,17},{29,25},{6,2},{1... | collective-permute-start | bytes 1179656 | tf_op jit(solution)/shard_map/ppermute | solution.py:15
  13.1 19.2 %collective-permute-start.17 = (bf16[256,384]{1,0:T(8,128)(2,1)S(1)}, bf16[256,384]{1,0:T(8,128)(2,1)S(1)}, u32[]{:S(2)}, u32[]{:S(2)}) collective-permute-start(bf16[256,384]{1,0:T(8,128)(2,1)S(1)} %collective-permute-done.7.rest_2_), channel_id=1, source_target_pairs={{0,24},{4,28},{8,0},{12,4},{16,8},{20,12},{24,16},{28,20},{1,25},{... | collective-permute-start | bytes 589832 | tf_op jit(solution)/shard_map/ppermute | solution.py:15
  17.4 3.7 %collective-permute-start.1 = (f32[2,384]{1,0:T(2,128)S(1)}, f32[2,384]{1,0:T(2,128)S(1)}, u32[]{:S(2)}, u32[]{:S(2)}) collective-permute-start(f32[2,384]{1,0:T(2,128)S(1)} %get-tuple-element.13), channel_id=1, source_target_pairs={{0,4},{4,0},{8,12},{12,8},{16,20},{20,16},{24,28},{28,24},{1,5},{5... | collective-permute-start | bytes 9224 | tf_op jit(solution)/shard_map/ppermute | solution.py:15
  21.1 3.6 %collective-permute-start.2 = (f32[2,384]{1,0:T(2,128)S(1)}, f32[2,384]{1,0:T(2,128)S(1)}, u32[]{:S(2)}, u32[]{:S(2)}) collective-permute-start(f32[2,384]{1,0:T(2,128)S(1)} %add.14), channel_id=1, source_target_pairs={{0,8},{4,12},{8,0},{12,4},{16,24},{20,28},{24,16},{28,20},{1,9},{5... | collective-permute-start | bytes 9224 | tf_op jit(solution)/shard_map/ppermute | solution.py:15
  24.7 4.5 %collective-permute-start.3 = (f32[2,384]{1,0:T(2,128)S(1)}, f32[2,384]{1,0:T(2,128)S(1)}, u32[]{:S(2)}, u32[]{:S(2)}) collective-permute-start(f32[2,384]{1,0:T(2,128)S(1)} %add.15), channel_id=1, source_target_pairs={{0,16},{4,20},{8,24},{12,28},{16,0},{20,4},{24,8},{28,12},{1,17},{... | collective-permute-start | bytes 9224 | tf_op jit(solution)/shard_map/ppermute | solution.py:15
  29.2 1.2 %collective-permute-start.4 = (f32[2,384]{1,0:T(2,128)S(1)}, f32[2,384]{1,0:T(2,128)S(1)}, u32[]{:S(2)}, u32[]{:S(2)}) collective-permute-start(f32[2,384]{1,0:T(2,128)S(1)} %add.16.sums_ref), channel_id=1, source_target_pairs={{0,1},{1,0},{2,3},{3,2},{4,5},{5,4},{6,7},{7,6},{8,9},{9,8},{10,11... | collective-permute-start | bytes 9224 | tf_op jit(solution)/shard_map/ppermute | solution.py:15
  30.4 2.6 %collective-permute-start.22 = (bf16[256,384]{1,0:T(8,128)(2,1)S(1)}, bf16[256,384]{1,0:T(8,128)(2,1)S(1)}, u32[]{:S(2)}, u32[]{:S(2)}) collective-permute-start(bf16[256,384]{1,0:T(8,128)(2,1)S(1)} %collective-permute-done.7.rest_2_), channel_id=1, source_target_pairs={{0,1},{1,0},{2,3},{3,2},{4,5},{5,4},{6,7},{7,6},{8,9},{9,8},{10,11... | collective-permute-start | bytes 589832 | tf_op jit(solution)/shard_map/ppermute | solution.py:15
  30.6 3.4 %collective-permute-start.23 = (bf16[256,384]{1,0:T(8,128)(2,1)S(1)}, bf16[256,384]{1,0:T(8,128)(2,1)S(1)}, u32[]{:S(2)}, u32[]{:S(2)}) collective-permute-start(bf16[256,384]{1,0:T(8,128)(2,1)S(1)} %collective-permute-done.10.rest_4_), channel_id=1, source_target_pairs={{0,1},{1,0},{2,3},{3,2},{4,5},{5,4},{6,7},{7,6},{8,9},{9,8},{10,11... | collective-permute-start | bytes 589832 | tf_op jit(solution)/shard_map/ppermute | solution.py:15
  30.9 7.8 %collective-permute-start.11 = (bf16[256,384]{1,0:T(8,128)(2,1)S(1)}, bf16[256,384]{1,0:T(8,128)(2,1)S(1)}, u32[]{:S(2)}, u32[]{:S(2)}) collective-permute-start(bf16[256,384]{1,0:T(8,128)(2,1)S(1)} %collective-permute-done.10.rest_4_), channel_id=1, source_target_pairs={{0,4},{4,0},{8,12},{12,8},{16,20},{20,16},{24,28},{28,24},{1,5},{5... | collective-permute-start | bytes 589832 | tf_op jit(solution)/shard_map/ppermute | solution.py:15
  32.3 9.8 %collective-permute-start.8 = (bf16[256,384]{1,0:T(8,128)(2,1)S(1)}, bf16[256,384]{1,0:T(8,128)(2,1)S(1)}, u32[]{:S(2)}, u32[]{:S(2)}) collective-permute-start(bf16[256,384]{1,0:T(8,128)(2,1)S(1)} %collective-permute-done.7.rest_2_), channel_id=1, source_target_pairs={{0,4},{4,0},{8,12},{12,8},{16,20},{20,16},{24,28},{28,24},{1,5},{5... | collective-permute-start | bytes 589832 | tf_op jit(solution)/shard_map/ppermute | solution.py:15
  33.0 13.1 %collective-permute-start.13 = (bf16[256,384]{1,0:T(8,128)(2,1)S(1)}, bf16[256,384]{1,0:T(8,128)(2,1)}, u32[]{:S(2)}, u32[]{:S(2)}) collective-permute-start(bf16[256,384]{1,0:T(8,128)(2,1)S(1)} %collective-permute-done.10.rest_4_), channel_id=1, source_target_pairs={{0,24},{4,28},{8,0},{12,4},{16,8},{20,12},{24,16},{28,20},{1,25},{... | collective-permute-start | bytes 589832 | tf_op jit(solution)/shard_map/ppermute | solution.py:15
  34.0 13.4 %collective-permute-start.24 = (bf16[256,384]{1,0:T(8,128)(2,1)S(1)}, bf16[256,384]{1,0:T(8,128)(2,1)S(1)}, u32[]{:S(2)}, u32[]{:S(2)}) collective-permute-start(bf16[256,384]{1,0:T(8,128)(2,1)S(1)} %collective-permute-done.17.rest_6_), channel_id=1, source_target_pairs={{0,1},{1,0},{2,3},{3,2},{4,5},{5,4},{6,7},{7,6},{8,9},{9,8},{10,11... | collective-permute-start | bytes 589832 | tf_op jit(solution)/shard_map/ppermute | solution.py:15
  34.0 23.4 %collective-permute-start.6 = (bf16[512,384]{1,0:T(8,128)(2,1)S(1)}, bf16[512,384]{1,0:T(8,128)(2,1)S(1)}, u32[]{:S(2)}, u32[]{:S(2)}) collective-permute-start(bf16[512,384]{1,0:T(8,128)(2,1)S(1)} %collective-permute-done.5.rest_0_.rest_2_), channel_id=1, source_target_pairs={{0,1},{1,0},{2,3},{3,2},{4,5},{5,4},{6,7},{7,6},{8,9},{9,8},{10,11... | collective-permute-start | bytes 1179656 | tf_op jit(solution)/shard_map/ppermute | solution.py:15
  38.7 9.4 %collective-permute-start.12 = (bf16[256,384]{1,0:T(8,128)(2,1)S(1)}, bf16[256,384]{1,0:T(8,128)(2,1)S(1)}, u32[]{:S(2)}, u32[]{:S(2)}) collective-permute-start(bf16[256,384]{1,0:T(8,128)(2,1)S(1)} %collective-permute-done.11.rest_4_), channel_id=1, source_target_pairs={{0,1},{1,0},{2,3},{3,2},{4,5},{5,4},{6,7},{7,6},{8,9},{9,8},{10,11... | collective-permute-start | bytes 589832 | tf_op jit(solution)/shard_map/ppermute | solution.py:15
  42.1 8.6 %collective-permute-start.18 = (bf16[256,384]{1,0:T(8,128)(2,1)S(1)}, bf16[256,384]{1,0:T(8,128)(2,1)}, u32[]{:S(2)}, u32[]{:S(2)}) collective-permute-start(bf16[256,384]{1,0:T(8,128)(2,1)S(1)} %collective-permute-done.17.rest_6_), channel_id=1, source_target_pairs={{0,4},{8,12},{16,20},{24,28},{1,5},{9,13},{17,21},{25,29},{2,6},{1... | collective-permute-start | bytes 589832 | tf_op jit(solution)/shard_map/ppermute | solution.py:15
  46.1 7.3 %collective-permute-start.14 = (bf16[256,384]{1,0:T(8,128)(2,1)}, bf16[256,384]{1,0:T(8,128)(2,1)S(1)}, u32[]{:S(2)}, u32[]{:S(2)}) collective-permute-start(bf16[256,384]{1,0:T(8,128)(2,1)} %collective-permute-done.13.rest_10_), channel_id=1, source_target_pairs={{0,4},{8,12},{16,20},{24,28},{1,5},{9,13},{17,21},{25,29},{2,6},{1... | collective-permute-start | bytes 589832 | tf_op jit(solution)/shard_map/ppermute | solution.py:15
  47.4 0.7 copy-start
  48.1 7.8 %collective-permute-start.9 = (bf16[256,384]{1,0:T(8,128)(2,1)S(1)}, bf16[256,384]{1,0:T(8,128)(2,1)S(1)}, u32[]{:S(2)}, u32[]{:S(2)}) collective-permute-start(bf16[256,384]{1,0:T(8,128)(2,1)S(1)} %collective-permute-done.8.rest_2_.rest_6_), channel_id=1, source_target_pairs={{0,1},{1,0},{2,3},{3,2},{4,5},{5,4},{6,7},{7,6},{8,9},{9,8},{10,11... | collective-permute-start | bytes 589832 | tf_op jit(solution)/shard_map/ppermute | solution.py:15
  48.1 9.4 %collective-permute-start.20 = (bf16[256,384]{1,0:T(8,128)(2,1)}, bf16[256,384]{1,0:T(8,128)(2,1)}, u32[]{:S(2)}, u32[]{:S(2)}) collective-permute-start(bf16[256,384]{1,0:T(8,128)(2,1)} %collective-permute-done.13.rest_10_), channel_id=1, source_target_pairs={{0,1},{1,0},{2,3},{3,2},{4,5},{5,4},{6,7},{7,6},{8,9},{9,8},{10,11... | collective-permute-start | bytes 589832 | tf_op jit(solution)/shard_map/ppermute | solution.py:15
  50.7 6.8 %collective-permute-start.19 = (bf16[256,384]{1,0:T(8,128)(2,1)}, bf16[256,384]{1,0:T(8,128)(2,1)}, u32[]{:S(2)}, u32[]{:S(2)}) collective-permute-start(bf16[256,384]{1,0:T(8,128)(2,1)} %collective-permute-done.18.rest_8_), channel_id=1, source_target_pairs={{0,1},{1,0},{2,3},{3,2},{4,5},{5,4},{6,7},{7,6},{8,9},{9,8},{10,11... | collective-permute-start | bytes 589832 | tf_op jit(solution)/shard_map/ppermute | solution.py:15
  53.3 6.6 %collective-permute-start.15 = (bf16[256,384]{1,0:T(8,128)(2,1)S(1)}, bf16[256,384]{1,0:T(8,128)(2,1)S(1)}, u32[]{:S(2)}, u32[]{:S(2)}) collective-permute-start(bf16[256,384]{1,0:T(8,128)(2,1)S(1)} %collective-permute-done.14.rest_6_), channel_id=1, source_target_pairs={{0,1},{1,0},{2,3},{3,2},{4,5},{5,4},{6,7},{7,6},{8,9},{9,8},{10,11... | collective-permute-start | bytes 589832 | tf_op jit(solution)/shard_map/ppermute | solution.py:15
  53.8 0.9 %copy-start.1 = (bf16[256,384]{1,0:T(8,128)(2,1)S(1)}, bf16[256,384]{1,0:T(8,128)(2,1)}, u32[]{:S(2)}) copy-start(bf16[256,384]{1,0:T(8,128)(2,1)} %copy-done) | copy-start | bytes 589828
  55.9 9.2 %collective-permute-start.25 = (f16[512,256]{1,0:T(8,128)(2,1)S(1)}, f16[512,256]{1,0:T(8,128)(2,1)S(1)}, u32[]{:S(2)}, u32[]{:S(2)}) collective-permute-start(f16[512,256]{1,0:T(8,128)(2,1)S(1)} %convert_element_type.22), channel_id=1, source_target_pairs={{0,2},{1,3},{2,0},{3,1},{4,6},{5,7},{6,4},{7,5},{8,10},{9,11},{10,... | collective-permute-start | bytes 786440 | tf_op jit(solution)/shard_map/ppermute | solution.py:15
  59.3 13.8 %collective-permute-start.21 = (f16[512,256]{1,0:T(8,128)(2,1)S(1)}, f16[512,256]{1,0:T(8,128)(2,1)S(1)}, u32[]{:S(2)}, u32[]{:S(2)}) collective-permute-start(f16[512,256]{1,0:T(8,128)(2,1)S(1)} %convert_element_type.20), channel_id=1, source_target_pairs={{0,2},{1,3},{2,0},{3,1},{4,6},{5,7},{6,4},{7,5},{8,10},{9,11},{10,... | collective-permute-start | bytes 786440 | tf_op jit(solution)/shard_map/ppermute | solution.py:15
  61.0 12.1 %collective-permute-start.16 = (f16[512,128]{1,0:T(8,128)(2,1)S(1)}, f16[512,128]{1,0:T(8,128)(2,1)S(1)}, u32[]{:S(2)}, u32[]{:S(2)}) collective-permute-start(f16[512,128]{1,0:T(8,128)(2,1)S(1)} %convert_element_type.18), channel_id=1, source_target_pairs={{0,2},{1,3},{2,0},{3,1},{4,6},{5,7},{6,4},{7,5},{8,10},{9,11},{10,... | collective-permute-start | bytes 393224 | tf_op jit(solution)/shard_map/ppermute | solution.py:15

commit v2 on v1

v2 whole, which is shorter than its diff:
```python
import functools
import math

import jax
import jax.numpy as jnp
from jax import lax
from jax.experimental import pallas as pl
from jax.experimental.pallas import tpu as pltpu
from jax.sharding import PartitionSpec as P


def send(value, axis, route):
    count = lax.axis_size(axis)
    pairs = [(source, route(source)) for source in range(count)]
    return lax.ppermute(value, axis, [pair for pair in pairs if pair[1] is not None])


def swap_core(value):
    return send(value, "snps", lambda s: s ^ 1)


def arrival(piece):
    k, half = piece
    return k + 0.5 * half + (1.6 if k % 2 else 0.0)


def strips(samples):
    whole_count = (samples + 2) // 4
    result = []
    for strip in range(4):
        first = strip * (samples + 2) // 4
        begin = first + strip % 2
        wholes = [divmod(begin + n, 2) for n in range(whole_count)]
        cut = divmod(first if strip % 2 else first + whole_count, 2)
        result.append((sorted(wholes, key=arrival), wholes, cut))
    return result


def call_kernel(body, shapes, operands, specs, flops, moved, **more):
    return pl.pallas_call(
        body,
        out_shape=shapes,
        in_specs=specs,
        compiler_params=pltpu.CompilerParams(vmem_limit_bytes=24 * 2**20),
        cost_estimate=pl.CostEstimate(flops=flops, bytes_accessed=moved, transcendentals=0),
        **more,
    )(*operands)


VMEM = pl.BlockSpec(memory_space=pltpu.VMEM)
SMEM = pl.BlockSpec(memory_space=pltpu.SMEM)
ANY = pl.BlockSpec(memory_space=pl.ANY)


def encode_body(genotype_ref, mask_ref, whole_ref, first_ref, second_ref, sums_ref,
                dosage_in, mask_in, sems):
    rows = first_ref.shape[0]
    copies = []
    for half in range(2):
        at = pl.ds(half * rows, rows)
        copies.append([
            pltpu.make_async_copy(source.at[at], target.at[at], sems.at[2 * half + n])
            for n, (source, target) in enumerate(((genotype_ref, dosage_in), (mask_ref, mask_in)))
        ])
    for copy in copies[0] + copies[1]:
        copy.start()
    totals = []
    for half, part_ref in enumerate((first_ref, second_ref)):
        for copy in copies[half]:
            copy.wait()
        at = pl.ds(half * rows, rows)
        mask = mask_in[at, :]
        dosage = mask * dosage_in[at, :]
        calls = (dosage + mask).astype(jnp.float32).astype(jnp.bfloat16)
        whole_ref[at, :] = calls
        part_ref[...] = calls
        totals.append([
            jnp.sum(value.astype(jnp.float32), axis=0, keepdims=True) for value in (dosage, mask)
        ])
    for n in range(2):
        sums_ref[n : n + 1, :] = totals[0][n] + totals[1][n]


def encode(genotype, mask):
    rows, columns = genotype.shape
    half = rows // 2
    calls = lambda n: jax.ShapeDtypeStruct((n, columns), jnp.bfloat16)
    return pl.pallas_call(
        encode_body,
        name="encode",
        out_shape=(calls(rows), calls(half), calls(half), jax.ShapeDtypeStruct((2, columns), jnp.float32)),
        in_specs=[ANY, ANY],
        out_specs=(VMEM,) * 4,
        scratch_shapes=[
            pltpu.VMEM((rows, columns), jnp.int32),
            pltpu.VMEM((rows, columns), jnp.int32),
            pltpu.SemaphoreType.DMA((4,)),
        ],
        compiler_params=pltpu.CompilerParams(vmem_limit_bytes=40 * 2**20),
    )(pltpu.with_memory_space_constraint(genotype, pltpu.HBM), pltpu.with_memory_space_constraint(mask, pltpu.HBM))


def factors(sums):
    frequency = (sums[0:1] + 1.0) / (2.0 * sums[1:2] + 2.0)
    return 1.0 + 2.0 * frequency, 1.0 / jnp.sqrt(2.0 * frequency * (1.0 - frequency))


def standardized(calls, shift, scale):
    wide = calls.astype(jnp.float32)
    return jnp.where(wide > 0.0, (wide - shift) * scale, 0.0).astype(jnp.bfloat16)


def left_body(calls_ref, sums_ref, left_ref):
    left_ref[...] = standardized(calls_ref[...], *factors(sums_ref[...]))


def multiply(left, right):
    return lax.dot_general(
        left, right, (((1,), (1,)), ((), ())), preferred_element_type=jnp.float32
    )


def products_body(cases, where_ref, left_ref, sums_ref, *rest):
    *refs, keep_ref, away_ref, right_ref = rest
    shift, scale = factors(sums_ref[...])
    for strip, by_parity in cases:
        for odd, (at, begin) in enumerate(by_parity):

            def fill(at=at, begin=begin):
                rows = refs[at][pl.ds(begin, right_ref.shape[0]), :]
                right_ref[...] = standardized(rows, shift, scale)

            if by_parity[0] != by_parity[1]:
                pl.when(where_ref[1] == odd)(fill)
            elif not odd:
                fill()
        place = where_ref[0] ^ strip
        for bit, target_ref in enumerate((keep_ref, away_ref)):

            @pl.when(place % 2 == bit)
            def _(target_ref=target_ref, place=place):
                target_ref[place // 2] = multiply(left_ref[...], right_ref[...])


def products_more_body(cases, where_ref, left_ref, sums_ref, *rest):
    *refs, _, _, keep_ref, away_ref, right_ref = rest
    products_body(cases, where_ref, left_ref, sums_ref, *refs, keep_ref, away_ref, right_ref)


def add_body(places, up, where_ref, keep_ref, other_ref, got_ref, *rest):
    out_ref, total_ref, sem = rest[-3:]
    total_ref[...] = (keep_ref[0] + other_ref[0]) * up[0] + got_ref[...] * up[1]
    width = total_ref.shape[1]
    for strip, begin in enumerate(places):

        @pl.when(where_ref[0] == strip)
        def _(begin=begin):
            copy = pltpu.make_async_copy(total_ref, out_ref.at[:, pl.ds(begin, width)], sem)
            copy.start()
            copy.wait()


def per_device(genotype, mask):
    samples = lax.axis_size("samples")
    parts = lax.axis_size("snps")
    assert samples % 4 == 0 and samples & (samples - 1) == 0 and parts == 4
    rows, snp_part = genotype.shape
    snp_total = snp_part * parts
    turns = samples // 4
    half_rows = rows // 2
    width = rows * (samples // 2 + 1) // parts

    calls, first, second, sums = encode(genotype, mask)

    along = lambda s: (s - 2) % samples
    line = [[first, second]]
    for _ in range(1, turns + 1):
        line.append([send(line[-1][h], "samples", along) for h in range(2)])
    beside = send(calls, "samples", lambda s: s - 1 if s % 2 else None)
    side = [None]
    for t in range(1, turns):
        side.append([send(line[t][h], "samples", lambda s: s ^ 1) for h in range(2)])
    side.append([
        send(line[turns][h], "samples", lambda s: None if s % 2 else s + 1)
        for h in range(2)
    ])

    for bit in range(samples.bit_length() - 1):
        sums = sums + send(sums, "samples", lambda s, step=1 << bit: s ^ step)

    def source(k, h, odd):
        if k == 0:
            return calls, h * half_rows
        if k % 2 == 0:
            return line[k // 2][h], 0
        if k == 1 and not odd:
            return beside, h * half_rows
        return side[(k + odd) // 2][h], 0

    left = call_kernel(
        left_body, jax.ShapeDtypeStruct((rows, snp_part), jnp.bfloat16), (calls, sums),
        [VMEM] * 2, 5 * rows * snp_part, 4 * rows * snp_part, out_specs=VMEM,
    )
    device = lax.axis_index("snps").astype(jnp.int32)
    parity = (lax.axis_index("samples") % 2).astype(jnp.int32)
    where = jnp.stack([device, parity])
    table = strips(samples)
    bound = snp_total / 2 * 4 * (samples * rows + 1) / 3
    down = 2.0 ** -math.ceil(math.log2(bound / 32768.0))
    count = len(table[0][0])
    quarter = half_rows // 2

    def products(n, chosen, so_far):
        columns = half_rows if n < count else quarter
        arrays, cases = [], []
        for strip in chosen:
            by_arrival, _, cut = table[strip]
            by_parity = []
            for odd in range(2):
                array, begin = source(*(by_arrival[n] if n < count else cut), odd)
                at = next((i for i, known in enumerate(arrays) if known is array), len(arrays))
                if at == len(arrays):
                    arrays.append(array)
                if n == count and strip % 2:
                    begin += quarter
                by_parity.append((at, begin))
            cases.append((strip, tuple(by_parity)))
        shape = jax.ShapeDtypeStruct((2, rows, columns), jnp.float32)
        operands = (where, left, sums, *arrays, *so_far)
        return call_kernel(
            functools.partial(products_body if not so_far else products_more_body, tuple(cases)),
            (shape, shape), operands, [SMEM] + [VMEM] * (len(operands) - 1),
            2 * rows * snp_part * columns * len(chosen), 4 * rows * columns,
            out_specs=(VMEM, VMEM),
            scratch_shapes=[pltpu.VMEM((columns, snp_part), jnp.bfloat16)],
            input_output_aliases={len(operands) - 2 + i: i for i in range(len(so_far))},
        )

    pieces = []
    for n in range(count + 1):
        late = [
            strip for strip, (by_arrival, _, cut) in enumerate(table)
            if (by_arrival[n] if n < count else cut)[0] >= 2 * turns - 1
        ]
        both = ()
        for chosen in ([s for s in range(4) if s not in late], late):
            if chosen:
                both = products(n, chosen, both)
        keep, away = both
        other = swap_core(away)
        theirs = ((keep[1] + other[1]) * down).astype(jnp.float16)
        got = send(theirs, "snps", lambda s: s ^ 2).astype(jnp.float32)
        pieces.append((keep, other, got))
    out = None
    for n, operands in enumerate(pieces):
        places = []
        for strip, (by_arrival, natural, _) in enumerate(table):
            if n < count:
                places.append(natural.index(by_arrival[n]) * half_rows + (strip % 2) * quarter)
            else:
                places.append(0 if strip % 2 else count * half_rows)
        columns = operands[2].shape[1]
        last = () if out is None else (out,)
        operands = (where, *operands, *last)
        out = call_kernel(
            functools.partial(add_body, tuple(places), (1.0 / snp_total, 1.0 / (down * snp_total))),
            jax.ShapeDtypeStruct((rows, width), jnp.float32), operands,
            [SMEM] + [VMEM] * 3 + [ANY] * len(last), rows * columns, 4 * rows * columns,
            out_specs=ANY,
            scratch_shapes=[pltpu.VMEM((rows, columns), jnp.float32), pltpu.SemaphoreType.DMA],
            input_output_aliases={len(operands) - 1: 0} if last else {},
        )
    return out


def solution(mesh):
    return jax.shard_map(
        per_device,
        mesh=mesh,
        in_specs=(P("samples", "snps"), P("samples", "snps")),
        out_specs=P("samples", "snps"),
        check_vma=False,
    )
```

time: 77.9 us -> 77.9 us (level)
  local copies, waits for them, and re-layouts: 3.86 us -> 0 us
  Pallas kernels: 10.9 us -> 13.8 us
  waiting for transfers between devices: 34.4 us -> 36.6 us
  starting transfers between devices: 27.9 us -> 26.8 us
    unnamed x8 -> x0, local copies, waits for them, and re-layouts: 3.86 us -> none
    ppermute x26 -> x18, waiting for transfers between devices: 34.4 us -> 36.6 us  [send(): lax.ppermute(value, axis, [pair for pair in pairs if pair[1] is not None])]
    pallas_call x7 -> x10, Pallas kernels: 10.6 us -> 12.3 us  [call_kernel(): pl.pallas_call(body, out_shape=shapes, in_specs=specs, compiler_params=pl...]
    pallas_call x1, Pallas kernels: 0.35 us -> 1.49 us  [encode(): pl.pallas_call(encode_body, name='encode', out_shape=(calls(rows), calls(...]
    ppermute x26 -> x18, starting transfers between devices: 27.9 us -> 26.8 us  [send(): lax.ppermute(value, axis, [pair for pair in pairs if pair[1] is not None])]
  transfers between devices with their start and end apart: 26 -> 18, of which waited for: 11 -> 11; matrix products, arithmetic and copies ran while one was open for 0% -> 0% of each run, Pallas kernels for 8% -> 12%
where the time goes in v2:
time: 77.9 us; the launch traced here: 77.7 us
  waiting for transfers between devices  36.6 us (47%)
  starting transfers between devices  26.8 us (34%)
  Pallas kernels  13.8 us (18%)
    ppermute x18, waiting for transfers between devices, send(): lax.ppermute(value, axis, [pair for pair in pairs if pair[1] is not None])  36.6 us
    ppermute x18, starting transfers between devices, send(): lax.ppermute(value, axis, [pair for pair in pairs if pair[1] is not None])  26.8 us
    pallas_call x10, Pallas kernels, call_kernel(): pl.pallas_call(body, out_shape=shapes, in_specs=specs, compiler_params=pl...  12.3 us
  transfers between devices with their start and end apart: 18, of which 11 were waited for; matrix products, arithmetic and copies ran while one was open for 0% of the time, Pallas kernels for 12%

profile of v2, /device:TPU:0, one launch (start us, length us, event | category | flops | bytes accessed | tf_op | source)
XLA Modules:
  0.0 77.7 jit_solution(11184087915615671454)
XLA Ops:
  0.0 1.5 %encode.1 = (bf16[512,384]{1,0:T(8,128)(2,1)S(1)}, bf16[256,384]{1,0:T(8,128)(2,1)S(1)}, bf16[256,384]{1,0:T(8,128)(2,1)S(1)}, f32[2,384]{1,0:T(2,128)S(1)}) custom-call(s32[512,384]{1,0:T(8,128)} %genotype_ref.1, s32[512,384]{1,0:T(8,128)} %mask_ref.1), custom_call_target="tpu_custom_call" | custom-call | tf_op jit(solution)/shard_map/encode/pallas_call | solution.py:88
  1.5 5.1 %collective-permute-start.8 = (bf16[256,384]{1,0:T(8,128)(2,1)S(1)}, bf16[256,384]{1,0:T(8,128)(2,1)S(1)}, u32[]{:S(2)}, u32[]{:S(2)}) collective-permute-start(bf16[256,384]{1,0:T(8,128)(2,1)S(1)} %get-tuple-element.24), channel_id=1, source_target_pairs={{0,24},{4,28},{8,0},{12,4},{16,8},{20,12},{24,16},{28,20},{1,25},{... | collective-permute-start | bytes 589832 | tf_op jit(solution)/shard_map/ppermute | solution.py:15
  6.6 1.3 %collective-permute-start.7 = (bf16[512,384]{1,0:T(8,128)(2,1)S(1)}, bf16[512,384]{1,0:T(8,128)(2,1)S(1)}, u32[]{:S(2)}, u32[]{:S(2)}) collective-permute-start(bf16[512,384]{1,0:T(8,128)(2,1)S(1)} %get-tuple-element.21.calls_ref.rest_0_), channel_id=1, source_target_pairs={{4,0},{12,8},{20,16},{28,24},{5,1},{13,9},{21,17},{29,25},{6,2},{1... | collective-permute-start | bytes 1179656 | tf_op jit(solution)/shard_map/ppermute | solution.py:15
  7.9 0.5 collective-permute-start.3
  8.4 3.5 %collective-permute-done.8.rest_1_ = bf16[256,384]{1,0:T(8,128)(2,1)S(1)} collective-permute-done((bf16[256,384]{1,0:T(8,128)(2,1)S(1)}, bf16[256,384]{1,0:T(8,128)(2,1)S(1)}, u32[]{:S(2)}, u32[]{:S(2)}) %collective-permute-start.8) | collective-permute-done | bytes 196640 | tf_op jit(solution)/shard_map/ppermute | solution.py:15
  11.9 4.3 %collective-permute-start.12 = (bf16[256,384]{1,0:T(8,128)(2,1)S(1)}, bf16[256,384]{1,0:T(8,128)(2,1)S(1)}, u32[]{:S(2)}, u32[]{:S(2)}) collective-permute-start(bf16[256,384]{1,0:T(8,128)(2,1)S(1)} %collective-permute-done.8.rest_1_), channel_id=1, source_target_pairs={{0,24},{4,28},{8,0},{12,4},{16,8},{20,12},{24,16},{28,20},{1,25},{... | collective-permute-start | bytes 589832 | tf_op jit(solution)/shard_map/ppermute | solution.py:15
  16.2 1.5 %collective-permute-start = (f32[2,384]{1,0:T(2,128)S(1)}, f32[2,384]{1,0:T(2,128)S(1)}, u32[]{:S(2)}, u32[]{:S(2)}) collective-permute-start(f32[2,384]{1,0:T(2,128)S(1)} %get-tuple-element.22), channel_id=1, source_target_pairs={{0,4},{4,0},{8,12},{12,8},{16,20},{20,16},{24,28},{28,24},{1,5},{5... | collective-permute-start | bytes 9224 | tf_op jit(solution)/shard_map/ppermute | solution.py:15
  17.7 2.1 %collective-permute-done = f32[2,384]{1,0:T(2,128)S(1)} collective-permute-done((f32[2,384]{1,0:T(2,128)S(1)}, f32[2,384]{1,0:T(2,128)S(1)}, u32[]{:S(2)}, u32[]{:S(2)}) %collective-permute-start) | collective-permute-done | bytes 3104 | tf_op jit(solution)/shard_map/ppermute | solution.py:15
  19.8 0.0 collective-permute-start.1
  19.8 3.6 %collective-permute-done.1 = f32[2,384]{1,0:T(2,128)S(1)} collective-permute-done((f32[2,384]{1,0:T(2,128)S(1)}, f32[2,384]{1,0:T(2,128)S(1)}, u32[]{:S(2)}, u32[]{:S(2)}) %collective-permute-start.1) | collective-permute-done | bytes 3104 | tf_op jit(solution)/shard_map/ppermute | solution.py:15
  23.4 0.0 collective-permute-start.2
  23.4 0.1 pad_add_fusion.where_ref
  23.5 4.4 %collective-permute-done.2 = f32[2,384]{1,0:T(2,128)S(1)} collective-permute-done((f32[2,384]{1,0:T(2,128)S(1)}, f32[2,384]{1,0:T(2,128)S(1)}, u32[]{:S(2)}, u32[]{:S(2)}) %collective-permute-start.2) | collective-permute-done | bytes 3104 | tf_op jit(solution)/shard_map/ppermute | solution.py:15
  27.9 0.2 shard_map.28.left_ref
  28.1 0.0 collective-permute-done.3.rest_2_
  28.1 1.8 %shard_map.33 = (f32[2,512,256]{2,1,0:T(8,128)S(1)}, f32[2,512,256]{2,1,0:T(8,128)S(1)}) custom-call(s32[2]{0:T(128)S(1)} %pad_add_fusion.where_ref, bf16[512,384]{1,0:T(8,128)(2,1)S(1)} %shard_map.28.left_ref, f32[2,384]{1,0:T(2,128)S(1)} %add.28.sums_ref, bf16[512,384]{1,0:T(8,128)(2,1)S(1)} %get-tuple-element.21.calls_ref.rest_0_, ...), custom_call_target="tpu_custom_call" | custom-call | flops 301989888 | bytes 524288 | tf_op jit(solution)/shard_map/pallas_call | solution.py:40
  29.9 0.0 collective-permute-done.12.rest_0_
  29.9 1.0 %shard_map.34 = (f32[2,512,256]{2,1,0:T(8,128)S(1)}, f32[2,512,256]{2,1,0:T(8,128)S(1)}) custom-call(s32[2]{0:T(128)S(1)} %pad_add_fusion.where_ref, bf16[512,384]{1,0:T(8,128)(2,1)S(1)} %shard_map.28.left_ref, f32[2,384]{1,0:T(2,128)S(1)} %add.28.sums_ref, ...), custom_call_target="tpu_custom_call", output_to_operand_aliasing={{0}: (4, {}), {1}: (5, {})} | custom-call | flops 100663296 | bytes 524288 | tf_op jit(solution)/shard_map/pallas_call | solution.py:40
  30.8 0.1 collective-permute-start.16
  30.9 1.6 %collective-permute-start.4 = (bf16[256,384]{1,0:T(8,128)(2,1)S(1)}, bf16[256,384]{1,0:T(8,128)(2,1)S(1)}, u32[]{:S(2)}, u32[]{:S(2)}) collective-permute-start(bf16[256,384]{1,0:T(8,128)(2,1)S(1)} %collective-permute-done.3.rest_2_), channel_id=1, source_target_pairs={{0,4},{4,0},{8,12},{12,8},{16,20},{20,16},{24,28},{28,24},{1,5},{5... | collective-permute-start | bytes 589832 | tf_op jit(solution)/shard_map/ppermute | solution.py:15
  32.5 0.3 collective-permute-start.5
  32.8 0.5 collective-permute-start.9
  33.3 0.0 collective-permute-done.7.rest_0_.rest_1_
  33.3 3.4 %collective-permute-start.13 = (bf16[256,384]{1,0:T(8,128)(2,1)S(1)}, bf16[256,384]{1,0:T(8,128)(2,1)S(1)}, u32[]{:S(2)}, u32[]{:S(2)}) collective-permute-start(bf16[256,384]{1,0:T(8,128)(2,1)S(1)} %collective-permute-done.12.rest_0_), channel_id=1, source_target_pairs={{0,4},{8,12},{16,20},{24,28},{1,5},{9,13},{17,21},{25,29},{2,6},{1... | collective-permute-start | bytes 589832 | tf_op jit(solution)/shard_map/ppermute | solution.py:15
  36.7 2.1 %collective-permute-done.4.rest_0_.rest_2_ = bf16[256,384]{1,0:T(8,128)(2,1)S(1)} collective-permute-done((bf16[256,384]{1,0:T(8,128)(2,1)S(1)}, bf16[256,384]{1,0:T(8,128)(2,1)S(1)}, u32[]{:S(2)}, u32[]{:S(2)}) %collective-permute-start.4) | collective-permute-done | bytes 196640 | tf_op jit(solution)/shard_map/ppermute | solution.py:15
  38.8 1.4 %shard_map.31 = (f32[2,512,256]{2,1,0:T(8,128)S(1)}, f32[2,512,256]{2,1,0:T(8,128)S(1)}) custom-call(s32[2]{0:T(128)S(1)} %pad_add_fusion.where_ref, bf16[512,384]{1,0:T(8,128)(2,1)S(1)} %shard_map.28.left_ref, f32[2,384]{1,0:T(2,128)S(1)} %add.28.sums_ref, bf16[512,384]{1,0:T(8,128)(2,1)S(1)} %get-tuple-element.21.calls_ref.rest_0_, ...), custom_call_target="tpu_custom_call" | custom-call | flops 201326592 | bytes 524288 | tf_op jit(solution)/shard_map/pallas_call | solution.py:40
  40.1 0.0 collective-permute-done.5.rest_2_
  40.2 2.3 %collective-permute-done.9.rest_1_.rest_0_ = bf16[256,384]{1,0:T(8,128)(2,1)S(1)} collective-permute-done((bf16[256,384]{1,0:T(8,128)(2,1)S(1)}, bf16[256,384]{1,0:T(8,128)(2,1)S(1)}, u32[]{:S(2)}, u32[]{:S(2)}) %collective-permute-start.9) | collective-permute-done | bytes 196640 | tf_op jit(solution)/shard_map/ppermute | solution.py:15
  42.4 3.2 %collective-permute-done.13.rest_1_ = bf16[256,384]{1,0:T(8,128)(2,1)S(1)} collective-permute-done((bf16[256,384]{1,0:T(8,128)(2,1)S(1)}, bf16[256,384]{1,0:T(8,128)(2,1)S(1)}, u32[]{:S(2)}, u32[]{:S(2)}) %collective-permute-start.13) | collective-permute-done | bytes 196640 | tf_op jit(solution)/shard_map/ppermute | solution.py:15
  45.7 1.4 %shard_map.32 = (f32[2,512,256]{2,1,0:T(8,128)S(1)}, f32[2,512,256]{2,1,0:T(8,128)S(1)}) custom-call(s32[2]{0:T(128)S(1)} %pad_add_fusion.where_ref, bf16[512,384]{1,0:T(8,128)(2,1)S(1)} %shard_map.28.left_ref, f32[2,384]{1,0:T(2,128)S(1)} %add.28.sums_ref, ...), custom_call_target="tpu_custom_call", output_to_operand_aliasing={{0}: (6, {}), {1}: (7, {})} | custom-call | flops 201326592 | bytes 524288 | tf_op jit(solution)/shard_map/pallas_call | solution.py:40
  47.1 0.1 collective-permute-start.14
  47.1 4.4 %collective-permute-start.6 = (bf16[256,384]{1,0:T(8,128)(2,1)S(1)}, bf16[256,384]{1,0:T(8,128)(2,1)S(1)}, u32[]{:S(2)}, u32[]{:S(2)}) collective-permute-start(bf16[256,384]{1,0:T(8,128)(2,1)S(1)} %collective-permute-done.5.rest_2_), channel_id=1, source_target_pairs={{0,4},{8,12},{16,20},{24,28},{1,5},{9,13},{17,21},{25,29},{2,6},{1... | collective-permute-start | bytes 589832 | tf_op jit(solution)/shard_map/ppermute | solution.py:15
  51.5 1.2 %shard_map.29 = (f32[2,512,128]{2,1,0:T(8,128)S(1)}, f32[2,512,128]{2,1,0:T(8,128)S(1)}) custom-call(s32[2]{0:T(128)S(1)} %pad_add_fusion.where_ref, bf16[512,384]{1,0:T(8,128)(2,1)S(1)} %shard_map.28.left_ref, f32[2,384]{1,0:T(2,128)S(1)} %add.28.sums_ref, bf16[512,384]{1,0:T(8,128)(2,1)S(1)} %collective-permute-done.7.rest_0_.rest_1_, ...), custom_call_target="tpu_custom_call" | custom-call | flops 100663296 | bytes 262144 | tf_op jit(solution)/shard_map/pallas_call | solution.py:40
  52.8 3.6 %collective-permute-done.6.rest_1_ = bf16[256,384]{1,0:T(8,128)(2,1)S(1)} collective-permute-done((bf16[256,384]{1,0:T(8,128)(2,1)S(1)}, bf16[256,384]{1,0:T(8,128)(2,1)S(1)}, u32[]{:S(2)}, u32[]{:S(2)}) %collective-permute-start.6) | collective-permute-done | bytes 196640 | tf_op jit(solution)/shard_map/ppermute | solution.py:15
  56.3 1.2 %shard_map.30 = (f32[2,512,128]{2,1,0:T(8,128)S(1)}, f32[2,512,128]{2,1,0:T(8,128)S(1)}) custom-call(s32[2]{0:T(128)S(1)} %pad_add_fusion.where_ref, bf16[512,384]{1,0:T(8,128)(2,1)S(1)} %shard_map.28.left_ref, f32[2,384]{1,0:T(2,128)S(1)} %add.28.sums_ref, ...), custom_call_target="tpu_custom_call", output_to_operand_aliasing={{0}: (5, {}), {1}: (6, {})} | custom-call | flops 100663296 | bytes 262144 | tf_op jit(solution)/shard_map/pallas_call | solution.py:40
  57.5 0.1 collective-permute-start.10
  57.6 0.0 collective-permute-done.16.other_ref
  57.6 0.1 fusion.5
  57.7 1.6 %collective-permute-start.17 = (f16[512,256]{1,0:T(8,128)(2,1)S(1)}, f16[512,256]{1,0:T(8,128)(2,1)S(1)}, u32[]{:S(2)}, u32[]{:S(2)}) collective-permute-start(f16[512,256]{1,0:T(8,128)(2,1)S(1)} %fusion.5), channel_id=1, source_target_pairs={{0,2},{1,3},{2,0},{3,1},{4,6},{5,7},{6,4},{7,5},{8,10},{9,11},{10,... | collective-permute-start | bytes 786440 | tf_op jit(solution)/shard_map/ppermute | solution.py:15
  59.3 0.0 collective-permute-done.14.other_ref
  59.3 0.1 fusion.4
  59.4 0.6 collective-permute-start.15
  60.0 0.0 collective-permute-done.10.other_ref
  60.0 1.6 %collective-permute-start.11 = (f16[512,128]{1,0:T(8,128)(2,1)S(1)}, f16[512,128]{1,0:T(8,128)(2,1)S(1)}, u32[]{:S(2)}, u32[]{:S(2)}) collective-permute-start(f16[512,128]{1,0:T(8,128)(2,1)S(1)} %fusion.8), channel_id=1, source_target_pairs={{0,2},{1,3},{2,0},{3,1},{4,6},{5,7},{6,4},{7,5},{8,10},{9,11},{10,... | collective-permute-start | bytes 393224 | tf_op jit(solution)/shard_map/ppermute | solution.py:15
  61.6 5.4 %collective-permute-done.17 = f16[512,256]{1,0:T(8,128)(2,1)S(1)} collective-permute-done((f16[512,256]{1,0:T(8,128)(2,1)S(1)}, f16[512,256]{1,0:T(8,128)(2,1)S(1)}, u32[]{:S(2)}, u32[]{:S(2)}) %collective-permute-start.17) | collective-permute-done | bytes 262176 | tf_op jit(solution)/shard_map/ppermute | solution.py:15
  67.0 1.4 %shard_map.35.rest_0_ = f32[512,640]{1,0:T(8,128)} custom-call(s32[2]{0:T(128)S(1)} %pad_add_fusion.where_ref, f32[2,512,256]{2,1,0:T(8,128)S(1)} %get-tuple-element.35.keep_ref, f32[2,512,256]{2,1,0:T(8,128)S(1)} %collective-permute-done.16.other_ref, f32[512,256]{1,0:T(8,128)S(1)} %convert_element_type.35.got_ref), custom_call_target="tpu_custom_call" | custom-call | flops 131072 | bytes 524288 | tf_op jit(solution)/shard_map/pallas_call | solution.py:40
  68.5 4.1 %collective-permute-done.15 = f16[512,256]{1,0:T(8,128)(2,1)S(1)} collective-permute-done((f16[512,256]{1,0:T(8,128)(2,1)S(1)}, f16[512,256]{1,0:T(8,128)(2,1)S(1)}, u32[]{:S(2)}, u32[]{:S(2)}) %collective-permute-start.15) | collective-permute-done | bytes 262176 | tf_op jit(solution)/shard_map/ppermute | solution.py:15
  72.6 2.3 %collective-permute-done.11 = f16[512,128]{1,0:T(8,128)(2,1)S(1)} collective-permute-done((f16[512,128]{1,0:T(8,128)(2,1)S(1)}, f16[512,128]{1,0:T(8,128)(2,1)S(1)}, u32[]{:S(2)}, u32[]{:S(2)}) %collective-permute-start.11) | collective-permute-done | bytes 131104 | tf_op jit(solution)/shard_map/ppermute | solution.py:15
  74.9 1.4 %shard_map.36.rest_0_ = f32[512,640]{1,0:T(8,128)} custom-call(s32[2]{0:T(128)S(1)} %pad_add_fusion.where_ref, f32[2,512,256]{2,1,0:T(8,128)S(1)} %get-tuple-element.31.keep_ref, f32[2,512,256]{2,1,0:T(8,128)S(1)} %collective-permute-done.14.other_ref, f32[512,256]{1,0:T(8,128)S(1)} %convert_element_type.32.got_ref, ...), custom_call_target="tpu_custom_call", output_to_operand_aliasing={{}: (4, {})} | custom-call | flops 131072 | bytes 524288 | tf_op jit(solution)/shard_map/pallas_call | solution.py:40
  76.4 1.3 %shard_map.37 = f32[512,640]{1,0:T(8,128)} custom-call(s32[2]{0:T(128)S(1)} %pad_add_fusion.where_ref, f32[2,512,128]{2,1,0:T(8,128)S(1)} %get-tuple-element.27.keep_ref, f32[2,512,128]{2,1,0:T(8,128)S(1)} %collective-permute-done.10.other_ref, f32[512,128]{1,0:T(8,128)S(1)} %convert_element_type.29.got_ref, ...), custom_call_target="tpu_custom_call", output_to_operand_aliasing={{}: (4, {})} | custom-call | flops 65536 | bytes 262144 | tf_op jit(solution)/shard_map/pallas_call | solution.py:40
  (7 shorter events, 0.1 us)
Async XLA Ops:
  1.5 10.4 %collective-permute-start.8 = (bf16[256,384]{1,0:T(8,128)(2,1)S(1)}, bf16[256,384]{1,0:T(8,128)(2,1)S(1)}, u32[]{:S(2)}, u32[]{:S(2)}) collective-permute-start(bf16[256,384]{1,0:T(8,128)(2,1)S(1)} %get-tuple-element.24), channel_id=1, source_target_pairs={{0,24},{4,28},{8,0},{12,4},{16,8},{20,12},{24,16},{28,20},{1,25},{... | collective-permute-start | bytes 589832 | tf_op jit(solution)/shard_map/ppermute | solution.py:15
  6.6 26.6 %collective-permute-start.7 = (bf16[512,384]{1,0:T(8,128)(2,1)S(1)}, bf16[512,384]{1,0:T(8,128)(2,1)S(1)}, u32[]{:S(2)}, u32[]{:S(2)}) collective-permute-start(bf16[512,384]{1,0:T(8,128)(2,1)S(1)} %get-tuple-element.21.calls_ref.rest_0_), channel_id=1, source_target_pairs={{4,0},{12,8},{20,16},{28,24},{5,1},{13,9},{21,17},{29,25},{6,2},{1... | collective-permute-start | bytes 1179656 | tf_op jit(solution)/shard_map/ppermute | solution.py:15
  7.9 20.2 %collective-permute-start.3 = (bf16[256,384]{1,0:T(8,128)(2,1)S(1)}, bf16[256,384]{1,0:T(8,128)(2,1)S(1)}, u32[]{:S(2)}, u32[]{:S(2)}) collective-permute-start(bf16[256,384]{1,0:T(8,128)(2,1)S(1)} %get-tuple-element.23), channel_id=1, source_target_pairs={{0,24},{4,28},{8,0},{12,4},{16,8},{20,12},{24,16},{28,20},{1,25},{... | collective-permute-start | bytes 589832 | tf_op jit(solution)/shard_map/ppermute | solution.py:15
  11.9 17.9 %collective-permute-start.12 = (bf16[256,384]{1,0:T(8,128)(2,1)S(1)}, bf16[256,384]{1,0:T(8,128)(2,1)S(1)}, u32[]{:S(2)}, u32[]{:S(2)}) collective-permute-start(bf16[256,384]{1,0:T(8,128)(2,1)S(1)} %collective-permute-done.8.rest_1_), channel_id=1, source_target_pairs={{0,24},{4,28},{8,0},{12,4},{16,8},{20,12},{24,16},{28,20},{1,25},{... | collective-permute-start | bytes 589832 | tf_op jit(solution)/shard_map/ppermute | solution.py:15
  16.2 3.6 %collective-permute-start = (f32[2,384]{1,0:T(2,128)S(1)}, f32[2,384]{1,0:T(2,128)S(1)}, u32[]{:S(2)}, u32[]{:S(2)}) collective-permute-start(f32[2,384]{1,0:T(2,128)S(1)} %get-tuple-element.22), channel_id=1, source_target_pairs={{0,4},{4,0},{8,12},{12,8},{16,20},{20,16},{24,28},{28,24},{1,5},{5... | collective-permute-start | bytes 9224 | tf_op jit(solution)/shard_map/ppermute | solution.py:15
  19.8 3.6 %collective-permute-start.1 = (f32[2,384]{1,0:T(2,128)S(1)}, f32[2,384]{1,0:T(2,128)S(1)}, u32[]{:S(2)}, u32[]{:S(2)}) collective-permute-start(f32[2,384]{1,0:T(2,128)S(1)} %add.26), channel_id=1, source_target_pairs={{0,8},{4,12},{8,0},{12,4},{16,24},{20,28},{24,16},{28,20},{1,9},{5... | collective-permute-start | bytes 9224 | tf_op jit(solution)/shard_map/ppermute | solution.py:15
  23.4 4.5 %collective-permute-start.2 = (f32[2,384]{1,0:T(2,128)S(1)}, f32[2,384]{1,0:T(2,128)S(1)}, u32[]{:S(2)}, u32[]{:S(2)}) collective-permute-start(f32[2,384]{1,0:T(2,128)S(1)} %add.27), channel_id=1, source_target_pairs={{0,16},{4,20},{8,24},{12,28},{16,0},{20,4},{24,8},{28,12},{1,17},{... | collective-permute-start | bytes 9224 | tf_op jit(solution)/shard_map/ppermute | solution.py:15
  30.8 26.8 %collective-permute-start.16 = (f32[2,512,256]{2,1,0:T(8,128)S(1)}, f32[2,512,256]{2,1,0:T(8,128)S(1)}, u32[]{:S(2)}, u32[]{:S(2)}) collective-permute-start(f32[2,512,256]{2,1,0:T(8,128)S(1)} %get-tuple-element.36), channel_id=1, source_target_pairs={{0,1},{1,0},{2,3},{3,2},{4,5},{5,4},{6,7},{7,6},{8,9},{9,8},{10,11... | collective-permute-start | bytes 3145736 | tf_op jit(solution)/shard_map/ppermute | solution.py:15
  30.9 7.8 %collective-permute-start.4 = (bf16[256,384]{1,0:T(8,128)(2,1)S(1)}, bf16[256,384]{1,0:T(8,128)(2,1)S(1)}, u32[]{:S(2)}, u32[]{:S(2)}) collective-permute-start(bf16[256,384]{1,0:T(8,128)(2,1)S(1)} %collective-permute-done.3.rest_2_), channel_id=1, source_target_pairs={{0,4},{4,0},{8,12},{12,8},{16,20},{20,16},{24,28},{28,24},{1,5},{5... | collective-permute-start | bytes 589832 | tf_op jit(solution)/shard_map/ppermute | solution.py:15
  32.5 7.6 %collective-permute-start.5 = (bf16[256,384]{1,0:T(8,128)(2,1)S(1)}, bf16[256,384]{1,0:T(8,128)(2,1)S(1)}, u32[]{:S(2)}, u32[]{:S(2)}) collective-permute-start(bf16[256,384]{1,0:T(8,128)(2,1)S(1)} %collective-permute-done.3.rest_2_), channel_id=1, source_target_pairs={{0,24},{4,28},{8,0},{12,4},{16,8},{20,12},{24,16},{28,20},{1,25},{... | collective-permute-start | bytes 589832 | tf_op jit(solution)/shard_map/ppermute | solution.py:15
  32.8 9.7 %collective-permute-start.9 = (bf16[256,384]{1,0:T(8,128)(2,1)S(1)}, bf16[256,384]{1,0:T(8,128)(2,1)S(1)}, u32[]{:S(2)}, u32[]{:S(2)}) collective-permute-start(bf16[256,384]{1,0:T(8,128)(2,1)S(1)} %collective-permute-done.8.rest_1_), channel_id=1, source_target_pairs={{0,4},{4,0},{8,12},{12,8},{16,20},{20,16},{24,28},{28,24},{1,5},{5... | collective-permute-start | bytes 589832 | tf_op jit(solution)/shard_map/ppermute | solution.py:15
  33.3 12.4 %collective-permute-start.13 = (bf16[256,384]{1,0:T(8,128)(2,1)S(1)}, bf16[256,384]{1,0:T(8,128)(2,1)S(1)}, u32[]{:S(2)}, u32[]{:S(2)}) collective-permute-start(bf16[256,384]{1,0:T(8,128)(2,1)S(1)} %collective-permute-done.12.rest_0_), channel_id=1, source_target_pairs={{0,4},{8,12},{16,20},{24,28},{1,5},{9,13},{17,21},{25,29},{2,6},{1... | collective-permute-start | bytes 589832 | tf_op jit(solution)/shard_map/ppermute | solution.py:15
  47.1 12.2 %collective-permute-start.14 = (f32[2,512,256]{2,1,0:T(8,128)S(1)}, f32[2,512,256]{2,1,0:T(8,128)S(1)}, u32[]{:S(2)}, u32[]{:S(2)}) collective-permute-start(f32[2,512,256]{2,1,0:T(8,128)S(1)} %get-tuple-element.32), channel_id=1, source_target_pairs={{0,1},{1,0},{2,3},{3,2},{4,5},{5,4},{6,7},{7,6},{8,9},{9,8},{10,11... | collective-permute-start | bytes 3145736 | tf_op jit(solution)/shard_map/ppermute | solution.py:15
  47.1 9.2 %collective-permute-start.6 = (bf16[256,384]{1,0:T(8,128)(2,1)S(1)}, bf16[256,384]{1,0:T(8,128)(2,1)S(1)}, u32[]{:S(2)}, u32[]{:S(2)}) collective-permute-start(bf16[256,384]{1,0:T(8,128)(2,1)S(1)} %collective-permute-done.5.rest_2_), channel_id=1, source_target_pairs={{0,4},{8,12},{16,20},{24,28},{1,5},{9,13},{17,21},{25,29},{2,6},{1... | collective-permute-start | bytes 589832 | tf_op jit(solution)/shard_map/ppermute | solution.py:15
  57.5 2.4 %collective-permute-start.10 = (f32[2,512,128]{2,1,0:T(8,128)S(1)}, f32[2,512,128]{2,1,0:T(8,128)S(1)}, u32[]{:S(2)}, u32[]{:S(2)}) collective-permute-start(f32[2,512,128]{2,1,0:T(8,128)S(1)} %get-tuple-element.28), channel_id=1, source_target_pairs={{0,1},{1,0},{2,3},{3,2},{4,5},{5,4},{6,7},{7,6},{8,9},{9,8},{10,11... | collective-permute-start | bytes 1572872 | tf_op jit(solution)/shard_map/ppermute | solution.py:15
  57.7 9.2 %collective-permute-start.17 = (f16[512,256]{1,0:T(8,128)(2,1)S(1)}, f16[512,256]{1,0:T(8,128)(2,1)S(1)}, u32[]{:S(2)}, u32[]{:S(2)}) collective-permute-start(f16[512,256]{1,0:T(8,128)(2,1)S(1)} %fusion.5), channel_id=1, source_target_pairs={{0,2},{1,3},{2,0},{3,1},{4,6},{5,7},{6,4},{7,5},{8,10},{9,11},{10,... | collective-permute-start | bytes 786440 | tf_op jit(solution)/shard_map/ppermute | solution.py:15
  59.4 13.2 %collective-permute-start.15 = (f16[512,256]{1,0:T(8,128)(2,1)S(1)}, f16[512,256]{1,0:T(8,128)(2,1)S(1)}, u32[]{:S(2)}, u32[]{:S(2)}) collective-permute-start(f16[512,256]{1,0:T(8,128)(2,1)S(1)} %fusion.4), channel_id=1, source_target_pairs={{0,2},{1,3},{2,0},{3,1},{4,6},{5,7},{6,4},{7,5},{8,10},{9,11},{10,... | collective-permute-start | bytes 786440 | tf_op jit(solution)/shard_map/ppermute | solution.py:15
  60.0 14.9 %collective-permute-start.11 = (f16[512,128]{1,0:T(8,128)(2,1)S(1)}, f16[512,128]{1,0:T(8,128)(2,1)S(1)}, u32[]{:S(2)}, u32[]{:S(2)}) collective-permute-start(f16[512,128]{1,0:T(8,128)(2,1)S(1)} %fusion.8), channel_id=1, source_target_pairs={{0,2},{1,3},{2,0},{3,1},{4,6},{5,7},{6,4},{7,5},{8,10},{9,11},{10,... | collective-permute-start | bytes 393224 | tf_op jit(solution)/shard_map/ppermute | solution.py:15

commit v3 on v2

--- a/solution.py
+++ b/solution.py
@@ -48,7 +48,6 @@
 
 
 VMEM = pl.BlockSpec(memory_space=pltpu.VMEM)
-SMEM = pl.BlockSpec(memory_space=pltpu.SMEM)
 ANY = pl.BlockSpec(memory_space=pl.ANY)
 
 
@@ -110,8 +109,11 @@
     return jnp.where(wide > 0.0, (wide - shift) * scale, 0.0).astype(jnp.bfloat16)
 
 
-def left_body(calls_ref, sums_ref, left_ref):
-    left_ref[...] = standardized(calls_ref[...], *factors(sums_ref[...]))
+def left_body(calls_ref, sums_ref, more_ref, left_ref, factors_ref):
+    shift, scale = factors(sums_ref[...] + more_ref[...])
+    factors_ref[0:1, :] = shift
+    factors_ref[1:2, :] = scale
+    left_ref[...] = standardized(calls_ref[...], shift, scale)
 
 
 def multiply(left, right):
@@ -120,9 +122,11 @@
     )
 
 
-def products_body(cases, where_ref, left_ref, sums_ref, *rest):
+def products_body(cases, down, left_ref, factors_ref, *rest):
     *refs, keep_ref, away_ref, right_ref = rest
-    shift, scale = factors(sums_ref[...])
+    shift, scale = factors_ref[0:1, :], factors_ref[1:2, :]
+    device = lax.axis_index("snps")
+    parity = lax.axis_index("samples") % 2
     for strip, by_parity in cases:
         for odd, (at, begin) in enumerate(by_parity):
 
@@ -131,29 +135,30 @@
                 right_ref[...] = standardized(rows, shift, scale)
 
             if by_parity[0] != by_parity[1]:
-                pl.when(where_ref[1] == odd)(fill)
+                pl.when(parity == odd)(fill)
             elif not odd:
                 fill()
-        place = where_ref[0] ^ strip
+        place = device ^ strip
         for bit, target_ref in enumerate((keep_ref, away_ref)):
 
             @pl.when(place % 2 == bit)
             def _(target_ref=target_ref, place=place):
-                target_ref[place // 2] = multiply(left_ref[...], right_ref[...])
-
-
-def products_more_body(cases, where_ref, left_ref, sums_ref, *rest):
+                target_ref[place // 2] = multiply(left_ref[...], right_ref[...]) * down
+
+
+def products_more_body(cases, down, left_ref, factors_ref, *rest):
     *refs, _, _, keep_ref, away_ref, right_ref = rest
-    products_body(cases, where_ref, left_ref, sums_ref, *refs, keep_ref, away_ref, right_ref)
-
-
-def add_body(places, up, where_ref, keep_ref, other_ref, got_ref, *rest):
+    products_body(cases, down, left_ref, factors_ref, *refs, keep_ref, away_ref, right_ref)
+
+
+def add_body(places, up, ours_ref, got_ref, *rest):
     out_ref, total_ref, sem = rest[-3:]
-    total_ref[...] = (keep_ref[0] + other_ref[0]) * up[0] + got_ref[...] * up[1]
+    total_ref[...] = (ours_ref[...] + got_ref[...]) * up
+    device = lax.axis_index("snps")
     width = total_ref.shape[1]
     for strip, begin in enumerate(places):
 
-        @pl.when(where_ref[0] == strip)
+        @pl.when(device == strip)
         def _(begin=begin):
             copy = pltpu.make_async_copy(total_ref, out_ref.at[:, pl.ds(begin, width)], sem)
             copy.start()
@@ -177,16 +182,12 @@
     for _ in range(1, turns + 1):
         line.append([send(line[-1][h], "samples", along) for h in range(2)])
     beside = send(calls, "samples", lambda s: s - 1 if s % 2 else None)
-    side = [None]
-    for t in range(1, turns):
-        side.append([send(line[t][h], "samples", lambda s: s ^ 1) for h in range(2)])
-    side.append([
-        send(line[turns][h], "samples", lambda s: None if s % 2 else s + 1)
-        for h in range(2)
-    ])
+    side = [None] + [[send(line[t][h], "samples", lambda s: s ^ 1) for h in range(2)] for t in range(1, turns + 1)]
 
     for bit in range(samples.bit_length() - 1):
-        sums = sums + send(sums, "samples", lambda s, step=1 << bit: s ^ step)
+        more = send(sums, "samples", lambda s, step=1 << bit: s ^ step)
+        if 2 << bit < samples:
+            sums = sums + more
 
     def source(k, h, odd):
         if k == 0:
@@ -197,13 +198,11 @@
             return beside, h * half_rows
         return side[(k + odd) // 2][h], 0
 
-    left = call_kernel(
-        left_body, jax.ShapeDtypeStruct((rows, snp_part), jnp.bfloat16), (calls, sums),
-        [VMEM] * 2, 5 * rows * snp_part, 4 * rows * snp_part, out_specs=VMEM,
+    left, pair = call_kernel(
+        left_body,
+        (jax.ShapeDtypeStruct((rows, snp_part), jnp.bfloat16), jax.ShapeDtypeStruct((2, snp_part), jnp.float32)),
+        (calls, sums, more), [VMEM] * 3, 5 * rows * snp_part, 4 * rows * snp_part, out_specs=(VMEM, VMEM),
     )
-    device = lax.axis_index("snps").astype(jnp.int32)
-    parity = (lax.axis_index("samples") % 2).astype(jnp.int32)
-    where = jnp.stack([device, parity])
     table = strips(samples)
     bound = snp_total / 2 * 4 * (samples * rows + 1) / 3
     down = 2.0 ** -math.ceil(math.log2(bound / 32768.0))
@@ -226,10 +225,10 @@
                 by_parity.append((at, begin))
             cases.append((strip, tuple(by_parity)))
         shape = jax.ShapeDtypeStruct((2, rows, columns), jnp.float32)
-        operands = (where, left, sums, *arrays, *so_far)
+        operands = (left, pair, *arrays, *so_far)
         return call_kernel(
-            functools.partial(products_body if not so_far else products_more_body, tuple(cases)),
-            (shape, shape), operands, [SMEM] + [VMEM] * (len(operands) - 1),
+            functools.partial(products_body if not so_far else products_more_body, tuple(cases), down),
+            (shape, shape), operands, [VMEM] * len(operands),
             2 * rows * snp_part * columns * len(chosen), 4 * rows * columns,
             out_specs=(VMEM, VMEM),
             scratch_shapes=[pltpu.VMEM((columns, snp_part), jnp.bfloat16)],
@@ -247,10 +246,9 @@
             if chosen:
                 both = products(n, chosen, both)
         keep, away = both
-        other = swap_core(away)
-        theirs = ((keep[1] + other[1]) * down).astype(jnp.float16)
-        got = send(theirs, "snps", lambda s: s ^ 2).astype(jnp.float32)
-        pieces.append((keep, other, got))
+        summed = keep + swap_core(away.astype(jnp.float16)).astype(jnp.float32)
+        got = send(summed[1].astype(jnp.float16), "snps", lambda s: s ^ 2)
+        pieces.append((summed[0], got.astype(jnp.float32)))
     out = None
     for n, operands in enumerate(pieces):
         places = []
@@ -259,13 +257,13 @@
                 places.append(natural.index(by_arrival[n]) * half_rows + (strip % 2) * quarter)
             else:
                 places.append(0 if strip % 2 else count * half_rows)
-        columns = operands[2].shape[1]
+        columns = operands[1].shape[1]
         last = () if out is None else (out,)
-        operands = (where, *operands, *last)
+        operands = (*operands, *last)
         out = call_kernel(
-            functools.partial(add_body, tuple(places), (1.0 / snp_total, 1.0 / (down * snp_total))),
+            functools.partial(add_body, tuple(places), 1.0 / (down * snp_total)),
             jax.ShapeDtypeStruct((rows, width), jnp.float32), operands,
-            [SMEM] + [VMEM] * 3 + [ANY] * len(last), rows * columns, 4 * rows * columns,
+            [VMEM] * 2 + [ANY] * len(last), rows * columns, 4 * rows * columns,
             out_specs=ANY,
             scratch_shapes=[pltpu.VMEM((rows, columns), jnp.float32), pltpu.SemaphoreType.DMA],
             input_output_aliases={len(operands) - 1: 0} if last else {},

time: 77.9 us -> 71 us (0.911)
  Pallas kernels: 13.8 us -> 8.67 us
  starting transfers between devices: 26.8 us -> 24.6 us
    pallas_call x10, Pallas kernels: 12.3 us -> 7.17 us  [call_kernel(): pl.pallas_call(body, out_shape=shapes, in_specs=specs, compiler_params=pl...]
    ppermute x18, starting transfers between devices: 26.8 us -> 24.6 us  [send(): lax.ppermute(value, axis, [pair for pair in pairs if pair[1] is not None])]
  transfers between devices with their start and end apart: 18 -> 18, of which waited for: 11 -> 8; matrix products, arithmetic and copies ran while one was open for 0% -> 1% of each run, Pallas kernels for 12% -> 8%
where the time goes in v3:
time: 71 us; the launch traced here: 70.9 us
  waiting for transfers between devices  36.5 us (51%)
  starting transfers between devices  24.6 us (35%)
  Pallas kernels  8.67 us (12%)
  other arithmetic  0.81 us (1%)
    ppermute x18, waiting for transfers between devices, send(): lax.ppermute(value, axis, [pair for pair in pairs if pair[1] is not None])  36.5 us
    ppermute x18, starting transfers between devices, send(): lax.ppermute(value, axis, [pair for pair in pairs if pair[1] is not None])  24.6 us
    pallas_call x10, Pallas kernels, call_kernel(): pl.pallas_call(body, out_shape=shapes, in_specs=specs, compiler_params=pl...  7.17 us
    pallas_call x1, Pallas kernels, encode(): pl.pallas_call(encode_body, name='encode', out_shape=(calls(rows), calls(...  1.49 us
  transfers between devices with their start and end apart: 18, of which 8 were waited for; matrix products, arithmetic and copies ran while one was open for 1% of the time, Pallas kernels for 8%

profile of v3, /device:TPU:0, one launch (start us, length us, event | category | flops | bytes accessed | tf_op | source)
XLA Modules:
  0.0 70.9 jit_solution(4695449724682661858)
XLA Ops:
  0.0 1.5 %encode.1 = (bf16[512,384]{1,0:T(8,128)(2,1)S(1)}, bf16[256,384]{1,0:T(8,128)(2,1)S(1)}, bf16[256,384]{1,0:T(8,128)(2,1)S(1)}, f32[2,384]{1,0:T(2,128)S(1)}) custom-call(s32[512,384]{1,0:T(8,128)} %genotype_ref.1, s32[512,384]{1,0:T(8,128)} %mask_ref.1), custom_call_target="tpu_custom_call" | custom-call | tf_op jit(solution)/shard_map/encode/pallas_call | solution.py:87
  1.5 5.1 %collective-permute-start.3 = (bf16[256,384]{1,0:T(8,128)(2,1)S(1)}, bf16[256,384]{1,0:T(8,128)(2,1)S(1)}, u32[]{:S(2)}, u32[]{:S(2)}) collective-permute-start(bf16[256,384]{1,0:T(8,128)(2,1)S(1)} %get-tuple-element.27), channel_id=1, source_target_pairs={{0,24},{4,28},{8,0},{12,4},{16,8},{20,12},{24,16},{28,20},{1,25},{... | collective-permute-start | bytes 589832 | tf_op jit(solution)/shard_map/ppermute | solution.py:15
  6.6 0.4 collective-permute-start.8
  7.1 1.3 %collective-permute-start.7 = (bf16[512,384]{1,0:T(8,128)(2,1)S(1)}, bf16[512,384]{1,0:T(8,128)(2,1)S(1)}, u32[]{:S(2)}, u32[]{:S(2)}) collective-permute-start(bf16[512,384]{1,0:T(8,128)(2,1)S(1)} %get-tuple-element.23.calls_ref.rest_0_), channel_id=1, source_target_pairs={{4,0},{12,8},{20,16},{28,24},{5,1},{13,9},{21,17},{29,25},{6,2},{1... | collective-permute-start | bytes 1179656 | tf_op jit(solution)/shard_map/ppermute | solution.py:15
  8.4 3.6 %collective-permute-done.3.rest_2_ = bf16[256,384]{1,0:T(8,128)(2,1)S(1)} collective-permute-done((bf16[256,384]{1,0:T(8,128)(2,1)S(1)}, bf16[256,384]{1,0:T(8,128)(2,1)S(1)}, u32[]{:S(2)}, u32[]{:S(2)}) %collective-permute-start.3) | collective-permute-done | bytes 196640 | tf_op jit(solution)/shard_map/ppermute | solution.py:15
  11.9 4.3 %collective-permute-start.5 = (bf16[256,384]{1,0:T(8,128)(2,1)S(1)}, bf16[256,384]{1,0:T(8,128)(2,1)S(1)}, u32[]{:S(2)}, u32[]{:S(2)}) collective-permute-start(bf16[256,384]{1,0:T(8,128)(2,1)S(1)} %collective-permute-done.3.rest_2_), channel_id=1, source_target_pairs={{0,24},{4,28},{8,0},{12,4},{16,8},{20,12},{24,16},{28,20},{1,25},{... | collective-permute-start | bytes 589832 | tf_op jit(solution)/shard_map/ppermute | solution.py:15
  16.2 0.0 collective-permute-done.8.rest_1_
  16.2 3.9 %collective-permute-start.12 = (bf16[256,384]{1,0:T(8,128)(2,1)S(1)}, bf16[256,384]{1,0:T(8,128)(2,1)S(1)}, u32[]{:S(2)}, u32[]{:S(2)}) collective-permute-start(bf16[256,384]{1,0:T(8,128)(2,1)S(1)} %collective-permute-done.8.rest_1_), channel_id=1, source_target_pairs={{0,24},{4,28},{8,0},{12,4},{16,8},{20,12},{24,16},{28,20},{1,25},{... | collective-permute-start | bytes 589832 | tf_op jit(solution)/shard_map/ppermute | solution.py:15
  20.1 1.5 %collective-permute-start.9 = (bf16[256,384]{1,0:T(8,128)(2,1)S(1)}, bf16[256,384]{1,0:T(8,128)(2,1)S(1)}, u32[]{:S(2)}, u32[]{:S(2)}) collective-permute-start(bf16[256,384]{1,0:T(8,128)(2,1)S(1)} %collective-permute-done.8.rest_1_), channel_id=1, source_target_pairs={{0,4},{4,0},{8,12},{12,8},{16,20},{20,16},{24,28},{28,24},{1,5},{5... | collective-permute-start | bytes 589832 | tf_op jit(solution)/shard_map/ppermute | solution.py:15
  21.6 0.5 collective-permute-start
  22.2 3.7 %collective-permute-done = f32[2,384]{1,0:T(2,128)S(1)} collective-permute-done((f32[2,384]{1,0:T(2,128)S(1)}, f32[2,384]{1,0:T(2,128)S(1)}, u32[]{:S(2)}, u32[]{:S(2)}) %collective-permute-start) | collective-permute-done | bytes 3104 | tf_op jit(solution)/shard_map/ppermute | solution.py:15
  25.8 0.0 collective-permute-start.1
  25.8 3.6 %collective-permute-done.1 = f32[2,384]{1,0:T(2,128)S(1)} collective-permute-done((f32[2,384]{1,0:T(2,128)S(1)}, f32[2,384]{1,0:T(2,128)S(1)}, u32[]{:S(2)}, u32[]{:S(2)}) %collective-permute-start.1) | collective-permute-done | bytes 3104 | tf_op jit(solution)/shard_map/ppermute | solution.py:15
  29.4 0.0 collective-permute-start.2
  29.4 4.5 %collective-permute-done.2.more_ref = f32[2,384]{1,0:T(2,128)S(1)} collective-permute-done((f32[2,384]{1,0:T(2,128)S(1)}, f32[2,384]{1,0:T(2,128)S(1)}, u32[]{:S(2)}, u32[]{:S(2)}) %collective-permute-start.2) | collective-permute-done | bytes 3104 | tf_op jit(solution)/shard_map/ppermute | solution.py:15
  33.9 1.5 %collective-permute-start.4 = (bf16[256,384]{1,0:T(8,128)(2,1)S(1)}, bf16[256,384]{1,0:T(8,128)(2,1)S(1)}, u32[]{:S(2)}, u32[]{:S(2)}) collective-permute-start(bf16[256,384]{1,0:T(8,128)(2,1)S(1)} %collective-permute-done.3.rest_2_), channel_id=1, source_target_pairs={{0,4},{4,0},{8,12},{12,8},{16,20},{20,16},{24,28},{28,24},{1,5},{5... | collective-permute-start | bytes 589832 | tf_op jit(solution)/shard_map/ppermute | solution.py:15
  35.4 0.0 collective-permute-done.5.rest_2_
  35.5 0.5 collective-permute-start.6
  36.0 0.2 shard_map.28
  36.1 1.2 %shard_map.33 = (f32[2,512,256]{2,1,0:T(8,128)S(1)}, f32[2,512,256]{2,1,0:T(8,128)S(1)}) custom-call(bf16[512,384]{1,0:T(8,128)(2,1)S(1)} %get-tuple-element.25.left_ref, f32[2,384]{1,0:T(2,128)S(1)} %get-tuple-element.26.factors_ref, bf16[512,384]{1,0:T(8,128)(2,1)S(1)} %get-tuple-element.23.calls_ref.rest_0_, ...), custom_call_target="tpu_custom_call" | custom-call | flops 301989888 | bytes 524288 | tf_op jit(solution)/shard_map/pallas_call | solution.py:40
  37.3 0.0 collective-permute-done.12.rest_0_
  37.4 0.4 shard_map.34
  37.8 0.1 convert_element_type.47
  37.9 0.1 collective-permute-start.16
  37.9 0.0 collective-permute-done.9.rest_1_.rest_0_
  38.0 0.0 collective-permute-done.7.rest_0_.rest_1_
  38.0 0.7 shard_map.29
  38.6 1.0 %collective-permute-done.4.rest_0_.rest_2_ = bf16[256,384]{1,0:T(8,128)(2,1)S(1)} collective-permute-done((bf16[256,384]{1,0:T(8,128)(2,1)S(1)}, bf16[256,384]{1,0:T(8,128)(2,1)S(1)}, u32[]{:S(2)}, u32[]{:S(2)}) %collective-permute-start.4) | collective-permute-done | bytes 196640 | tf_op jit(solution)/shard_map/ppermute | solution.py:15
  39.6 2.1 %collective-permute-done.6.rest_1_ = bf16[256,384]{1,0:T(8,128)(2,1)S(1)} collective-permute-done((bf16[256,384]{1,0:T(8,128)(2,1)S(1)}, bf16[256,384]{1,0:T(8,128)(2,1)S(1)}, u32[]{:S(2)}, u32[]{:S(2)}) %collective-permute-start.6) | collective-permute-done | bytes 196640 | tf_op jit(solution)/shard_map/ppermute | solution.py:15
  41.7 0.6 shard_map.30
  42.4 0.1 collective-permute-start.10
  42.5 1.6 %collective-permute-start.13 = (bf16[256,384]{1,0:T(8,128)(2,1)S(1)}, bf16[256,384]{1,0:T(8,128)(2,1)S(1)}, u32[]{:S(2)}, u32[]{:S(2)}) collective-permute-start(bf16[256,384]{1,0:T(8,128)(2,1)S(1)} %collective-permute-done.12.rest_0_), channel_id=1, source_target_pairs={{0,4},{4,0},{8,12},{12,8},{16,20},{20,16},{24,28},{28,24},{1,5},{5... | collective-permute-start | bytes 589832 | tf_op jit(solution)/shard_map/ppermute | solution.py:15
  44.1 0.8 %shard_map.31 = (f32[2,512,256]{2,1,0:T(8,128)S(1)}, f32[2,512,256]{2,1,0:T(8,128)S(1)}) custom-call(bf16[512,384]{1,0:T(8,128)(2,1)S(1)} %get-tuple-element.25.left_ref, f32[2,384]{1,0:T(2,128)S(1)} %get-tuple-element.26.factors_ref, bf16[512,384]{1,0:T(8,128)(2,1)S(1)} %get-tuple-element.23.calls_ref.rest_0_, ...), custom_call_target="tpu_custom_call" | custom-call | flops 201326592 | bytes 524288 | tf_op jit(solution)/shard_map/pallas_call | solution.py:40
  44.9 4.9 %collective-permute-done.13.rest_1_ = bf16[256,384]{1,0:T(8,128)(2,1)S(1)} collective-permute-done((bf16[256,384]{1,0:T(8,128)(2,1)S(1)}, bf16[256,384]{1,0:T(8,128)(2,1)S(1)}, u32[]{:S(2)}, u32[]{:S(2)}) %collective-permute-start.13) | collective-permute-done | bytes 196640 | tf_op jit(solution)/shard_map/ppermute | solution.py:15
  49.8 0.8 %shard_map.32 = (f32[2,512,256]{2,1,0:T(8,128)S(1)}, f32[2,512,256]{2,1,0:T(8,128)S(1)}) custom-call(bf16[512,384]{1,0:T(8,128)(2,1)S(1)} %get-tuple-element.25.left_ref, f32[2,384]{1,0:T(2,128)S(1)} %get-tuple-element.26.factors_ref, bf16[256,384]{1,0:T(8,128)(2,1)S(1)} %collective-permute-done.9.rest_1_.rest_0_, ...), custom_call_target="tpu_custom_call", output_to_operand_aliasing={{0}: (5, {}), {1}: (6, {})} | custom-call | flops 201326592 | bytes 524288 | tf_op jit(solution)/shard_map/pallas_call | solution.py:40
  50.6 0.1 convert_element_type.43
  50.7 0.1 collective-permute-start.14
  50.8 0.0 collective-permute-done.10
  50.8 0.1 convert_add_fusion.2
  50.9 0.0 collective-permute-done.16
  50.9 0.1 convert_add_fusion
  51.0 0.1 fusion.1
  51.1 1.6 %collective-permute-start.17 = (f16[512,256]{1,0:T(8,128)(2,1)S(1)}, f16[512,256]{1,0:T(8,128)(2,1)S(1)}, u32[]{:S(2)}, u32[]{:S(2)}) collective-permute-start(f16[512,256]{1,0:T(8,128)(2,1)S(1)} %get-tuple-element.41), channel_id=1, source_target_pairs={{0,2},{1,3},{2,0},{3,1},{4,6},{5,7},{6,4},{7,5},{8,10},{9,11},{10,... | collective-permute-start | bytes 786440 | tf_op jit(solution)/shard_map/ppermute | solution.py:15
  52.6 0.0 collective-permute-done.14
  52.7 0.1 convert_add_fusion.1
  52.8 0.1 fusion
  52.9 1.6 %collective-permute-start.15 = (f16[512,256]{1,0:T(8,128)(2,1)S(1)}, f16[512,256]{1,0:T(8,128)(2,1)S(1)}, u32[]{:S(2)}, u32[]{:S(2)}) collective-permute-start(f16[512,256]{1,0:T(8,128)(2,1)S(1)} %get-tuple-element.43), channel_id=1, source_target_pairs={{0,2},{1,3},{2,0},{3,1},{4,6},{5,7},{6,4},{7,5},{8,10},{9,11},{10,... | collective-permute-start | bytes 786440 | tf_op jit(solution)/shard_map/ppermute | solution.py:15
  54.5 0.6 collective-permute-start.11
  55.1 13.2 %collective-permute-done.11 = f16[512,128]{1,0:T(8,128)(2,1)S(1)} collective-permute-done((f16[512,128]{1,0:T(8,128)(2,1)S(1)}, f16[512,128]{1,0:T(8,128)(2,1)S(1)}, u32[]{:S(2)}, u32[]{:S(2)}) %collective-permute-start.11) | collective-permute-done | bytes 131104 | tf_op jit(solution)/shard_map/ppermute | solution.py:15
  68.3 0.0 collective-permute-done.17
  68.3 0.9 %shard_map.35.rest_0_ = f32[512,640]{1,0:T(8,128)} custom-call(f32[512,256]{1,0:T(8,128)S(1)} %get-tuple-element.42.ours_ref, f32[512,256]{1,0:T(8,128)S(1)} %convert_element_type.50.got_ref), custom_call_target="tpu_custom_call" | custom-call | flops 131072 | bytes 524288 | tf_op jit(solution)/shard_map/pallas_call | solution.py:40
  69.2 0.0 collective-permute-done.15
  69.3 0.9 %shard_map.36.rest_0_ = f32[512,640]{1,0:T(8,128)} custom-call(f32[512,256]{1,0:T(8,128)S(1)} %get-tuple-element.44.ours_ref, f32[512,256]{1,0:T(8,128)S(1)} %convert_element_type.46.got_ref, f32[512,640]{1,0:T(8,128)} %shard_map.35.rest_0_), custom_call_target="tpu_custom_call", output_to_operand_aliasing={{}: (2, {})} | custom-call | flops 131072 | bytes 524288 | tf_op jit(solution)/shard_map/pallas_call | solution.py:40
  70.1 0.7 %shard_map.37 = f32[512,640]{1,0:T(8,128)} custom-call(f32[512,128]{1,0:T(8,128)S(1)} %get-tuple-element.46.ours_ref, f32[512,128]{1,0:T(8,128)S(1)} %convert_element_type.42.got_ref, f32[512,640]{1,0:T(8,128)} %shard_map.36.rest_0_), custom_call_target="tpu_custom_call", output_to_operand_aliasing={{}: (2, {})} | custom-call | flops 65536 | bytes 262144 | tf_op jit(solution)/shard_map/pallas_call | solution.py:40
  (7 shorter events, 0.2 us)
Async XLA Ops:
  1.5 10.4 %collective-permute-start.3 = (bf16[256,384]{1,0:T(8,128)(2,1)S(1)}, bf16[256,384]{1,0:T(8,128)(2,1)S(1)}, u32[]{:S(2)}, u32[]{:S(2)}) collective-permute-start(bf16[256,384]{1,0:T(8,128)(2,1)S(1)} %get-tuple-element.27), channel_id=1, source_target_pairs={{0,24},{4,28},{8,0},{12,4},{16,8},{20,12},{24,16},{28,20},{1,25},{... | collective-permute-start | bytes 589832 | tf_op jit(solution)/shard_map/ppermute | solution.py:15
  6.6 9.6 %collective-permute-start.8 = (bf16[256,384]{1,0:T(8,128)(2,1)S(1)}, bf16[256,384]{1,0:T(8,128)(2,1)S(1)}, u32[]{:S(2)}, u32[]{:S(2)}) collective-permute-start(bf16[256,384]{1,0:T(8,128)(2,1)S(1)} %get-tuple-element.28), channel_id=1, source_target_pairs={{0,24},{4,28},{8,0},{12,4},{16,8},{20,12},{24,16},{28,20},{1,25},{... | collective-permute-start | bytes 589832 | tf_op jit(solution)/shard_map/ppermute | solution.py:15
  7.1 30.9 %collective-permute-start.7 = (bf16[512,384]{1,0:T(8,128)(2,1)S(1)}, bf16[512,384]{1,0:T(8,128)(2,1)S(1)}, u32[]{:S(2)}, u32[]{:S(2)}) collective-permute-start(bf16[512,384]{1,0:T(8,128)(2,1)S(1)} %get-tuple-element.23.calls_ref.rest_0_), channel_id=1, source_target_pairs={{4,0},{12,8},{20,16},{28,24},{5,1},{13,9},{21,17},{29,25},{6,2},{1... | collective-permute-start | bytes 1179656 | tf_op jit(solution)/shard_map/ppermute | solution.py:15
  11.9 23.5 %collective-permute-start.5 = (bf16[256,384]{1,0:T(8,128)(2,1)S(1)}, bf16[256,384]{1,0:T(8,128)(2,1)S(1)}, u32[]{:S(2)}, u32[]{:S(2)}) collective-permute-start(bf16[256,384]{1,0:T(8,128)(2,1)S(1)} %collective-permute-done.3.rest_2_), channel_id=1, source_target_pairs={{0,24},{4,28},{8,0},{12,4},{16,8},{20,12},{24,16},{28,20},{1,25},{... | collective-permute-start | bytes 589832 | tf_op jit(solution)/shard_map/ppermute | solution.py:15
  16.2 21.1 %collective-permute-start.12 = (bf16[256,384]{1,0:T(8,128)(2,1)S(1)}, bf16[256,384]{1,0:T(8,128)(2,1)S(1)}, u32[]{:S(2)}, u32[]{:S(2)}) collective-permute-start(bf16[256,384]{1,0:T(8,128)(2,1)S(1)} %collective-permute-done.8.rest_1_), channel_id=1, source_target_pairs={{0,24},{4,28},{8,0},{12,4},{16,8},{20,12},{24,16},{28,20},{1,25},{... | collective-permute-start | bytes 589832 | tf_op jit(solution)/shard_map/ppermute | solution.py:15
  20.1 17.8 %collective-permute-start.9 = (bf16[256,384]{1,0:T(8,128)(2,1)S(1)}, bf16[256,384]{1,0:T(8,128)(2,1)S(1)}, u32[]{:S(2)}, u32[]{:S(2)}) collective-permute-start(bf16[256,384]{1,0:T(8,128)(2,1)S(1)} %collective-permute-done.8.rest_1_), channel_id=1, source_target_pairs={{0,4},{4,0},{8,12},{12,8},{16,20},{20,16},{24,28},{28,24},{1,5},{5... | collective-permute-start | bytes 589832 | tf_op jit(solution)/shard_map/ppermute | solution.py:15
  21.6 4.2 %collective-permute-start = (f32[2,384]{1,0:T(2,128)S(1)}, f32[2,384]{1,0:T(2,128)S(1)}, u32[]{:S(2)}, u32[]{:S(2)}) collective-permute-start(f32[2,384]{1,0:T(2,128)S(1)} %get-tuple-element.24), channel_id=1, source_target_pairs={{0,4},{4,0},{8,12},{12,8},{16,20},{20,16},{24,28},{28,24},{1,5},{5... | collective-permute-start | bytes 9224 | tf_op jit(solution)/shard_map/ppermute | solution.py:15
  25.8 3.6 %collective-permute-start.1 = (f32[2,384]{1,0:T(2,128)S(1)}, f32[2,384]{1,0:T(2,128)S(1)}, u32[]{:S(2)}, u32[]{:S(2)}) collective-permute-start(f32[2,384]{1,0:T(2,128)S(1)} %add.15), channel_id=1, source_target_pairs={{0,8},{4,12},{8,0},{12,4},{16,24},{20,28},{24,16},{28,20},{1,9},{5... | collective-permute-start | bytes 9224 | tf_op jit(solution)/shard_map/ppermute | solution.py:15
  29.4 4.5 %collective-permute-start.2 = (f32[2,384]{1,0:T(2,128)S(1)}, f32[2,384]{1,0:T(2,128)S(1)}, u32[]{:S(2)}, u32[]{:S(2)}) collective-permute-start(f32[2,384]{1,0:T(2,128)S(1)} %add.16.sums_ref), channel_id=1, source_target_pairs={{0,16},{4,20},{8,24},{12,28},{16,0},{20,4},{24,8},{28,12},{1,17},{... | collective-permute-start | bytes 9224 | tf_op jit(solution)/shard_map/ppermute | solution.py:15
  33.9 5.7 %collective-permute-start.4 = (bf16[256,384]{1,0:T(8,128)(2,1)S(1)}, bf16[256,384]{1,0:T(8,128)(2,1)S(1)}, u32[]{:S(2)}, u32[]{:S(2)}) collective-permute-start(bf16[256,384]{1,0:T(8,128)(2,1)S(1)} %collective-permute-done.3.rest_2_), channel_id=1, source_target_pairs={{0,4},{4,0},{8,12},{12,8},{16,20},{20,16},{24,28},{28,24},{1,5},{5... | collective-permute-start | bytes 589832 | tf_op jit(solution)/shard_map/ppermute | solution.py:15
  35.5 6.3 %collective-permute-start.6 = (bf16[256,384]{1,0:T(8,128)(2,1)S(1)}, bf16[256,384]{1,0:T(8,128)(2,1)S(1)}, u32[]{:S(2)}, u32[]{:S(2)}) collective-permute-start(bf16[256,384]{1,0:T(8,128)(2,1)S(1)} %collective-permute-done.5.rest_2_), channel_id=1, source_target_pairs={{0,4},{4,0},{8,12},{12,8},{16,20},{20,16},{24,28},{28,24},{1,5},{5... | collective-permute-start | bytes 589832 | tf_op jit(solution)/shard_map/ppermute | solution.py:15
  37.9 13.0 %collective-permute-start.16 = (f16[2,512,256]{2,1,0:T(8,128)(2,1)S(1)}, f16[2,512,256]{2,1,0:T(8,128)(2,1)S(1)}, u32[]{:S(2)}, u32[]{:S(2)}) collective-permute-start(f16[2,512,256]{2,1,0:T(8,128)(2,1)S(1)} %convert_element_type.47), channel_id=1, source_target_pairs={{0,1},{1,0},{2,3},{3,2},{4,5},{5,4},{6,7},{7,6},{8,9},{9,8},{10,11... | collective-permute-start | bytes 1572872 | tf_op jit(solution)/shard_map/ppermute | solution.py:15
  42.4 8.4 %collective-permute-start.10 = (f16[2,512,128]{2,1,0:T(8,128)(2,1)S(1)}, f16[2,512,128]{2,1,0:T(8,128)(2,1)S(1)}, u32[]{:S(2)}, u32[]{:S(2)}) collective-permute-start(f16[2,512,128]{2,1,0:T(8,128)(2,1)S(1)} %convert_element_type.39), channel_id=1, source_target_pairs={{0,1},{1,0},{2,3},{3,2},{4,5},{5,4},{6,7},{7,6},{8,9},{9,8},{10,11... | collective-permute-start | bytes 786440 | tf_op jit(solution)/shard_map/ppermute | solution.py:15
  42.5 7.3 %collective-permute-start.13 = (bf16[256,384]{1,0:T(8,128)(2,1)S(1)}, bf16[256,384]{1,0:T(8,128)(2,1)S(1)}, u32[]{:S(2)}, u32[]{:S(2)}) collective-permute-start(bf16[256,384]{1,0:T(8,128)(2,1)S(1)} %collective-permute-done.12.rest_0_), channel_id=1, source_target_pairs={{0,4},{4,0},{8,12},{12,8},{16,20},{20,16},{24,28},{28,24},{1,5},{5... | collective-permute-start | bytes 589832 | tf_op jit(solution)/shard_map/ppermute | solution.py:15
  50.7 2.0 %collective-permute-start.14 = (f16[2,512,256]{2,1,0:T(8,128)(2,1)S(1)}, f16[2,512,256]{2,1,0:T(8,128)(2,1)S(1)}, u32[]{:S(2)}, u32[]{:S(2)}) collective-permute-start(f16[2,512,256]{2,1,0:T(8,128)(2,1)S(1)} %convert_element_type.43), channel_id=1, source_target_pairs={{0,1},{1,0},{2,3},{3,2},{4,5},{5,4},{6,7},{7,6},{8,9},{9,8},{10,11... | collective-permute-start | bytes 1572872 | tf_op jit(solution)/shard_map/ppermute | solution.py:15
  51.1 17.2 %collective-permute-start.17 = (f16[512,256]{1,0:T(8,128)(2,1)S(1)}, f16[512,256]{1,0:T(8,128)(2,1)S(1)}, u32[]{:S(2)}, u32[]{:S(2)}) collective-permute-start(f16[512,256]{1,0:T(8,128)(2,1)S(1)} %get-tuple-element.41), channel_id=1, source_target_pairs={{0,2},{1,3},{2,0},{3,1},{4,6},{5,7},{6,4},{7,5},{8,10},{9,11},{10,... | collective-permute-start | bytes 786440 | tf_op jit(solution)/shard_map/ppermute | solution.py:15
  52.9 16.3 %collective-permute-start.15 = (f16[512,256]{1,0:T(8,128)(2,1)S(1)}, f16[512,256]{1,0:T(8,128)(2,1)S(1)}, u32[]{:S(2)}, u32[]{:S(2)}) collective-permute-start(f16[512,256]{1,0:T(8,128)(2,1)S(1)} %get-tuple-element.43), channel_id=1, source_target_pairs={{0,2},{1,3},{2,0},{3,1},{4,6},{5,7},{6,4},{7,5},{8,10},{9,11},{10,... | collective-permute-start | bytes 786440 | tf_op jit(solution)/shard_map/ppermute | solution.py:15
  54.5 13.8 %collective-permute-start.11 = (f16[512,128]{1,0:T(8,128)(2,1)S(1)}, f16[512,128]{1,0:T(8,128)(2,1)S(1)}, u32[]{:S(2)}, u32[]{:S(2)}) collective-permute-start(f16[512,128]{1,0:T(8,128)(2,1)S(1)} %get-tuple-element.45), channel_id=1, source_target_pairs={{0,2},{1,3},{2,0},{3,1},{4,6},{5,7},{6,4},{7,5},{8,10},{9,11},{10,... | collective-permute-start | bytes 393224 | tf_op jit(solution)/shard_map/ppermute | solution.py:15

commit v4 on v3

--- a/solution.py
+++ b/solution.py
@@ -178,11 +178,12 @@
     calls, first, second, sums = encode(genotype, mask)
 
     along = lambda s: (s - 2) % samples
+    even = lax.axis_index("samples") % 2 == 0
     line = [[first, second]]
     for _ in range(1, turns + 1):
         line.append([send(line[-1][h], "samples", along) for h in range(2)])
-    beside = send(calls, "samples", lambda s: s - 1 if s % 2 else None)
-    side = [None] + [[send(line[t][h], "samples", lambda s: s ^ 1) for h in range(2)] for t in range(1, turns + 1)]
+    side = [None] + [[send(line[t][h], "samples", lambda s: s ^ 1) for h in range(2)] for t in range(1, turns)]
+    side.append([send(jnp.where(even, line[turns][h], line[0][1 - h]), "samples", lambda s: s ^ 1) for h in range(2)])
 
     for bit in range(samples.bit_length() - 1):
         more = send(sums, "samples", lambda s, step=1 << bit: s ^ step)
@@ -195,7 +196,7 @@
         if k % 2 == 0:
             return line[k // 2][h], 0
         if k == 1 and not odd:
-            return beside, h * half_rows
+            return side[turns][1 - h], 0
         return side[(k + odd) // 2][h], 0
 
     left, pair = call_kernel(
@@ -237,9 +238,10 @@
 
     pieces = []
     for n in range(count + 1):
+        last_in = (1, 2 * turns - 1) + ((2 * turns,) if n == 0 else ())
         late = [
             strip for strip, (by_arrival, _, cut) in enumerate(table)
-            if (by_arrival[n] if n < count else cut)[0] >= 2 * turns - 1
+            if (by_arrival[n] if n < count else cut)[0] in last_in
         ]
         both = ()
         for chosen in ([s for s in range(4) if s not in late], late):

time: 71 us -> 69.3 us (0.976)
  starting transfers between devices: 24.6 us -> 23.4 us
    ppermute x18 -> x17, starting transfers between devices: 24.6 us -> 23.4 us  [send(): lax.ppermute(value, axis, [pair for pair in pairs if pair[1] is not None])]
    ppermute x18 -> x17, waiting for transfers between devices: 36.5 us -> 36 us  [send(): lax.ppermute(value, axis, [pair for pair in pairs if pair[1] is not None])]
    pallas_call x10 -> x9, Pallas kernels: 7.17 us -> 7.17 us  [call_kernel(): pl.pallas_call(body, out_shape=shapes, in_specs=specs, compiler_params=pl...]
  transfers between devices with their start and end apart: 18 -> 17, of which waited for: 8 -> 7; matrix products, arithmetic and copies ran while one was open for 1% -> 1% of each run, Pallas kernels for 8% -> 8%
where the time goes in v4:
time: 69.3 us; the launch traced here: 69.1 us
  waiting for transfers between devices  36 us (52%)
  starting transfers between devices  23.4 us (34%)
  Pallas kernels  8.66 us (12%)
  other arithmetic  0.84 us (1%)
    ppermute x17, waiting for transfers between devices, send(): lax.ppermute(value, axis, [pair for pair in pairs if pair[1] is not None])  36 us
    ppermute x17, starting transfers between devices, send(): lax.ppermute(value, axis, [pair for pair in pairs if pair[1] is not None])  23.4 us
    pallas_call x9, Pallas kernels, call_kernel(): pl.pallas_call(body, out_shape=shapes, in_specs=specs, compiler_params=pl...  7.17 us
    pallas_call x1, Pallas kernels, encode(): pl.pallas_call(encode_body, name='encode', out_shape=(calls(rows), calls(...  1.49 us
  transfers between devices with their start and end apart: 17, of which 7 were waited for; matrix products, arithmetic and copies ran while one was open for 1% of the time, Pallas kernels for 8%

profile of v4, /device:TPU:0, one launch (start us, length us, event | category | flops | bytes accessed | tf_op | source)
XLA Modules:
  0.0 69.1 jit_solution(9437940773549149972)
XLA Ops:
  0.0 1.5 %encode.1 = (bf16[512,384]{1,0:T(8,128)(2,1)S(1)}, bf16[256,384]{1,0:T(8,128)(2,1)S(1)}, bf16[256,384]{1,0:T(8,128)(2,1)S(1)}, f32[2,384]{1,0:T(2,128)S(1)}) custom-call(s32[512,384]{1,0:T(8,128)} %genotype_ref.1, s32[512,384]{1,0:T(8,128)} %mask_ref.1), custom_call_target="tpu_custom_call" | custom-call | tf_op jit(solution)/shard_map/encode/pallas_call | solution.py:87
  1.5 5.1 %collective-permute-start.3 = (bf16[256,384]{1,0:T(8,128)(2,1)S(1)}, bf16[256,384]{1,0:T(8,128)(2,1)S(1)}, u32[]{:S(2)}, u32[]{:S(2)}) collective-permute-start(bf16[256,384]{1,0:T(8,128)(2,1)S(1)} %get-tuple-element.25), channel_id=1, source_target_pairs={{0,24},{4,28},{8,0},{12,4},{16,8},{20,12},{24,16},{28,20},{1,25},{... | collective-permute-start | bytes 589832 | tf_op jit(solution)/shard_map/ppermute | solution.py:15
  6.6 0.4 collective-permute-start.6
  7.1 4.8 %collective-permute-done.3.rest_2_ = bf16[256,384]{1,0:T(8,128)(2,1)S(1)} collective-permute-done((bf16[256,384]{1,0:T(8,128)(2,1)S(1)}, bf16[256,384]{1,0:T(8,128)(2,1)S(1)}, u32[]{:S(2)}, u32[]{:S(2)}) %collective-permute-start.3) | collective-permute-done | bytes 196640 | tf_op jit(solution)/shard_map/ppermute | solution.py:15
  11.9 4.3 %collective-permute-start.4 = (bf16[256,384]{1,0:T(8,128)(2,1)S(1)}, bf16[256,384]{1,0:T(8,128)(2,1)S(1)}, u32[]{:S(2)}, u32[]{:S(2)}) collective-permute-start(bf16[256,384]{1,0:T(8,128)(2,1)S(1)} %collective-permute-done.3.rest_2_), channel_id=1, source_target_pairs={{0,24},{4,28},{8,0},{12,4},{16,8},{20,12},{24,16},{28,20},{1,25},{... | collective-permute-start | bytes 589832 | tf_op jit(solution)/shard_map/ppermute | solution.py:15
  16.2 1.5 %collective-permute-start.8 = (bf16[256,384]{1,0:T(8,128)(2,1)S(1)}, bf16[256,384]{1,0:T(8,128)(2,1)S(1)}, u32[]{:S(2)}, u32[]{:S(2)}) collective-permute-start(bf16[256,384]{1,0:T(8,128)(2,1)S(1)} %collective-permute-done.3.rest_2_), channel_id=1, source_target_pairs={{0,4},{4,0},{8,12},{12,8},{16,20},{20,16},{24,28},{28,24},{1,5},{5... | collective-permute-start | bytes 589832 | tf_op jit(solution)/shard_map/ppermute | solution.py:15
  17.7 0.0 collective-permute-done.6.rest_1_
  17.7 0.5 collective-permute-start.7
  18.2 3.4 %collective-permute-start.11 = (bf16[256,384]{1,0:T(8,128)(2,1)S(1)}, bf16[256,384]{1,0:T(8,128)(2,1)S(1)}, u32[]{:S(2)}, u32[]{:S(2)}) collective-permute-start(bf16[256,384]{1,0:T(8,128)(2,1)S(1)} %collective-permute-done.6.rest_1_), channel_id=1, source_target_pairs={{0,24},{4,28},{8,0},{12,4},{16,8},{20,12},{24,16},{28,20},{1,25},{... | collective-permute-start | bytes 589832 | tf_op jit(solution)/shard_map/ppermute | solution.py:15
  21.6 0.0 collective-permute-done.4.rest_1_
  21.7 0.6 collective-permute-start.5
  22.2 1.5 %collective-permute-start = (f32[2,384]{1,0:T(2,128)S(1)}, f32[2,384]{1,0:T(2,128)S(1)}, u32[]{:S(2)}, u32[]{:S(2)}) collective-permute-start(f32[2,384]{1,0:T(2,128)S(1)} %get-tuple-element.22), channel_id=1, source_target_pairs={{0,4},{4,0},{8,12},{12,8},{16,20},{20,16},{24,28},{28,24},{1,5},{5... | collective-permute-start | bytes 9224 | tf_op jit(solution)/shard_map/ppermute | solution.py:15
  23.8 5.3 %collective-permute-done = f32[2,384]{1,0:T(2,128)S(1)} collective-permute-done((f32[2,384]{1,0:T(2,128)S(1)}, f32[2,384]{1,0:T(2,128)S(1)}, u32[]{:S(2)}, u32[]{:S(2)}) %collective-permute-start) | collective-permute-done | bytes 3104 | tf_op jit(solution)/shard_map/ppermute | solution.py:15
  29.1 0.0 collective-permute-start.1
  29.1 3.6 %collective-permute-done.1 = f32[2,384]{1,0:T(2,128)S(1)} collective-permute-done((f32[2,384]{1,0:T(2,128)S(1)}, f32[2,384]{1,0:T(2,128)S(1)}, u32[]{:S(2)}, u32[]{:S(2)}) %collective-permute-start.1) | collective-permute-done | bytes 3104 | tf_op jit(solution)/shard_map/ppermute | solution.py:15
  32.7 0.0 collective-permute-start.2
  32.7 4.5 %collective-permute-done.2.more_ref = f32[2,384]{1,0:T(2,128)S(1)} collective-permute-done((f32[2,384]{1,0:T(2,128)S(1)}, f32[2,384]{1,0:T(2,128)S(1)}, u32[]{:S(2)}, u32[]{:S(2)}) %collective-permute-start.2) | collective-permute-done | bytes 3104 | tf_op jit(solution)/shard_map/ppermute | solution.py:15
  37.2 0.2 shard_map.28
  37.4 1.2 %shard_map.32 = (f32[2,512,256]{2,1,0:T(8,128)S(1)}, f32[2,512,256]{2,1,0:T(8,128)S(1)}) custom-call(bf16[512,384]{1,0:T(8,128)(2,1)S(1)} %get-tuple-element.23.left_ref, f32[2,384]{1,0:T(2,128)S(1)} %get-tuple-element.24.factors_ref, bf16[512,384]{1,0:T(8,128)(2,1)S(1)} %get-tuple-element.21.calls_ref.rest_0_, ...), custom_call_target="tpu_custom_call" | custom-call | flops 301989888 | bytes 524288 | tf_op jit(solution)/shard_map/pallas_call | solution.py:40
  38.6 0.0 collective-permute-done.11.rest_0_
  38.6 0.4 shard_map.33
  39.0 0.1 convert_element_type.47
  39.1 0.1 collective-permute-start.15
  39.2 0.0 collective-permute-done.7.rest_1_.rest_2_
  39.2 0.0 collective-permute-done.8.rest_2_.rest_1_
  39.2 0.0 collective-permute-done.5.rest_0_
  39.2 1.3 %shard_map.29 = (f32[2,512,128]{2,1,0:T(8,128)S(1)}, f32[2,512,128]{2,1,0:T(8,128)S(1)}) custom-call(bf16[512,384]{1,0:T(8,128)(2,1)S(1)} %get-tuple-element.23.left_ref, f32[2,384]{1,0:T(2,128)S(1)} %get-tuple-element.24.factors_ref, bf16[256,384]{1,0:T(8,128)(2,1)S(1)} %collective-permute-done.5.rest_0_, ...), custom_call_target="tpu_custom_call" | custom-call | flops 201326592 | bytes 262144 | tf_op jit(solution)/shard_map/pallas_call | solution.py:40
  40.5 0.5 collective-permute-start.9
  41.1 1.6 %collective-permute-start.12 = (bf16[256,384]{1,0:T(8,128)(2,1)S(1)}, bf16[256,384]{1,0:T(8,128)(2,1)S(1)}, u32[]{:S(2)}, u32[]{:S(2)}) collective-permute-start(bf16[256,384]{1,0:T(8,128)(2,1)S(1)} %broadcast_select_fusion), channel_id=1, source_target_pairs={{0,4},{4,0},{8,12},{12,8},{16,20},{20,16},{24,28},{28,24},{1,5},{5... | collective-permute-start | bytes 589832 | tf_op jit(solution)/shard_map/ppermute | solution.py:15
  42.7 0.8 %shard_map.30 = (f32[2,512,256]{2,1,0:T(8,128)S(1)}, f32[2,512,256]{2,1,0:T(8,128)S(1)}) custom-call(bf16[512,384]{1,0:T(8,128)(2,1)S(1)} %get-tuple-element.23.left_ref, f32[2,384]{1,0:T(2,128)S(1)} %get-tuple-element.24.factors_ref, bf16[512,384]{1,0:T(8,128)(2,1)S(1)} %get-tuple-element.21.calls_ref.rest_0_, ...), custom_call_target="tpu_custom_call" | custom-call | flops 201326592 | bytes 524288 | tf_op jit(solution)/shard_map/pallas_call | solution.py:40
  43.5 4.5 %collective-permute-done.12.rest_0_ = bf16[256,384]{1,0:T(8,128)(2,1)S(1)} collective-permute-done((bf16[256,384]{1,0:T(8,128)(2,1)S(1)}, bf16[256,384]{1,0:T(8,128)(2,1)S(1)}, u32[]{:S(2)}, u32[]{:S(2)}) %collective-permute-start.12) | collective-permute-done | bytes 196640 | tf_op jit(solution)/shard_map/ppermute | solution.py:15
  48.0 0.8 %shard_map.31 = (f32[2,512,256]{2,1,0:T(8,128)S(1)}, f32[2,512,256]{2,1,0:T(8,128)S(1)}) custom-call(bf16[512,384]{1,0:T(8,128)(2,1)S(1)} %get-tuple-element.23.left_ref, f32[2,384]{1,0:T(2,128)S(1)} %get-tuple-element.24.factors_ref, bf16[256,384]{1,0:T(8,128)(2,1)S(1)} %collective-permute-done.12.rest_0_, ...), custom_call_target="tpu_custom_call", output_to_operand_aliasing={{0}: (5, {}), {1}: (6, {})} | custom-call | flops 201326592 | bytes 524288 | tf_op jit(solution)/shard_map/pallas_call | solution.py:40
  48.8 0.1 convert_element_type.43
  48.9 0.1 collective-permute-start.13
  49.0 0.0 collective-permute-done.9
  49.0 0.1 convert_add_fusion.2
  49.1 0.0 collective-permute-done.15
  49.1 0.1 convert_add_fusion
  49.2 0.1 fusion.1
  49.3 1.6 %collective-permute-start.16 = (f16[512,256]{1,0:T(8,128)(2,1)S(1)}, f16[512,256]{1,0:T(8,128)(2,1)S(1)}, u32[]{:S(2)}, u32[]{:S(2)}) collective-permute-start(f16[512,256]{1,0:T(8,128)(2,1)S(1)} %get-tuple-element.37), channel_id=1, source_target_pairs={{0,2},{1,3},{2,0},{3,1},{4,6},{5,7},{6,4},{7,5},{8,10},{9,11},{10,... | collective-permute-start | bytes 786440 | tf_op jit(solution)/shard_map/ppermute | solution.py:15
  50.9 0.1 collective-permute-done.13
  50.9 0.1 convert_add_fusion.1
  51.0 0.1 fusion
  51.1 1.6 %collective-permute-start.14 = (f16[512,256]{1,0:T(8,128)(2,1)S(1)}, f16[512,256]{1,0:T(8,128)(2,1)S(1)}, u32[]{:S(2)}, u32[]{:S(2)}) collective-permute-start(f16[512,256]{1,0:T(8,128)(2,1)S(1)} %get-tuple-element.39), channel_id=1, source_target_pairs={{0,2},{1,3},{2,0},{3,1},{4,6},{5,7},{6,4},{7,5},{8,10},{9,11},{10,... | collective-permute-start | bytes 786440 | tf_op jit(solution)/shard_map/ppermute | solution.py:15
  52.7 0.6 collective-permute-start.10
  53.3 13.2 %collective-permute-done.10 = f16[512,128]{1,0:T(8,128)(2,1)S(1)} collective-permute-done((f16[512,128]{1,0:T(8,128)(2,1)S(1)}, f16[512,128]{1,0:T(8,128)(2,1)S(1)}, u32[]{:S(2)}, u32[]{:S(2)}) %collective-permute-start.10) | collective-permute-done | bytes 131104 | tf_op jit(solution)/shard_map/ppermute | solution.py:15
  66.5 0.0 collective-permute-done.16
  66.6 0.9 %shard_map.34.rest_0_ = f32[512,640]{1,0:T(8,128)} custom-call(f32[512,256]{1,0:T(8,128)S(1)} %get-tuple-element.38.ours_ref, f32[512,256]{1,0:T(8,128)S(1)} %convert_element_type.50.got_ref), custom_call_target="tpu_custom_call" | custom-call | flops 131072 | bytes 524288 | tf_op jit(solution)/shard_map/pallas_call | solution.py:40
  67.4 0.0 collective-permute-done.14
  67.5 0.9 %shard_map.35.rest_0_ = f32[512,640]{1,0:T(8,128)} custom-call(f32[512,256]{1,0:T(8,128)S(1)} %get-tuple-element.40.ours_ref, f32[512,256]{1,0:T(8,128)S(1)} %convert_element_type.46.got_ref, f32[512,640]{1,0:T(8,128)} %shard_map.34.rest_0_), custom_call_target="tpu_custom_call", output_to_operand_aliasing={{}: (2, {})} | custom-call | flops 131072 | bytes 524288 | tf_op jit(solution)/shard_map/pallas_call | solution.py:40
  68.4 0.7 %shard_map.36 = f32[512,640]{1,0:T(8,128)} custom-call(f32[512,128]{1,0:T(8,128)S(1)} %get-tuple-element.42.ours_ref, f32[512,128]{1,0:T(8,128)S(1)} %convert_element_type.42.got_ref, f32[512,640]{1,0:T(8,128)} %shard_map.35.rest_0_), custom_call_target="tpu_custom_call", output_to_operand_aliasing={{}: (2, {})} | custom-call | flops 65536 | bytes 262144 | tf_op jit(solution)/shard_map/pallas_call | solution.py:40
  (9 shorter events, 0.2 us)
Async XLA Ops:
  1.5 10.4 %collective-permute-start.3 = (bf16[256,384]{1,0:T(8,128)(2,1)S(1)}, bf16[256,384]{1,0:T(8,128)(2,1)S(1)}, u32[]{:S(2)}, u32[]{:S(2)}) collective-permute-start(bf16[256,384]{1,0:T(8,128)(2,1)S(1)} %get-tuple-element.25), channel_id=1, source_target_pairs={{0,24},{4,28},{8,0},{12,4},{16,8},{20,12},{24,16},{28,20},{1,25},{... | collective-permute-start | bytes 589832 | tf_op jit(solution)/shard_map/ppermute | solution.py:15
  6.6 11.1 %collective-permute-start.6 = (bf16[256,384]{1,0:T(8,128)(2,1)S(1)}, bf16[256,384]{1,0:T(8,128)(2,1)S(1)}, u32[]{:S(2)}, u32[]{:S(2)}) collective-permute-start(bf16[256,384]{1,0:T(8,128)(2,1)S(1)} %get-tuple-element.26), channel_id=1, source_target_pairs={{0,24},{4,28},{8,0},{12,4},{16,8},{20,12},{24,16},{28,20},{1,25},{... | collective-permute-start | bytes 589832 | tf_op jit(solution)/shard_map/ppermute | solution.py:15
  11.9 9.7 %collective-permute-start.4 = (bf16[256,384]{1,0:T(8,128)(2,1)S(1)}, bf16[256,384]{1,0:T(8,128)(2,1)S(1)}, u32[]{:S(2)}, u32[]{:S(2)}) collective-permute-start(bf16[256,384]{1,0:T(8,128)(2,1)S(1)} %collective-permute-done.3.rest_2_), channel_id=1, source_target_pairs={{0,24},{4,28},{8,0},{12,4},{16,8},{20,12},{24,16},{28,20},{1,25},{... | collective-permute-start | bytes 589832 | tf_op jit(solution)/shard_map/ppermute | solution.py:15
  16.2 23.0 %collective-permute-start.8 = (bf16[256,384]{1,0:T(8,128)(2,1)S(1)}, bf16[256,384]{1,0:T(8,128)(2,1)S(1)}, u32[]{:S(2)}, u32[]{:S(2)}) collective-permute-start(bf16[256,384]{1,0:T(8,128)(2,1)S(1)} %collective-permute-done.3.rest_2_), channel_id=1, source_target_pairs={{0,4},{4,0},{8,12},{12,8},{16,20},{20,16},{24,28},{28,24},{1,5},{5... | collective-permute-start | bytes 589832 | tf_op jit(solution)/shard_map/ppermute | solution.py:15
  17.7 21.4 %collective-permute-start.7 = (bf16[256,384]{1,0:T(8,128)(2,1)S(1)}, bf16[256,384]{1,0:T(8,128)(2,1)S(1)}, u32[]{:S(2)}, u32[]{:S(2)}) collective-permute-start(bf16[256,384]{1,0:T(8,128)(2,1)S(1)} %collective-permute-done.6.rest_1_), channel_id=1, source_target_pairs={{0,4},{4,0},{8,12},{12,8},{16,20},{20,16},{24,28},{28,24},{1,5},{5... | collective-permute-start | bytes 589832 | tf_op jit(solution)/shard_map/ppermute | solution.py:15
  18.2 20.3 %collective-permute-start.11 = (bf16[256,384]{1,0:T(8,128)(2,1)S(1)}, bf16[256,384]{1,0:T(8,128)(2,1)S(1)}, u32[]{:S(2)}, u32[]{:S(2)}) collective-permute-start(bf16[256,384]{1,0:T(8,128)(2,1)S(1)} %collective-permute-done.6.rest_1_), channel_id=1, source_target_pairs={{0,24},{4,28},{8,0},{12,4},{16,8},{20,12},{24,16},{28,20},{1,25},{... | collective-permute-start | bytes 589832 | tf_op jit(solution)/shard_map/ppermute | solution.py:15
  21.7 17.5 %collective-permute-start.5 = (bf16[256,384]{1,0:T(8,128)(2,1)S(1)}, bf16[256,384]{1,0:T(8,128)(2,1)S(1)}, u32[]{:S(2)}, u32[]{:S(2)}) collective-permute-start(bf16[256,384]{1,0:T(8,128)(2,1)S(1)} %broadcast_select_fusion.1), channel_id=1, source_target_pairs={{0,4},{4,0},{8,12},{12,8},{16,20},{20,16},{24,28},{28,24},{1,5},{5... | collective-permute-start | bytes 589832 | tf_op jit(solution)/shard_map/ppermute | solution.py:15
  22.2 6.8 %collective-permute-start = (f32[2,384]{1,0:T(2,128)S(1)}, f32[2,384]{1,0:T(2,128)S(1)}, u32[]{:S(2)}, u32[]{:S(2)}) collective-permute-start(f32[2,384]{1,0:T(2,128)S(1)} %get-tuple-element.22), channel_id=1, source_target_pairs={{0,4},{4,0},{8,12},{12,8},{16,20},{20,16},{24,28},{28,24},{1,5},{5... | collective-permute-start | bytes 9224 | tf_op jit(solution)/shard_map/ppermute | solution.py:15
  29.1 3.6 %collective-permute-start.1 = (f32[2,384]{1,0:T(2,128)S(1)}, f32[2,384]{1,0:T(2,128)S(1)}, u32[]{:S(2)}, u32[]{:S(2)}) collective-permute-start(f32[2,384]{1,0:T(2,128)S(1)} %add.19), channel_id=1, source_target_pairs={{0,8},{4,12},{8,0},{12,4},{16,24},{20,28},{24,16},{28,20},{1,9},{5... | collective-permute-start | bytes 9224 | tf_op jit(solution)/shard_map/ppermute | solution.py:15
  32.7 4.5 %collective-permute-start.2 = (f32[2,384]{1,0:T(2,128)S(1)}, f32[2,384]{1,0:T(2,128)S(1)}, u32[]{:S(2)}, u32[]{:S(2)}) collective-permute-start(f32[2,384]{1,0:T(2,128)S(1)} %add.20.sums_ref), channel_id=1, source_target_pairs={{0,16},{4,20},{8,24},{12,28},{16,0},{20,4},{24,8},{28,12},{1,17},{... | collective-permute-start | bytes 9224 | tf_op jit(solution)/shard_map/ppermute | solution.py:15
  39.1 10.0 %collective-permute-start.15 = (f16[2,512,256]{2,1,0:T(8,128)(2,1)S(1)}, f16[2,512,256]{2,1,0:T(8,128)(2,1)S(1)}, u32[]{:S(2)}, u32[]{:S(2)}) collective-permute-start(f16[2,512,256]{2,1,0:T(8,128)(2,1)S(1)} %convert_element_type.47), channel_id=1, source_target_pairs={{0,1},{1,0},{2,3},{3,2},{4,5},{5,4},{6,7},{7,6},{8,9},{9,8},{10,11... | collective-permute-start | bytes 1572872 | tf_op jit(solution)/shard_map/ppermute | solution.py:15
  40.5 8.5 %collective-permute-start.9 = (f16[2,512,128]{2,1,0:T(8,128)(2,1)S(1)}, f16[2,512,128]{2,1,0:T(8,128)(2,1)S(1)}, u32[]{:S(2)}, u32[]{:S(2)}) collective-permute-start(f16[2,512,128]{2,1,0:T(8,128)(2,1)S(1)} %convert_element_type.39), channel_id=1, source_target_pairs={{0,1},{1,0},{2,3},{3,2},{4,5},{5,4},{6,7},{7,6},{8,9},{9,8},{10,11... | collective-permute-start | bytes 786440 | tf_op jit(solution)/shard_map/ppermute | solution.py:15
  41.1 6.9 %collective-permute-start.12 = (bf16[256,384]{1,0:T(8,128)(2,1)S(1)}, bf16[256,384]{1,0:T(8,128)(2,1)S(1)}, u32[]{:S(2)}, u32[]{:S(2)}) collective-permute-start(bf16[256,384]{1,0:T(8,128)(2,1)S(1)} %broadcast_select_fusion), channel_id=1, source_target_pairs={{0,4},{4,0},{8,12},{12,8},{16,20},{20,16},{24,28},{28,24},{1,5},{5... | collective-permute-start | bytes 589832 | tf_op jit(solution)/shard_map/ppermute | solution.py:15
  48.9 2.0 %collective-permute-start.13 = (f16[2,512,256]{2,1,0:T(8,128)(2,1)S(1)}, f16[2,512,256]{2,1,0:T(8,128)(2,1)S(1)}, u32[]{:S(2)}, u32[]{:S(2)}) collective-permute-start(f16[2,512,256]{2,1,0:T(8,128)(2,1)S(1)} %convert_element_type.43), channel_id=1, source_target_pairs={{0,1},{1,0},{2,3},{3,2},{4,5},{5,4},{6,7},{7,6},{8,9},{9,8},{10,11... | collective-permute-start | bytes 1572872 | tf_op jit(solution)/shard_map/ppermute | solution.py:15
  49.3 17.2 %collective-permute-start.16 = (f16[512,256]{1,0:T(8,128)(2,1)S(1)}, f16[512,256]{1,0:T(8,128)(2,1)S(1)}, u32[]{:S(2)}, u32[]{:S(2)}) collective-permute-start(f16[512,256]{1,0:T(8,128)(2,1)S(1)} %get-tuple-element.37), channel_id=1, source_target_pairs={{0,2},{1,3},{2,0},{3,1},{4,6},{5,7},{6,4},{7,5},{8,10},{9,11},{10,... | collective-permute-start | bytes 786440 | tf_op jit(solution)/shard_map/ppermute | solution.py:15
  51.1 16.3 %collective-permute-start.14 = (f16[512,256]{1,0:T(8,128)(2,1)S(1)}, f16[512,256]{1,0:T(8,128)(2,1)S(1)}, u32[]{:S(2)}, u32[]{:S(2)}) collective-permute-start(f16[512,256]{1,0:T(8,128)(2,1)S(1)} %get-tuple-element.39), channel_id=1, source_target_pairs={{0,2},{1,3},{2,0},{3,1},{4,6},{5,7},{6,4},{7,5},{8,10},{9,11},{10,... | collective-permute-start | bytes 786440 | tf_op jit(solution)/shard_map/ppermute | solution.py:15
  52.7 13.8 %collective-permute-start.10 = (f16[512,128]{1,0:T(8,128)(2,1)S(1)}, f16[512,128]{1,0:T(8,128)(2,1)S(1)}, u32[]{:S(2)}, u32[]{:S(2)}) collective-permute-start(f16[512,128]{1,0:T(8,128)(2,1)S(1)} %get-tuple-element.41), channel_id=1, source_target_pairs={{0,2},{1,3},{2,0},{3,1},{4,6},{5,7},{6,4},{7,5},{8,10},{9,11},{10,... | collective-permute-start | bytes 393224 | tf_op jit(solution)/shard_map/ppermute | solution.py:15

commit v5 on v4

--- a/solution.py
+++ b/solution.py
@@ -183,7 +183,10 @@
     for _ in range(1, turns + 1):
         line.append([send(line[-1][h], "samples", along) for h in range(2)])
     side = [None] + [[send(line[t][h], "samples", lambda s: s ^ 1) for h in range(2)] for t in range(1, turns)]
-    side.append([send(jnp.where(even, line[turns][h], line[0][1 - h]), "samples", lambda s: s ^ 1) for h in range(2)])
+    side.append([])
+    for h in range(2):
+        chosen = jnp.where(even, line[turns][h], line[0][1 - h])
+        side[turns].append(send(chosen, "samples", lambda s: s ^ 1))
 
     for bit in range(samples.bit_length() - 1):
         more = send(sums, "samples", lambda s, step=1 << bit: s ^ step)

time: 69.3 us -> 69.3 us (level)
  no operation moved by 1% of the time
where the time goes in v5:
time: 69.3 us; the launch traced here: 69.1 us
  waiting for transfers between devices  36 us (52%)
  starting transfers between devices  23.4 us (34%)
  Pallas kernels  8.66 us (12%)
  other arithmetic  0.84 us (1%)
    ppermute x17, waiting for transfers between devices, send(): lax.ppermute(value, axis, [pair for pair in pairs if pair[1] is not None])  36 us
    ppermute x17, starting transfers between devices, send(): lax.ppermute(value, axis, [pair for pair in pairs if pair[1] is not None])  23.4 us
    pallas_call x9, Pallas kernels, call_kernel(): pl.pallas_call(body, out_shape=shapes, in_specs=specs, compiler_params=pl...  7.17 us
    pallas_call x1, Pallas kernels, encode(): pl.pallas_call(encode_body, name='encode', out_shape=(calls(rows), calls(...  1.49 us
  transfers between devices with their start and end apart: 17, of which 7 were waited for; matrix products, arithmetic and copies ran while one was open for 1% of the time, Pallas kernels for 8%

profile of v5, /device:TPU:0, one launch (start us, length us, event | category | flops | bytes accessed | tf_op | source)
XLA Modules:
  0.0 69.1 jit_solution(9437940773549149972)
XLA Ops:
  0.0 1.5 %encode.1 = (bf16[512,384]{1,0:T(8,128)(2,1)S(1)}, bf16[256,384]{1,0:T(8,128)(2,1)S(1)}, bf16[256,384]{1,0:T(8,128)(2,1)S(1)}, f32[2,384]{1,0:T(2,128)S(1)}) custom-call(s32[512,384]{1,0:T(8,128)} %genotype_ref.1, s32[512,384]{1,0:T(8,128)} %mask_ref.1), custom_call_target="tpu_custom_call" | custom-call | tf_op jit(solution)/shard_map/encode/pallas_call | solution.py:87
  1.5 5.1 %collective-permute-start.3 = (bf16[256,384]{1,0:T(8,128)(2,1)S(1)}, bf16[256,384]{1,0:T(8,128)(2,1)S(1)}, u32[]{:S(2)}, u32[]{:S(2)}) collective-permute-start(bf16[256,384]{1,0:T(8,128)(2,1)S(1)} %get-tuple-element.25), channel_id=1, source_target_pairs={{0,24},{4,28},{8,0},{12,4},{16,8},{20,12},{24,16},{28,20},{1,25},{... | collective-permute-start | bytes 589832 | tf_op jit(solution)/shard_map/ppermute | solution.py:15
  6.6 0.4 collective-permute-start.6
  7.1 4.8 %collective-permute-done.3.rest_2_ = bf16[256,384]{1,0:T(8,128)(2,1)S(1)} collective-permute-done((bf16[256,384]{1,0:T(8,128)(2,1)S(1)}, bf16[256,384]{1,0:T(8,128)(2,1)S(1)}, u32[]{:S(2)}, u32[]{:S(2)}) %collective-permute-start.3) | collective-permute-done | bytes 196640 | tf_op jit(solution)/shard_map/ppermute | solution.py:15
  11.9 4.3 %collective-permute-start.4 = (bf16[256,384]{1,0:T(8,128)(2,1)S(1)}, bf16[256,384]{1,0:T(8,128)(2,1)S(1)}, u32[]{:S(2)}, u32[]{:S(2)}) collective-permute-start(bf16[256,384]{1,0:T(8,128)(2,1)S(1)} %collective-permute-done.3.rest_2_), channel_id=1, source_target_pairs={{0,24},{4,28},{8,0},{12,4},{16,8},{20,12},{24,16},{28,20},{1,25},{... | collective-permute-start | bytes 589832 | tf_op jit(solution)/shard_map/ppermute | solution.py:15
  16.2 1.5 %collective-permute-start.8 = (bf16[256,384]{1,0:T(8,128)(2,1)S(1)}, bf16[256,384]{1,0:T(8,128)(2,1)S(1)}, u32[]{:S(2)}, u32[]{:S(2)}) collective-permute-start(bf16[256,384]{1,0:T(8,128)(2,1)S(1)} %collective-permute-done.3.rest_2_), channel_id=1, source_target_pairs={{0,4},{4,0},{8,12},{12,8},{16,20},{20,16},{24,28},{28,24},{1,5},{5... | collective-permute-start | bytes 589832 | tf_op jit(solution)/shard_map/ppermute | solution.py:15
  17.7 0.0 collective-permute-done.6.rest_1_
  17.7 0.5 collective-permute-start.7
  18.2 3.4 %collective-permute-start.11 = (bf16[256,384]{1,0:T(8,128)(2,1)S(1)}, bf16[256,384]{1,0:T(8,128)(2,1)S(1)}, u32[]{:S(2)}, u32[]{:S(2)}) collective-permute-start(bf16[256,384]{1,0:T(8,128)(2,1)S(1)} %collective-permute-done.6.rest_1_), channel_id=1, source_target_pairs={{0,24},{4,28},{8,0},{12,4},{16,8},{20,12},{24,16},{28,20},{1,25},{... | collective-permute-start | bytes 589832 | tf_op jit(solution)/shard_map/ppermute | solution.py:15
  21.6 0.0 collective-permute-done.4.rest_1_
  21.7 0.6 collective-permute-start.5
  22.2 1.5 %collective-permute-start = (f32[2,384]{1,0:T(2,128)S(1)}, f32[2,384]{1,0:T(2,128)S(1)}, u32[]{:S(2)}, u32[]{:S(2)}) collective-permute-start(f32[2,384]{1,0:T(2,128)S(1)} %get-tuple-element.22), channel_id=1, source_target_pairs={{0,4},{4,0},{8,12},{12,8},{16,20},{20,16},{24,28},{28,24},{1,5},{5... | collective-permute-start | bytes 9224 | tf_op jit(solution)/shard_map/ppermute | solution.py:15
  23.8 5.3 %collective-permute-done = f32[2,384]{1,0:T(2,128)S(1)} collective-permute-done((f32[2,384]{1,0:T(2,128)S(1)}, f32[2,384]{1,0:T(2,128)S(1)}, u32[]{:S(2)}, u32[]{:S(2)}) %collective-permute-start) | collective-permute-done | bytes 3104 | tf_op jit(solution)/shard_map/ppermute | solution.py:15
  29.1 0.0 collective-permute-start.1
  29.1 3.6 %collective-permute-done.1 = f32[2,384]{1,0:T(2,128)S(1)} collective-permute-done((f32[2,384]{1,0:T(2,128)S(1)}, f32[2,384]{1,0:T(2,128)S(1)}, u32[]{:S(2)}, u32[]{:S(2)}) %collective-permute-start.1) | collective-permute-done | bytes 3104 | tf_op jit(solution)/shard_map/ppermute | solution.py:15
  32.7 0.0 collective-permute-start.2
  32.7 4.5 %collective-permute-done.2.more_ref = f32[2,384]{1,0:T(2,128)S(1)} collective-permute-done((f32[2,384]{1,0:T(2,128)S(1)}, f32[2,384]{1,0:T(2,128)S(1)}, u32[]{:S(2)}, u32[]{:S(2)}) %collective-permute-start.2) | collective-permute-done | bytes 3104 | tf_op jit(solution)/shard_map/ppermute | solution.py:15
  37.2 0.2 shard_map.28
  37.4 1.2 %shard_map.32 = (f32[2,512,256]{2,1,0:T(8,128)S(1)}, f32[2,512,256]{2,1,0:T(8,128)S(1)}) custom-call(bf16[512,384]{1,0:T(8,128)(2,1)S(1)} %get-tuple-element.23.left_ref, f32[2,384]{1,0:T(2,128)S(1)} %get-tuple-element.24.factors_ref, bf16[512,384]{1,0:T(8,128)(2,1)S(1)} %get-tuple-element.21.calls_ref.rest_0_, ...), custom_call_target="tpu_custom_call" | custom-call | flops 301989888 | bytes 524288 | tf_op jit(solution)/shard_map/pallas_call | solution.py:40
  38.6 0.0 collective-permute-done.11.rest_0_
  38.6 0.4 shard_map.33
  39.0 0.1 convert_element_type.47
  39.1 0.1 collective-permute-start.15
  39.2 0.0 collective-permute-done.7.rest_1_.rest_2_
  39.2 0.0 collective-permute-done.8.rest_2_.rest_1_
  39.2 0.0 collective-permute-done.5.rest_0_
  39.2 1.3 %shard_map.29 = (f32[2,512,128]{2,1,0:T(8,128)S(1)}, f32[2,512,128]{2,1,0:T(8,128)S(1)}) custom-call(bf16[512,384]{1,0:T(8,128)(2,1)S(1)} %get-tuple-element.23.left_ref, f32[2,384]{1,0:T(2,128)S(1)} %get-tuple-element.24.factors_ref, bf16[256,384]{1,0:T(8,128)(2,1)S(1)} %collective-permute-done.5.rest_0_, ...), custom_call_target="tpu_custom_call" | custom-call | flops 201326592 | bytes 262144 | tf_op jit(solution)/shard_map/pallas_call | solution.py:40
  40.5 0.5 collective-permute-start.9
  41.1 1.6 %collective-permute-start.12 = (bf16[256,384]{1,0:T(8,128)(2,1)S(1)}, bf16[256,384]{1,0:T(8,128)(2,1)S(1)}, u32[]{:S(2)}, u32[]{:S(2)}) collective-permute-start(bf16[256,384]{1,0:T(8,128)(2,1)S(1)} %broadcast_select_fusion), channel_id=1, source_target_pairs={{0,4},{4,0},{8,12},{12,8},{16,20},{20,16},{24,28},{28,24},{1,5},{5... | collective-permute-start | bytes 589832 | tf_op jit(solution)/shard_map/ppermute | solution.py:15
  42.7 0.8 %shard_map.30 = (f32[2,512,256]{2,1,0:T(8,128)S(1)}, f32[2,512,256]{2,1,0:T(8,128)S(1)}) custom-call(bf16[512,384]{1,0:T(8,128)(2,1)S(1)} %get-tuple-element.23.left_ref, f32[2,384]{1,0:T(2,128)S(1)} %get-tuple-element.24.factors_ref, bf16[512,384]{1,0:T(8,128)(2,1)S(1)} %get-tuple-element.21.calls_ref.rest_0_, ...), custom_call_target="tpu_custom_call" | custom-call | flops 201326592 | bytes 524288 | tf_op jit(solution)/shard_map/pallas_call | solution.py:40
  43.5 4.5 %collective-permute-done.12.rest_0_ = bf16[256,384]{1,0:T(8,128)(2,1)S(1)} collective-permute-done((bf16[256,384]{1,0:T(8,128)(2,1)S(1)}, bf16[256,384]{1,0:T(8,128)(2,1)S(1)}, u32[]{:S(2)}, u32[]{:S(2)}) %collective-permute-start.12) | collective-permute-done | bytes 196640 | tf_op jit(solution)/shard_map/ppermute | solution.py:15
  48.0 0.8 %shard_map.31 = (f32[2,512,256]{2,1,0:T(8,128)S(1)}, f32[2,512,256]{2,1,0:T(8,128)S(1)}) custom-call(bf16[512,384]{1,0:T(8,128)(2,1)S(1)} %get-tuple-element.23.left_ref, f32[2,384]{1,0:T(2,128)S(1)} %get-tuple-element.24.factors_ref, bf16[256,384]{1,0:T(8,128)(2,1)S(1)} %collective-permute-done.12.rest_0_, ...), custom_call_target="tpu_custom_call", output_to_operand_aliasing={{0}: (5, {}), {1}: (6, {})} | custom-call | flops 201326592 | bytes 524288 | tf_op jit(solution)/shard_map/pallas_call | solution.py:40
  48.8 0.1 convert_element_type.43
  48.9 0.1 collective-permute-start.13
  49.0 0.0 collective-permute-done.9
  49.0 0.1 convert_add_fusion.2
  49.1 0.0 collective-permute-done.15
  49.1 0.1 convert_add_fusion
  49.2 0.1 fusion.1
  49.3 1.6 %collective-permute-start.16 = (f16[512,256]{1,0:T(8,128)(2,1)S(1)}, f16[512,256]{1,0:T(8,128)(2,1)S(1)}, u32[]{:S(2)}, u32[]{:S(2)}) collective-permute-start(f16[512,256]{1,0:T(8,128)(2,1)S(1)} %get-tuple-element.37), channel_id=1, source_target_pairs={{0,2},{1,3},{2,0},{3,1},{4,6},{5,7},{6,4},{7,5},{8,10},{9,11},{10,... | collective-permute-start | bytes 786440 | tf_op jit(solution)/shard_map/ppermute | solution.py:15
  50.9 0.1 collective-permute-done.13
  50.9 0.1 convert_add_fusion.1
  51.0 0.1 fusion
  51.1 1.6 %collective-permute-start.14 = (f16[512,256]{1,0:T(8,128)(2,1)S(1)}, f16[512,256]{1,0:T(8,128)(2,1)S(1)}, u32[]{:S(2)}, u32[]{:S(2)}) collective-permute-start(f16[512,256]{1,0:T(8,128)(2,1)S(1)} %get-tuple-element.39), channel_id=1, source_target_pairs={{0,2},{1,3},{2,0},{3,1},{4,6},{5,7},{6,4},{7,5},{8,10},{9,11},{10,... | collective-permute-start | bytes 786440 | tf_op jit(solution)/shard_map/ppermute | solution.py:15
  52.7 0.6 collective-permute-start.10
  53.3 13.2 %collective-permute-done.10 = f16[512,128]{1,0:T(8,128)(2,1)S(1)} collective-permute-done((f16[512,128]{1,0:T(8,128)(2,1)S(1)}, f16[512,128]{1,0:T(8,128)(2,1)S(1)}, u32[]{:S(2)}, u32[]{:S(2)}) %collective-permute-start.10) | collective-permute-done | bytes 131104 | tf_op jit(solution)/shard_map/ppermute | solution.py:15
  66.5 0.0 collective-permute-done.16
  66.6 0.9 %shard_map.34.rest_0_ = f32[512,640]{1,0:T(8,128)} custom-call(f32[512,256]{1,0:T(8,128)S(1)} %get-tuple-element.38.ours_ref, f32[512,256]{1,0:T(8,128)S(1)} %convert_element_type.50.got_ref), custom_call_target="tpu_custom_call" | custom-call | flops 131072 | bytes 524288 | tf_op jit(solution)/shard_map/pallas_call | solution.py:40
  67.4 0.0 collective-permute-done.14
  67.5 0.9 %shard_map.35.rest_0_ = f32[512,640]{1,0:T(8,128)} custom-call(f32[512,256]{1,0:T(8,128)S(1)} %get-tuple-element.40.ours_ref, f32[512,256]{1,0:T(8,128)S(1)} %convert_element_type.46.got_ref, f32[512,640]{1,0:T(8,128)} %shard_map.34.rest_0_), custom_call_target="tpu_custom_call", output_to_operand_aliasing={{}: (2, {})} | custom-call | flops 131072 | bytes 524288 | tf_op jit(solution)/shard_map/pallas_call | solution.py:40
  68.4 0.7 %shard_map.36 = f32[512,640]{1,0:T(8,128)} custom-call(f32[512,128]{1,0:T(8,128)S(1)} %get-tuple-element.42.ours_ref, f32[512,128]{1,0:T(8,128)S(1)} %convert_element_type.42.got_ref, f32[512,640]{1,0:T(8,128)} %shard_map.35.rest_0_), custom_call_target="tpu_custom_call", output_to_operand_aliasing={{}: (2, {})} | custom-call | flops 65536 | bytes 262144 | tf_op jit(solution)/shard_map/pallas_call | solution.py:40
  (9 shorter events, 0.2 us)
Async XLA Ops:
  1.5 10.4 %collective-permute-start.3 = (bf16[256,384]{1,0:T(8,128)(2,1)S(1)}, bf16[256,384]{1,0:T(8,128)(2,1)S(1)}, u32[]{:S(2)}, u32[]{:S(2)}) collective-permute-start(bf16[256,384]{1,0:T(8,128)(2,1)S(1)} %get-tuple-element.25), channel_id=1, source_target_pairs={{0,24},{4,28},{8,0},{12,4},{16,8},{20,12},{24,16},{28,20},{1,25},{... | collective-permute-start | bytes 589832 | tf_op jit(solution)/shard_map/ppermute | solution.py:15
  6.6 11.1 %collective-permute-start.6 = (bf16[256,384]{1,0:T(8,128)(2,1)S(1)}, bf16[256,384]{1,0:T(8,128)(2,1)S(1)}, u32[]{:S(2)}, u32[]{:S(2)}) collective-permute-start(bf16[256,384]{1,0:T(8,128)(2,1)S(1)} %get-tuple-element.26), channel_id=1, source_target_pairs={{0,24},{4,28},{8,0},{12,4},{16,8},{20,12},{24,16},{28,20},{1,25},{... | collective-permute-start | bytes 589832 | tf_op jit(solution)/shard_map/ppermute | solution.py:15
  11.9 9.7 %collective-permute-start.4 = (bf16[256,384]{1,0:T(8,128)(2,1)S(1)}, bf16[256,384]{1,0:T(8,128)(2,1)S(1)}, u32[]{:S(2)}, u32[]{:S(2)}) collective-permute-start(bf16[256,384]{1,0:T(8,128)(2,1)S(1)} %collective-permute-done.3.rest_2_), channel_id=1, source_target_pairs={{0,24},{4,28},{8,0},{12,4},{16,8},{20,12},{24,16},{28,20},{1,25},{... | collective-permute-start | bytes 589832 | tf_op jit(solution)/shard_map/ppermute | solution.py:15
  16.2 23.0 %collective-permute-start.8 = (bf16[256,384]{1,0:T(8,128)(2,1)S(1)}, bf16[256,384]{1,0:T(8,128)(2,1)S(1)}, u32[]{:S(2)}, u32[]{:S(2)}) collective-permute-start(bf16[256,384]{1,0:T(8,128)(2,1)S(1)} %collective-permute-done.3.rest_2_), channel_id=1, source_target_pairs={{0,4},{4,0},{8,12},{12,8},{16,20},{20,16},{24,28},{28,24},{1,5},{5... | collective-permute-start | bytes 589832 | tf_op jit(solution)/shard_map/ppermute | solution.py:15
  17.7 21.4 %collective-permute-start.7 = (bf16[256,384]{1,0:T(8,128)(2,1)S(1)}, bf16[256,384]{1,0:T(8,128)(2,1)S(1)}, u32[]{:S(2)}, u32[]{:S(2)}) collective-permute-start(bf16[256,384]{1,0:T(8,128)(2,1)S(1)} %collective-permute-done.6.rest_1_), channel_id=1, source_target_pairs={{0,4},{4,0},{8,12},{12,8},{16,20},{20,16},{24,28},{28,24},{1,5},{5... | collective-permute-start | bytes 589832 | tf_op jit(solution)/shard_map/ppermute | solution.py:15
  18.2 20.3 %collective-permute-start.11 = (bf16[256,384]{1,0:T(8,128)(2,1)S(1)}, bf16[256,384]{1,0:T(8,128)(2,1)S(1)}, u32[]{:S(2)}, u32[]{:S(2)}) collective-permute-start(bf16[256,384]{1,0:T(8,128)(2,1)S(1)} %collective-permute-done.6.rest_1_), channel_id=1, source_target_pairs={{0,24},{4,28},{8,0},{12,4},{16,8},{20,12},{24,16},{28,20},{1,25},{... | collective-permute-start | bytes 589832 | tf_op jit(solution)/shard_map/ppermute | solution.py:15
  21.7 17.5 %collective-permute-start.5 = (bf16[256,384]{1,0:T(8,128)(2,1)S(1)}, bf16[256,384]{1,0:T(8,128)(2,1)S(1)}, u32[]{:S(2)}, u32[]{:S(2)}) collective-permute-start(bf16[256,384]{1,0:T(8,128)(2,1)S(1)} %broadcast_select_fusion.1), channel_id=1, source_target_pairs={{0,4},{4,0},{8,12},{12,8},{16,20},{20,16},{24,28},{28,24},{1,5},{5... | collective-permute-start | bytes 589832 | tf_op jit(solution)/shard_map/ppermute | solution.py:15
  22.2 6.8 %collective-permute-start = (f32[2,384]{1,0:T(2,128)S(1)}, f32[2,384]{1,0:T(2,128)S(1)}, u32[]{:S(2)}, u32[]{:S(2)}) collective-permute-start(f32[2,384]{1,0:T(2,128)S(1)} %get-tuple-element.22), channel_id=1, source_target_pairs={{0,4},{4,0},{8,12},{12,8},{16,20},{20,16},{24,28},{28,24},{1,5},{5... | collective-permute-start | bytes 9224 | tf_op jit(solution)/shard_map/ppermute | solution.py:15
  29.1 3.6 %collective-permute-start.1 = (f32[2,384]{1,0:T(2,128)S(1)}, f32[2,384]{1,0:T(2,128)S(1)}, u32[]{:S(2)}, u32[]{:S(2)}) collective-permute-start(f32[2,384]{1,0:T(2,128)S(1)} %add.19), channel_id=1, source_target_pairs={{0,8},{4,12},{8,0},{12,4},{16,24},{20,28},{24,16},{28,20},{1,9},{5... | collective-permute-start | bytes 9224 | tf_op jit(solution)/shard_map/ppermute | solution.py:15
  32.7 4.5 %collective-permute-start.2 = (f32[2,384]{1,0:T(2,128)S(1)}, f32[2,384]{1,0:T(2,128)S(1)}, u32[]{:S(2)}, u32[]{:S(2)}) collective-permute-start(f32[2,384]{1,0:T(2,128)S(1)} %add.20.sums_ref), channel_id=1, source_target_pairs={{0,16},{4,20},{8,24},{12,28},{16,0},{20,4},{24,8},{28,12},{1,17},{... | collective-permute-start | bytes 9224 | tf_op jit(solution)/shard_map/ppermute | solution.py:15
  39.1 10.0 %collective-permute-start.15 = (f16[2,512,256]{2,1,0:T(8,128)(2,1)S(1)}, f16[2,512,256]{2,1,0:T(8,128)(2,1)S(1)}, u32[]{:S(2)}, u32[]{:S(2)}) collective-permute-start(f16[2,512,256]{2,1,0:T(8,128)(2,1)S(1)} %convert_element_type.47), channel_id=1, source_target_pairs={{0,1},{1,0},{2,3},{3,2},{4,5},{5,4},{6,7},{7,6},{8,9},{9,8},{10,11... | collective-permute-start | bytes 1572872 | tf_op jit(solution)/shard_map/ppermute | solution.py:15
  40.5 8.5 %collective-permute-start.9 = (f16[2,512,128]{2,1,0:T(8,128)(2,1)S(1)}, f16[2,512,128]{2,1,0:T(8,128)(2,1)S(1)}, u32[]{:S(2)}, u32[]{:S(2)}) collective-permute-start(f16[2,512,128]{2,1,0:T(8,128)(2,1)S(1)} %convert_element_type.39), channel_id=1, source_target_pairs={{0,1},{1,0},{2,3},{3,2},{4,5},{5,4},{6,7},{7,6},{8,9},{9,8},{10,11... | collective-permute-start | bytes 786440 | tf_op jit(solution)/shard_map/ppermute | solution.py:15
  41.1 6.9 %collective-permute-start.12 = (bf16[256,384]{1,0:T(8,128)(2,1)S(1)}, bf16[256,384]{1,0:T(8,128)(2,1)S(1)}, u32[]{:S(2)}, u32[]{:S(2)}) collective-permute-start(bf16[256,384]{1,0:T(8,128)(2,1)S(1)} %broadcast_select_fusion), channel_id=1, source_target_pairs={{0,4},{4,0},{8,12},{12,8},{16,20},{20,16},{24,28},{28,24},{1,5},{5... | collective-permute-start | bytes 589832 | tf_op jit(solution)/shard_map/ppermute | solution.py:15
  48.9 2.0 %collective-permute-start.13 = (f16[2,512,256]{2,1,0:T(8,128)(2,1)S(1)}, f16[2,512,256]{2,1,0:T(8,128)(2,1)S(1)}, u32[]{:S(2)}, u32[]{:S(2)}) collective-permute-start(f16[2,512,256]{2,1,0:T(8,128)(2,1)S(1)} %convert_element_type.43), channel_id=1, source_target_pairs={{0,1},{1,0},{2,3},{3,2},{4,5},{5,4},{6,7},{7,6},{8,9},{9,8},{10,11... | collective-permute-start | bytes 1572872 | tf_op jit(solution)/shard_map/ppermute | solution.py:15
  49.3 17.2 %collective-permute-start.16 = (f16[512,256]{1,0:T(8,128)(2,1)S(1)}, f16[512,256]{1,0:T(8,128)(2,1)S(1)}, u32[]{:S(2)}, u32[]{:S(2)}) collective-permute-start(f16[512,256]{1,0:T(8,128)(2,1)S(1)} %get-tuple-element.37), channel_id=1, source_target_pairs={{0,2},{1,3},{2,0},{3,1},{4,6},{5,7},{6,4},{7,5},{8,10},{9,11},{10,... | collective-permute-start | bytes 786440 | tf_op jit(solution)/shard_map/ppermute | solution.py:15
  51.1 16.3 %collective-permute-start.14 = (f16[512,256]{1,0:T(8,128)(2,1)S(1)}, f16[512,256]{1,0:T(8,128)(2,1)S(1)}, u32[]{:S(2)}, u32[]{:S(2)}) collective-permute-start(f16[512,256]{1,0:T(8,128)(2,1)S(1)} %get-tuple-element.39), channel_id=1, source_target_pairs={{0,2},{1,3},{2,0},{3,1},{4,6},{5,7},{6,4},{7,5},{8,10},{9,11},{10,... | collective-permute-start | bytes 786440 | tf_op jit(solution)/shard_map/ppermute | solution.py:15
  52.7 13.8 %collective-permute-start.10 = (f16[512,128]{1,0:T(8,128)(2,1)S(1)}, f16[512,128]{1,0:T(8,128)(2,1)S(1)}, u32[]{:S(2)}, u32[]{:S(2)}) collective-permute-start(f16[512,128]{1,0:T(8,128)(2,1)S(1)} %get-tuple-element.41), channel_id=1, source_target_pairs={{0,2},{1,3},{2,0},{3,1},{4,6},{5,7},{6,4},{7,5},{8,10},{9,11},{10,... | collective-permute-start | bytes 393224 | tf_op jit(solution)/shard_map/ppermute | solution.py:15

commit v6 on v5

--- a/solution.py
+++ b/solution.py
@@ -41,7 +41,7 @@
         body,
         out_shape=shapes,
         in_specs=specs,
-        compiler_params=pltpu.CompilerParams(vmem_limit_bytes=24 * 2**20),
+        compiler_params=pltpu.CompilerParams(vmem_limit_bytes=12 * 2**20),
         cost_estimate=pl.CostEstimate(flops=flops, bytes_accessed=moved, transcendentals=0),
         **more,
     )(*operands)
@@ -123,32 +123,30 @@
 
 
 def products_body(cases, down, left_ref, factors_ref, *rest):
-    *refs, keep_ref, away_ref, right_ref = rest
+    refs, target_refs, right_ref = rest[:-5], rest[-5:-1], rest[-1]
     shift, scale = factors_ref[0:1, :], factors_ref[1:2, :]
     device = lax.axis_index("snps")
     parity = lax.axis_index("samples") % 2
-    for strip, by_parity in cases:
-        for odd, (at, begin) in enumerate(by_parity):
-
-            def fill(at=at, begin=begin):
-                rows = refs[at][pl.ds(begin, right_ref.shape[0]), :]
-                right_ref[...] = standardized(rows, shift, scale)
-
-            if by_parity[0] != by_parity[1]:
-                pl.when(parity == odd)(fill)
-            elif not odd:
-                fill()
-        place = device ^ strip
-        for bit, target_ref in enumerate((keep_ref, away_ref)):
-
-            @pl.when(place % 2 == bit)
-            def _(target_ref=target_ref, place=place):
-                target_ref[place // 2] = multiply(left_ref[...], right_ref[...]) * down
+    for strip, at, begin, only in cases:
+
+        def work(strip=strip, at=at, begin=begin):
+            rows = refs[at][pl.ds(begin, right_ref.shape[0]), :]
+            right_ref[...] = standardized(rows, shift, scale)
+            place = device ^ strip
+            for index, target_ref in enumerate(target_refs):
+
+                @pl.when(place == index)
+                def _(target_ref=target_ref):
+                    target_ref[...] = multiply(left_ref[...], right_ref[...]) * down
+
+        if only is None:
+            work()
+        else:
+            pl.when(parity == only)(work)
 
 
 def products_more_body(cases, down, left_ref, factors_ref, *rest):
-    *refs, _, _, keep_ref, away_ref, right_ref = rest
-    products_body(cases, down, left_ref, factors_ref, *refs, keep_ref, away_ref, right_ref)
+    products_body(cases, down, left_ref, factors_ref, *rest[:-9], *rest[-5:])
 
 
 def add_body(places, up, ours_ref, got_ref, *rest):
@@ -213,47 +211,55 @@
     count = len(table[0][0])
     quarter = half_rows // 2
 
-    def products(n, chosen, so_far):
-        columns = half_rows if n < count else quarter
+    def sources(n):
+        result = []
+        for strip, (by_arrival, _, cut) in enumerate(table):
+            k, h = by_arrival[n] if n < count else cut
+            shift_rows = quarter if n == count and strip % 2 else 0
+            for odd in range(2):
+                array, begin = source(k, h, odd)
+                last = (2 * turns - 1 if odd else 1) if k % 2 else (2 * turns if n == 0 else -1)
+                result.append((strip, array, begin + shift_rows, odd if k % 2 else None, k == last))
+                if k % 2 == 0:
+                    break
+        return result
+
+    def products(columns, chosen, so_far):
         arrays, cases = [], []
-        for strip in chosen:
-            by_arrival, _, cut = table[strip]
-            by_parity = []
-            for odd in range(2):
-                array, begin = source(*(by_arrival[n] if n < count else cut), odd)
-                at = next((i for i, known in enumerate(arrays) if known is array), len(arrays))
-                if at == len(arrays):
-                    arrays.append(array)
-                if n == count and strip % 2:
-                    begin += quarter
-                by_parity.append((at, begin))
-            cases.append((strip, tuple(by_parity)))
-        shape = jax.ShapeDtypeStruct((2, rows, columns), jnp.float32)
+        for strip, array, begin, only, _ in chosen:
+            at = next((i for i, known in enumerate(arrays) if known is array), len(arrays))
+            if at == len(arrays):
+                arrays.append(array)
+            cases.append((strip, at, begin, only))
+        shape = jax.ShapeDtypeStruct((rows, columns), jnp.float32)
         operands = (left, pair, *arrays, *so_far)
         return call_kernel(
             functools.partial(products_body if not so_far else products_more_body, tuple(cases), down),
-            (shape, shape), operands, [VMEM] * len(operands),
+            (shape,) * 4, operands, [VMEM] * len(operands),
             2 * rows * snp_part * columns * len(chosen), 4 * rows * columns,
-            out_specs=(VMEM, VMEM),
+            out_specs=(VMEM,) * 4,
             scratch_shapes=[pltpu.VMEM((columns, snp_part), jnp.bfloat16)],
-            input_output_aliases={len(operands) - 2 + i: i for i in range(len(so_far))},
+            input_output_aliases={len(operands) - 4 + i: i for i in range(len(so_far))},
         )
 
-    pieces = []
+    pieces, partners = [], []
     for n in range(count + 1):
-        last_in = (1, 2 * turns - 1) + ((2 * turns,) if n == 0 else ())
-        late = [
-            strip for strip, (by_arrival, _, cut) in enumerate(table)
-            if (by_arrival[n] if n < count else cut)[0] in last_in
-        ]
+        columns = half_rows if n < count else quarter
         both = ()
-        for chosen in ([s for s in range(4) if s not in late], late):
+        for wanted in (False, True):
+            chosen = [entry for entry in sources(n) if entry[-1] == wanted]
             if chosen:
-                both = products(n, chosen, both)
-        keep, away = both
-        summed = keep + swap_core(away.astype(jnp.float16)).astype(jnp.float32)
-        got = send(summed[1].astype(jnp.float16), "snps", lambda s: s ^ 2)
-        pieces.append((summed[0], got.astype(jnp.float32)))
+                both = products(columns, chosen, both)
+        own, own_away, neighbour, neighbour_away = both
+        other = swap_core(neighbour_away.astype(jnp.float16))
+        theirs = (neighbour + other.astype(jnp.float32)).astype(jnp.float16)
+        pieces.append((own, send(theirs, "snps", lambda s: s ^ 2)))
+        partners.append(own_away.astype(jnp.float16))
+    other = swap_core(jnp.concatenate(partners, axis=1))
+    for n, (keep, got) in enumerate(pieces):
+        begin = n * half_rows
+        ours = keep + other[:, begin : begin + keep.shape[1]].astype(jnp.float32)
+        pieces[n] = (ours, got.astype(jnp.float32))
     out = None
     for n, operands in enumerate(pieces):
         places = []

time: 69.3 us -> 69.4 us (level)
    ppermute x17 -> x18, starting transfers between devices: 23.4 us -> 23 us  [send(): lax.ppermute(value, axis, [pair for pair in pairs if pair[1] is not None])]
    pallas_call x9 -> x10, Pallas kernels: 7.17 us -> 7.42 us  [call_kernel(): pl.pallas_call(body, out_shape=shapes, in_specs=specs, compiler_params=pl...]
    ppermute x17 -> x18, waiting for transfers between devices: 36 us -> 36 us  [send(): lax.ppermute(value, axis, [pair for pair in pairs if pair[1] is not None])]
  transfers between devices with their start and end apart: 17 -> 18, of which waited for: 7 -> 6; matrix products, arithmetic and copies ran while one was open for 1% -> 1% of each run, Pallas kernels for 8% -> 7%
where the time goes in v6:
time: 69.4 us; the launch traced here: 69.2 us
  waiting for transfers between devices  36 us (52%)
  starting transfers between devices  23 us (33%)
  Pallas kernels  8.91 us (13%)
  other arithmetic  0.9 us (1%)
    ppermute x18, waiting for transfers between devices, send(): lax.ppermute(value, axis, [pair for pair in pairs if pair[1] is not None])  36 us
    ppermute x18, starting transfers between devices, send(): lax.ppermute(value, axis, [pair for pair in pairs if pair[1] is not None])  23 us
    pallas_call x10, Pallas kernels, call_kernel(): pl.pallas_call(body, out_shape=shapes, in_specs=specs, compiler_params=pl...  7.42 us
    pallas_call x1, Pallas kernels, encode(): pl.pallas_call(encode_body, name='encode', out_shape=(calls(rows), calls(...  1.49 us
  transfers between devices with their start and end apart: 18, of which 6 were waited for; matrix products, arithmetic and copies ran while one was open for 1% of the time, Pallas kernels for 7%

profile of v6, /device:TPU:0, one launch (start us, length us, event | category | flops | bytes accessed | tf_op | source)
XLA Modules:
  0.0 69.2 jit_solution(9026089418310460509)
XLA Ops:
  0.0 1.5 %encode.1 = (bf16[512,384]{1,0:T(8,128)(2,1)S(1)}, bf16[256,384]{1,0:T(8,128)(2,1)S(1)}, bf16[256,384]{1,0:T(8,128)(2,1)S(1)}, f32[2,384]{1,0:T(2,128)S(1)}) custom-call(s32[512,384]{1,0:T(8,128)} %genotype_ref.1, s32[512,384]{1,0:T(8,128)} %mask_ref.1), custom_call_target="tpu_custom_call" | custom-call | tf_op jit(solution)/shard_map/encode/pallas_call | solution.py:87
  1.5 5.1 %collective-permute-start.3 = (bf16[256,384]{1,0:T(8,128)(2,1)S(1)}, bf16[256,384]{1,0:T(8,128)(2,1)S(1)}, u32[]{:S(2)}, u32[]{:S(2)}) collective-permute-start(bf16[256,384]{1,0:T(8,128)(2,1)S(1)} %get-tuple-element.39), channel_id=1, source_target_pairs={{0,24},{4,28},{8,0},{12,4},{16,8},{20,12},{24,16},{28,20},{1,25},{... | collective-permute-start | bytes 589832 | tf_op jit(solution)/shard_map/ppermute | solution.py:15
  6.6 0.4 collective-permute-start.6
  7.1 4.8 %collective-permute-done.3.rest_2_ = bf16[256,384]{1,0:T(8,128)(2,1)S(1)} collective-permute-done((bf16[256,384]{1,0:T(8,128)(2,1)S(1)}, bf16[256,384]{1,0:T(8,128)(2,1)S(1)}, u32[]{:S(2)}, u32[]{:S(2)}) %collective-permute-start.3) | collective-permute-done | bytes 196640 | tf_op jit(solution)/shard_map/ppermute | solution.py:15
  11.9 4.3 %collective-permute-start.4 = (bf16[256,384]{1,0:T(8,128)(2,1)S(1)}, bf16[256,384]{1,0:T(8,128)(2,1)S(1)}, u32[]{:S(2)}, u32[]{:S(2)}) collective-permute-start(bf16[256,384]{1,0:T(8,128)(2,1)S(1)} %collective-permute-done.3.rest_2_), channel_id=1, source_target_pairs={{0,24},{4,28},{8,0},{12,4},{16,8},{20,12},{24,16},{28,20},{1,25},{... | collective-permute-start | bytes 589832 | tf_op jit(solution)/shard_map/ppermute | solution.py:15
  16.2 1.5 %collective-permute-start.8 = (bf16[256,384]{1,0:T(8,128)(2,1)S(1)}, bf16[256,384]{1,0:T(8,128)(2,1)S(1)}, u32[]{:S(2)}, u32[]{:S(2)}) collective-permute-start(bf16[256,384]{1,0:T(8,128)(2,1)S(1)} %collective-permute-done.3.rest_2_), channel_id=1, source_target_pairs={{0,4},{4,0},{8,12},{12,8},{16,20},{20,16},{24,28},{28,24},{1,5},{5... | collective-permute-start | bytes 589832 | tf_op jit(solution)/shard_map/ppermute | solution.py:15
  17.7 0.0 collective-permute-done.6.rest_1_
  17.7 2.4 %collective-permute-start.9 = (bf16[256,384]{1,0:T(8,128)(2,1)S(1)}, bf16[256,384]{1,0:T(8,128)(2,1)S(1)}, u32[]{:S(2)}, u32[]{:S(2)}) collective-permute-start(bf16[256,384]{1,0:T(8,128)(2,1)S(1)} %collective-permute-done.6.rest_1_), channel_id=1, source_target_pairs={{0,24},{4,28},{8,0},{12,4},{16,8},{20,12},{24,16},{28,20},{1,25},{... | collective-permute-start | bytes 589832 | tf_op jit(solution)/shard_map/ppermute | solution.py:15
  20.1 1.5 %collective-permute-start.7 = (bf16[256,384]{1,0:T(8,128)(2,1)S(1)}, bf16[256,384]{1,0:T(8,128)(2,1)S(1)}, u32[]{:S(2)}, u32[]{:S(2)}) collective-permute-start(bf16[256,384]{1,0:T(8,128)(2,1)S(1)} %collective-permute-done.6.rest_1_), channel_id=1, source_target_pairs={{0,4},{4,0},{8,12},{12,8},{16,20},{20,16},{24,28},{28,24},{1,5},{5... | collective-permute-start | bytes 589832 | tf_op jit(solution)/shard_map/ppermute | solution.py:15
  21.6 0.0 collective-permute-done.4.rest_3_
  21.7 0.6 collective-permute-start.5
  22.2 1.4 %collective-permute-done.9.rest_0_ = bf16[256,384]{1,0:T(8,128)(2,1)S(1)} collective-permute-done((bf16[256,384]{1,0:T(8,128)(2,1)S(1)}, bf16[256,384]{1,0:T(8,128)(2,1)S(1)}, u32[]{:S(2)}, u32[]{:S(2)}) %collective-permute-start.9) | collective-permute-done | bytes 196640 | tf_op jit(solution)/shard_map/ppermute | solution.py:15
  23.6 1.6 %collective-permute-start.10 = (bf16[256,384]{1,0:T(8,128)(2,1)S(1)}, bf16[256,384]{1,0:T(8,128)(2,1)S(1)}, u32[]{:S(2)}, u32[]{:S(2)}) collective-permute-start(bf16[256,384]{1,0:T(8,128)(2,1)S(1)} %broadcast_select_fusion), channel_id=1, source_target_pairs={{0,4},{4,0},{8,12},{12,8},{16,20},{20,16},{24,28},{28,24},{1,5},{5... | collective-permute-start | bytes 589832 | tf_op jit(solution)/shard_map/ppermute | solution.py:15
  25.2 0.5 collective-permute-start
  25.7 8.9 %collective-permute-done = f32[2,384]{1,0:T(2,128)S(1)} collective-permute-done((f32[2,384]{1,0:T(2,128)S(1)}, f32[2,384]{1,0:T(2,128)S(1)}, u32[]{:S(2)}, u32[]{:S(2)}) %collective-permute-start) | collective-permute-done | bytes 3104 | tf_op jit(solution)/shard_map/ppermute | solution.py:15
  34.6 0.0 collective-permute-start.1
  34.6 3.6 %collective-permute-done.1 = f32[2,384]{1,0:T(2,128)S(1)} collective-permute-done((f32[2,384]{1,0:T(2,128)S(1)}, f32[2,384]{1,0:T(2,128)S(1)}, u32[]{:S(2)}, u32[]{:S(2)}) %collective-permute-start.1) | collective-permute-done | bytes 3104 | tf_op jit(solution)/shard_map/ppermute | solution.py:15
  38.2 0.0 collective-permute-start.2
  38.2 4.5 %collective-permute-done.2.more_ref = f32[2,384]{1,0:T(2,128)S(1)} collective-permute-done((f32[2,384]{1,0:T(2,128)S(1)}, f32[2,384]{1,0:T(2,128)S(1)}, u32[]{:S(2)}, u32[]{:S(2)}) %collective-permute-start.2) | collective-permute-done | bytes 3104 | tf_op jit(solution)/shard_map/ppermute | solution.py:15
  42.7 0.2 shard_map.28
  42.9 1.2 %shard_map.31 = (f32[512,256]{1,0:T(8,128)S(1)}, f32[512,256]{1,0:T(8,128)S(1)}, f32[512,256]{1,0:T(8,128)S(1)}, f32[512,256]{1,0:T(8,128)S(1)}) custom-call(bf16[512,384]{1,0:T(8,128)(2,1)S(1)} %get-tuple-element.37.left_ref, f32[2,384]{1,0:T(2,128)S(1)} %get-tuple-element.38.factors_ref, bf16[512,384]{1,0:T(8,128)(2,1)S(1)} %get-tuple-element.35.calls_ref.rest_0_, ...), custom_call_target="tpu_custom_call" | custom-call | flops 301989888 | bytes 524288 | tf_op jit(solution)/shard_map/pallas_call | solution.py:40
  44.1 0.4 shard_map.32
  44.6 0.1 collective-permute-start.16
  44.7 0.0 collective-permute-done.8.rest_1_
  44.7 0.0 collective-permute-done.7.rest_0_.rest_2_
  44.7 0.7 shard_map.29
  45.4 1.4 %shard_map.33 = (f32[512,256]{1,0:T(8,128)S(1)}, f32[512,256]{1,0:T(8,128)S(1)}, f32[512,256]{1,0:T(8,128)S(1)}, f32[512,256]{1,0:T(8,128)S(1)}) custom-call(bf16[512,384]{1,0:T(8,128)(2,1)S(1)} %get-tuple-element.37.left_ref, f32[2,384]{1,0:T(2,128)S(1)} %get-tuple-element.38.factors_ref, bf16[512,384]{1,0:T(8,128)(2,1)S(1)} %get-tuple-element.35.calls_ref.rest_0_, ...), custom_call_target="tpu_custom_call" | custom-call | flops 402653184 | bytes 524288 | tf_op jit(solution)/shard_map/pallas_call | solution.py:40
  46.8 0.0 collective-permute-done.5.rest_0_
  46.8 0.7 shard_map.30
  47.5 0.6 collective-permute-start.12
  48.1 0.0 collective-permute-done.10.rest_0_
  48.1 0.4 shard_map.34
  48.6 0.1 collective-permute-start.14
  48.7 0.2 pad_maximum_fusion
  48.9 0.5 collective-permute-start.11
  49.4 0.0 collective-permute-done.16
  49.4 0.1 add_convert_fusion
  49.5 1.6 %collective-permute-start.17 = (f16[512,256]{1,0:T(8,128)(2,1)S(1)}, f16[512,256]{1,0:T(8,128)(2,1)S(1)}, u32[]{:S(2)}, u32[]{:S(2)}) collective-permute-start(f16[512,256]{1,0:T(8,128)(2,1)S(1)} %add_convert_fusion), channel_id=1, source_target_pairs={{0,2},{1,3},{2,0},{3,1},{4,6},{5,7},{6,4},{7,5},{8,10},{9,11},{10,... | collective-permute-start | bytes 786440 | tf_op jit(solution)/shard_map/ppermute | solution.py:15
  51.1 0.0 collective-permute-done.14
  51.1 0.1 add_convert_fusion.1
  51.2 0.7 collective-permute-start.15
  51.9 0.0 collective-permute-done.12
  51.9 0.1 add_convert_fusion.2
  51.9 1.5 %collective-permute-start.13 = (f16[512,128]{1,0:T(8,128)(2,1)S(1)}, f16[512,128]{1,0:T(8,128)(2,1)S(1)}, u32[]{:S(2)}, u32[]{:S(2)}) collective-permute-start(f16[512,128]{1,0:T(8,128)(2,1)S(1)} %add_convert_fusion.2), channel_id=1, source_target_pairs={{0,2},{1,3},{2,0},{3,1},{4,6},{5,7},{6,4},{7,5},{8,10},{9,11},{10,... | collective-permute-start | bytes 393224 | tf_op jit(solution)/shard_map/ppermute | solution.py:15
  53.4 12.9 %collective-permute-done.13 = f16[512,128]{1,0:T(8,128)(2,1)S(1)} collective-permute-done((f16[512,128]{1,0:T(8,128)(2,1)S(1)}, f16[512,128]{1,0:T(8,128)(2,1)S(1)}, u32[]{:S(2)}, u32[]{:S(2)}) %collective-permute-start.13) | collective-permute-done | bytes 131104 | tf_op jit(solution)/shard_map/ppermute | solution.py:15
  66.3 0.0 collective-permute-done.17
  66.3 0.0 collective-permute-done.15
  66.4 0.0 collective-permute-done.11
  66.4 0.1 convert_add_fusion
  66.5 0.9 %shard_map.35.rest_0_ = f32[512,640]{1,0:T(8,128)} custom-call(f32[512,256]{1,0:T(8,128)S(1)} %get-tuple-element.65.ours_ref, f32[512,256]{1,0:T(8,128)S(1)} %convert_element_type.71.got_ref), custom_call_target="tpu_custom_call" | custom-call | flops 131072 | bytes 524288 | tf_op jit(solution)/shard_map/pallas_call | solution.py:40
  67.4 0.9 %shard_map.36.rest_0_ = f32[512,640]{1,0:T(8,128)} custom-call(f32[512,256]{1,0:T(8,128)S(1)} %get-tuple-element.66.ours_ref, f32[512,256]{1,0:T(8,128)S(1)} %convert_element_type.66.got_ref, f32[512,640]{1,0:T(8,128)} %shard_map.35.rest_0_), custom_call_target="tpu_custom_call", output_to_operand_aliasing={{}: (2, {})} | custom-call | flops 131072 | bytes 524288 | tf_op jit(solution)/shard_map/pallas_call | solution.py:40
  68.3 0.7 %shard_map.37 = f32[512,640]{1,0:T(8,128)} custom-call(f32[512,128]{1,0:T(8,128)S(1)} %convert_add_fusion.2.ours_ref, f32[512,128]{1,0:T(8,128)S(1)} %convert_element_type.61.got_ref, f32[512,640]{1,0:T(8,128)} %shard_map.36.rest_0_), custom_call_target="tpu_custom_call", output_to_operand_aliasing={{}: (2, {})} | custom-call | flops 65536 | bytes 262144 | tf_op jit(solution)/shard_map/pallas_call | solution.py:40
  (14 shorter events, 0.4 us)
Async XLA Ops:
  1.5 10.4 %collective-permute-start.3 = (bf16[256,384]{1,0:T(8,128)(2,1)S(1)}, bf16[256,384]{1,0:T(8,128)(2,1)S(1)}, u32[]{:S(2)}, u32[]{:S(2)}) collective-permute-start(bf16[256,384]{1,0:T(8,128)(2,1)S(1)} %get-tuple-element.39), channel_id=1, source_target_pairs={{0,24},{4,28},{8,0},{12,4},{16,8},{20,12},{24,16},{28,20},{1,25},{... | collective-permute-start | bytes 589832 | tf_op jit(solution)/shard_map/ppermute | solution.py:15
  6.6 11.1 %collective-permute-start.6 = (bf16[256,384]{1,0:T(8,128)(2,1)S(1)}, bf16[256,384]{1,0:T(8,128)(2,1)S(1)}, u32[]{:S(2)}, u32[]{:S(2)}) collective-permute-start(bf16[256,384]{1,0:T(8,128)(2,1)S(1)} %get-tuple-element.40), channel_id=1, source_target_pairs={{0,24},{4,28},{8,0},{12,4},{16,8},{20,12},{24,16},{28,20},{1,25},{... | collective-permute-start | bytes 589832 | tf_op jit(solution)/shard_map/ppermute | solution.py:15
  11.9 9.7 %collective-permute-start.4 = (bf16[256,384]{1,0:T(8,128)(2,1)S(1)}, bf16[256,384]{1,0:T(8,128)(2,1)S(1)}, u32[]{:S(2)}, u32[]{:S(2)}) collective-permute-start(bf16[256,384]{1,0:T(8,128)(2,1)S(1)} %collective-permute-done.3.rest_2_), channel_id=1, source_target_pairs={{0,24},{4,28},{8,0},{12,4},{16,8},{20,12},{24,16},{28,20},{1,25},{... | collective-permute-start | bytes 589832 | tf_op jit(solution)/shard_map/ppermute | solution.py:15
  16.2 28.5 %collective-permute-start.8 = (bf16[256,384]{1,0:T(8,128)(2,1)S(1)}, bf16[256,384]{1,0:T(8,128)(2,1)S(1)}, u32[]{:S(2)}, u32[]{:S(2)}) collective-permute-start(bf16[256,384]{1,0:T(8,128)(2,1)S(1)} %collective-permute-done.3.rest_2_), channel_id=1, source_target_pairs={{0,4},{4,0},{8,12},{12,8},{16,20},{20,16},{24,28},{28,24},{1,5},{5... | collective-permute-start | bytes 589832 | tf_op jit(solution)/shard_map/ppermute | solution.py:15
  17.7 5.9 %collective-permute-start.9 = (bf16[256,384]{1,0:T(8,128)(2,1)S(1)}, bf16[256,384]{1,0:T(8,128)(2,1)S(1)}, u32[]{:S(2)}, u32[]{:S(2)}) collective-permute-start(bf16[256,384]{1,0:T(8,128)(2,1)S(1)} %collective-permute-done.6.rest_1_), channel_id=1, source_target_pairs={{0,24},{4,28},{8,0},{12,4},{16,8},{20,12},{24,16},{28,20},{1,25},{... | collective-permute-start | bytes 589832 | tf_op jit(solution)/shard_map/ppermute | solution.py:15
  20.1 24.6 %collective-permute-start.7 = (bf16[256,384]{1,0:T(8,128)(2,1)S(1)}, bf16[256,384]{1,0:T(8,128)(2,1)S(1)}, u32[]{:S(2)}, u32[]{:S(2)}) collective-permute-start(bf16[256,384]{1,0:T(8,128)(2,1)S(1)} %collective-permute-done.6.rest_1_), channel_id=1, source_target_pairs={{0,4},{4,0},{8,12},{12,8},{16,20},{20,16},{24,28},{28,24},{1,5},{5... | collective-permute-start | bytes 589832 | tf_op jit(solution)/shard_map/ppermute | solution.py:15
  21.7 25.1 %collective-permute-start.5 = (bf16[256,384]{1,0:T(8,128)(2,1)S(1)}, bf16[256,384]{1,0:T(8,128)(2,1)S(1)}, u32[]{:S(2)}, u32[]{:S(2)}) collective-permute-start(bf16[256,384]{1,0:T(8,128)(2,1)S(1)} %broadcast_select_fusion.1), channel_id=1, source_target_pairs={{0,4},{4,0},{8,12},{12,8},{16,20},{20,16},{24,28},{28,24},{1,5},{5... | collective-permute-start | bytes 589832 | tf_op jit(solution)/shard_map/ppermute | solution.py:15
  23.6 24.4 %collective-permute-start.10 = (bf16[256,384]{1,0:T(8,128)(2,1)S(1)}, bf16[256,384]{1,0:T(8,128)(2,1)S(1)}, u32[]{:S(2)}, u32[]{:S(2)}) collective-permute-start(bf16[256,384]{1,0:T(8,128)(2,1)S(1)} %broadcast_select_fusion), channel_id=1, source_target_pairs={{0,4},{4,0},{8,12},{12,8},{16,20},{20,16},{24,28},{28,24},{1,5},{5... | collective-permute-start | bytes 589832 | tf_op jit(solution)/shard_map/ppermute | solution.py:15
  25.2 9.4 %collective-permute-start = (f32[2,384]{1,0:T(2,128)S(1)}, f32[2,384]{1,0:T(2,128)S(1)}, u32[]{:S(2)}, u32[]{:S(2)}) collective-permute-start(f32[2,384]{1,0:T(2,128)S(1)} %get-tuple-element.36), channel_id=1, source_target_pairs={{0,4},{4,0},{8,12},{12,8},{16,20},{20,16},{24,28},{28,24},{1,5},{5... | collective-permute-start | bytes 9224 | tf_op jit(solution)/shard_map/ppermute | solution.py:15
  34.6 3.6 %collective-permute-start.1 = (f32[2,384]{1,0:T(2,128)S(1)}, f32[2,384]{1,0:T(2,128)S(1)}, u32[]{:S(2)}, u32[]{:S(2)}) collective-permute-start(f32[2,384]{1,0:T(2,128)S(1)} %add.28), channel_id=1, source_target_pairs={{0,8},{4,12},{8,0},{12,4},{16,24},{20,28},{24,16},{28,20},{1,9},{5... | collective-permute-start | bytes 9224 | tf_op jit(solution)/shard_map/ppermute | solution.py:15
  38.2 4.5 %collective-permute-start.2 = (f32[2,384]{1,0:T(2,128)S(1)}, f32[2,384]{1,0:T(2,128)S(1)}, u32[]{:S(2)}, u32[]{:S(2)}) collective-permute-start(f32[2,384]{1,0:T(2,128)S(1)} %add.29.sums_ref), channel_id=1, source_target_pairs={{0,16},{4,20},{8,24},{12,28},{16,0},{20,4},{24,8},{28,12},{1,17},{... | collective-permute-start | bytes 9224 | tf_op jit(solution)/shard_map/ppermute | solution.py:15
  44.6 4.9 %collective-permute-start.16 = (f16[512,256]{1,0:T(8,128)(2,1)S(1)}, f16[512,256]{1,0:T(8,128)(2,1)S(1)}, u32[]{:S(2)}, u32[]{:S(2)}) collective-permute-start(f16[512,256]{1,0:T(8,128)(2,1)S(1)} %convert_element_type.68), channel_id=1, source_target_pairs={{0,1},{1,0},{2,3},{3,2},{4,5},{5,4},{6,7},{7,6},{8,9},{9,8},{10,11... | collective-permute-start | bytes 786440 | tf_op jit(solution)/shard_map/ppermute | solution.py:15
  47.5 4.3 %collective-permute-start.12 = (f16[512,128]{1,0:T(8,128)(2,1)S(1)}, f16[512,128]{1,0:T(8,128)(2,1)S(1)}, u32[]{:S(2)}, u32[]{:S(2)}) collective-permute-start(f16[512,128]{1,0:T(8,128)(2,1)S(1)} %convert_element_type.58), channel_id=1, source_target_pairs={{0,1},{1,0},{2,3},{3,2},{4,5},{5,4},{6,7},{7,6},{8,9},{9,8},{10,11... | collective-permute-start | bytes 393224 | tf_op jit(solution)/shard_map/ppermute | solution.py:15
  48.6 2.5 %collective-permute-start.14 = (f16[512,256]{1,0:T(8,128)(2,1)S(1)}, f16[512,256]{1,0:T(8,128)(2,1)S(1)}, u32[]{:S(2)}, u32[]{:S(2)}) collective-permute-start(f16[512,256]{1,0:T(8,128)(2,1)S(1)} %convert_element_type.63), channel_id=1, source_target_pairs={{0,1},{1,0},{2,3},{3,2},{4,5},{5,4},{6,7},{7,6},{8,9},{9,8},{10,11... | collective-permute-start | bytes 786440 | tf_op jit(solution)/shard_map/ppermute | solution.py:15
  48.9 17.5 %collective-permute-start.11 = (f16[512,640]{1,0:T(8,128)(2,1)S(1)}, f16[512,640]{1,0:T(8,128)(2,1)S(1)}, u32[]{:S(2)}, u32[]{:S(2)}) collective-permute-start(f16[512,640]{1,0:T(8,128)(2,1)S(1)} %pad_maximum_fusion), channel_id=1, source_target_pairs={{0,1},{1,0},{2,3},{3,2},{4,5},{5,4},{6,7},{7,6},{8,9},{9,8},{10,11... | collective-permute-start | bytes 1966088 | tf_op jit(solution)/shard_map/ppermute | solution.py:15
  49.5 16.8 %collective-permute-start.17 = (f16[512,256]{1,0:T(8,128)(2,1)S(1)}, f16[512,256]{1,0:T(8,128)(2,1)S(1)}, u32[]{:S(2)}, u32[]{:S(2)}) collective-permute-start(f16[512,256]{1,0:T(8,128)(2,1)S(1)} %add_convert_fusion), channel_id=1, source_target_pairs={{0,2},{1,3},{2,0},{3,1},{4,6},{5,7},{6,4},{7,5},{8,10},{9,11},{10,... | collective-permute-start | bytes 786440 | tf_op jit(solution)/shard_map/ppermute | solution.py:15
  51.2 15.2 %collective-permute-start.15 = (f16[512,256]{1,0:T(8,128)(2,1)S(1)}, f16[512,256]{1,0:T(8,128)(2,1)S(1)}, u32[]{:S(2)}, u32[]{:S(2)}) collective-permute-start(f16[512,256]{1,0:T(8,128)(2,1)S(1)} %add_convert_fusion.1), channel_id=1, source_target_pairs={{0,2},{1,3},{2,0},{3,1},{4,6},{5,7},{6,4},{7,5},{8,10},{9,11},{10,... | collective-permute-start | bytes 786440 | tf_op jit(solution)/shard_map/ppermute | solution.py:15
  51.9 14.3 %collective-permute-start.13 = (f16[512,128]{1,0:T(8,128)(2,1)S(1)}, f16[512,128]{1,0:T(8,128)(2,1)S(1)}, u32[]{:S(2)}, u32[]{:S(2)}) collective-permute-start(f16[512,128]{1,0:T(8,128)(2,1)S(1)} %add_convert_fusion.2), channel_id=1, source_target_pairs={{0,2},{1,3},{2,0},{3,1},{4,6},{5,7},{6,4},{7,5},{8,10},{9,11},{10,... | collective-permute-start | bytes 393224 | tf_op jit(solution)/shard_map/ppermute | solution.py:15

commit v7 on v6

--- a/solution.py
+++ b/solution.py
@@ -149,9 +149,10 @@
     products_body(cases, down, left_ref, factors_ref, *rest[:-9], *rest[-5:])
 
 
-def add_body(places, up, ours_ref, got_ref, *rest):
+def add_body(places, at, up, ours_ref, got_ref, other_ref, *rest):
     out_ref, total_ref, sem = rest[-3:]
-    total_ref[...] = (ours_ref[...] + got_ref[...]) * up
+    other = other_ref[:, pl.ds(at, total_ref.shape[1])]
+    total_ref[...] = (ours_ref[...] + other + got_ref[...]) * up
     device = lax.axis_index("snps")
     width = total_ref.shape[1]
     for strip, begin in enumerate(places):
@@ -255,11 +256,7 @@
         theirs = (neighbour + other.astype(jnp.float32)).astype(jnp.float16)
         pieces.append((own, send(theirs, "snps", lambda s: s ^ 2)))
         partners.append(own_away.astype(jnp.float16))
-    other = swap_core(jnp.concatenate(partners, axis=1))
-    for n, (keep, got) in enumerate(pieces):
-        begin = n * half_rows
-        ours = keep + other[:, begin : begin + keep.shape[1]].astype(jnp.float32)
-        pieces[n] = (ours, got.astype(jnp.float32))
+    other = swap_core(jnp.concatenate(partners, axis=1)).astype(jnp.float32)
     out = None
     for n, operands in enumerate(pieces):
         places = []
@@ -268,13 +265,14 @@
                 places.append(natural.index(by_arrival[n]) * half_rows + (strip % 2) * quarter)
             else:
                 places.append(0 if strip % 2 else count * half_rows)
-        columns = operands[1].shape[1]
+        ours, got = operands
+        columns = got.shape[1]
         last = () if out is None else (out,)
-        operands = (*operands, *last)
+        operands = (ours, got.astype(jnp.float32), other, *last)
         out = call_kernel(
-            functools.partial(add_body, tuple(places), 1.0 / (down * snp_total)),
+            functools.partial(add_body, tuple(places), n * half_rows, 1.0 / (down * snp_total)),
             jax.ShapeDtypeStruct((rows, width), jnp.float32), operands,
-            [VMEM] * 2 + [ANY] * len(last), rows * columns, 4 * rows * columns,
+            [VMEM] * 3 + [ANY] * len(last), rows * columns, 4 * rows * columns,
             out_specs=ANY,
             scratch_shapes=[pltpu.VMEM((rows, columns), jnp.float32), pltpu.SemaphoreType.DMA],
             input_output_aliases={len(operands) - 1: 0} if last else {},

time: 69.4 us -> 69.3 us (level)
  no operation moved by 1% of the time
where the time goes in v7:
time: 69.3 us; the launch traced here: 69.2 us
  waiting for transfers between devices  36 us (52%)
  starting transfers between devices  23 us (33%)
  Pallas kernels  8.95 us (13%)
  other arithmetic  0.84 us (1%)
    ppermute x18, waiting for transfers between devices, send(): lax.ppermute(value, axis, [pair for pair in pairs if pair[1] is not None])  36 us
    ppermute x18, starting transfers between devices, send(): lax.ppermute(value, axis, [pair for pair in pairs if pair[1] is not None])  23 us
    pallas_call x10, Pallas kernels, call_kernel(): pl.pallas_call(body, out_shape=shapes, in_specs=specs, compiler_params=pl...  7.46 us
    pallas_call x1, Pallas kernels, encode(): pl.pallas_call(encode_body, name='encode', out_shape=(calls(rows), calls(...  1.49 us
  transfers between devices with their start and end apart: 18, of which 6 were waited for; matrix products, arithmetic and copies ran while one was open for 1% of the time, Pallas kernels for 7%

profile of v7, /device:TPU:0, one launch (start us, length us, event | category | flops | bytes accessed | tf_op | source)
XLA Modules:
  0.0 69.2 jit_solution(1711792344213098215)
XLA Ops:
  0.0 1.5 %encode.1 = (bf16[512,384]{1,0:T(8,128)(2,1)S(1)}, bf16[256,384]{1,0:T(8,128)(2,1)S(1)}, bf16[256,384]{1,0:T(8,128)(2,1)S(1)}, f32[2,384]{1,0:T(2,128)S(1)}) custom-call(s32[512,384]{1,0:T(8,128)} %genotype_ref.1, s32[512,384]{1,0:T(8,128)} %mask_ref.1), custom_call_target="tpu_custom_call" | custom-call | tf_op jit(solution)/shard_map/encode/pallas_call | solution.py:87
  1.5 5.1 %collective-permute-start.3 = (bf16[256,384]{1,0:T(8,128)(2,1)S(1)}, bf16[256,384]{1,0:T(8,128)(2,1)S(1)}, u32[]{:S(2)}, u32[]{:S(2)}) collective-permute-start(bf16[256,384]{1,0:T(8,128)(2,1)S(1)} %get-tuple-element.39), channel_id=1, source_target_pairs={{0,24},{4,28},{8,0},{12,4},{16,8},{20,12},{24,16},{28,20},{1,25},{... | collective-permute-start | bytes 589832 | tf_op jit(solution)/shard_map/ppermute | solution.py:15
  6.6 0.4 collective-permute-start.6
  7.1 4.8 %collective-permute-done.3.rest_2_ = bf16[256,384]{1,0:T(8,128)(2,1)S(1)} collective-permute-done((bf16[256,384]{1,0:T(8,128)(2,1)S(1)}, bf16[256,384]{1,0:T(8,128)(2,1)S(1)}, u32[]{:S(2)}, u32[]{:S(2)}) %collective-permute-start.3) | collective-permute-done | bytes 196640 | tf_op jit(solution)/shard_map/ppermute | solution.py:15
  11.9 4.3 %collective-permute-start.4 = (bf16[256,384]{1,0:T(8,128)(2,1)S(1)}, bf16[256,384]{1,0:T(8,128)(2,1)S(1)}, u32[]{:S(2)}, u32[]{:S(2)}) collective-permute-start(bf16[256,384]{1,0:T(8,128)(2,1)S(1)} %collective-permute-done.3.rest_2_), channel_id=1, source_target_pairs={{0,24},{4,28},{8,0},{12,4},{16,8},{20,12},{24,16},{28,20},{1,25},{... | collective-permute-start | bytes 589832 | tf_op jit(solution)/shard_map/ppermute | solution.py:15
  16.2 1.5 %collective-permute-start.8 = (bf16[256,384]{1,0:T(8,128)(2,1)S(1)}, bf16[256,384]{1,0:T(8,128)(2,1)S(1)}, u32[]{:S(2)}, u32[]{:S(2)}) collective-permute-start(bf16[256,384]{1,0:T(8,128)(2,1)S(1)} %collective-permute-done.3.rest_2_), channel_id=1, source_target_pairs={{0,4},{4,0},{8,12},{12,8},{16,20},{20,16},{24,28},{28,24},{1,5},{5... | collective-permute-start | bytes 589832 | tf_op jit(solution)/shard_map/ppermute | solution.py:15
  17.7 0.0 collective-permute-done.6.rest_1_
  17.7 2.4 %collective-permute-start.11 = (bf16[256,384]{1,0:T(8,128)(2,1)S(1)}, bf16[256,384]{1,0:T(8,128)(2,1)S(1)}, u32[]{:S(2)}, u32[]{:S(2)}) collective-permute-start(bf16[256,384]{1,0:T(8,128)(2,1)S(1)} %collective-permute-done.6.rest_1_), channel_id=1, source_target_pairs={{0,24},{4,28},{8,0},{12,4},{16,8},{20,12},{24,16},{28,20},{1,25},{... | collective-permute-start | bytes 589832 | tf_op jit(solution)/shard_map/ppermute | solution.py:15
  20.1 1.5 %collective-permute-start.7 = (bf16[256,384]{1,0:T(8,128)(2,1)S(1)}, bf16[256,384]{1,0:T(8,128)(2,1)S(1)}, u32[]{:S(2)}, u32[]{:S(2)}) collective-permute-start(bf16[256,384]{1,0:T(8,128)(2,1)S(1)} %collective-permute-done.6.rest_1_), channel_id=1, source_target_pairs={{0,4},{4,0},{8,12},{12,8},{16,20},{20,16},{24,28},{28,24},{1,5},{5... | collective-permute-start | bytes 589832 | tf_op jit(solution)/shard_map/ppermute | solution.py:15
  21.6 0.0 collective-permute-done.4.rest_3_
  21.7 0.6 collective-permute-start.5
  22.2 1.4 %collective-permute-done.11.rest_0_ = bf16[256,384]{1,0:T(8,128)(2,1)S(1)} collective-permute-done((bf16[256,384]{1,0:T(8,128)(2,1)S(1)}, bf16[256,384]{1,0:T(8,128)(2,1)S(1)}, u32[]{:S(2)}, u32[]{:S(2)}) %collective-permute-start.11) | collective-permute-done | bytes 196640 | tf_op jit(solution)/shard_map/ppermute | solution.py:15
  23.6 1.6 %collective-permute-start.12 = (bf16[256,384]{1,0:T(8,128)(2,1)S(1)}, bf16[256,384]{1,0:T(8,128)(2,1)S(1)}, u32[]{:S(2)}, u32[]{:S(2)}) collective-permute-start(bf16[256,384]{1,0:T(8,128)(2,1)S(1)} %broadcast_select_fusion), channel_id=1, source_target_pairs={{0,4},{4,0},{8,12},{12,8},{16,20},{20,16},{24,28},{28,24},{1,5},{5... | collective-permute-start | bytes 589832 | tf_op jit(solution)/shard_map/ppermute | solution.py:15
  25.2 0.5 collective-permute-start
  25.7 8.9 %collective-permute-done = f32[2,384]{1,0:T(2,128)S(1)} collective-permute-done((f32[2,384]{1,0:T(2,128)S(1)}, f32[2,384]{1,0:T(2,128)S(1)}, u32[]{:S(2)}, u32[]{:S(2)}) %collective-permute-start) | collective-permute-done | bytes 3104 | tf_op jit(solution)/shard_map/ppermute | solution.py:15
  34.6 0.0 collective-permute-start.1
  34.6 3.6 %collective-permute-done.1 = f32[2,384]{1,0:T(2,128)S(1)} collective-permute-done((f32[2,384]{1,0:T(2,128)S(1)}, f32[2,384]{1,0:T(2,128)S(1)}, u32[]{:S(2)}, u32[]{:S(2)}) %collective-permute-start.1) | collective-permute-done | bytes 3104 | tf_op jit(solution)/shard_map/ppermute | solution.py:15
  38.2 0.0 collective-permute-start.2
  38.2 4.5 %collective-permute-done.2.more_ref = f32[2,384]{1,0:T(2,128)S(1)} collective-permute-done((f32[2,384]{1,0:T(2,128)S(1)}, f32[2,384]{1,0:T(2,128)S(1)}, u32[]{:S(2)}, u32[]{:S(2)}) %collective-permute-start.2) | collective-permute-done | bytes 3104 | tf_op jit(solution)/shard_map/ppermute | solution.py:15
  42.7 0.2 shard_map.28
  42.9 1.2 %shard_map.31 = (f32[512,256]{1,0:T(8,128)S(1)}, f32[512,256]{1,0:T(8,128)S(1)}, f32[512,256]{1,0:T(8,128)S(1)}, f32[512,256]{1,0:T(8,128)S(1)}) custom-call(bf16[512,384]{1,0:T(8,128)(2,1)S(1)} %get-tuple-element.37.left_ref, f32[2,384]{1,0:T(2,128)S(1)} %get-tuple-element.38.factors_ref, bf16[512,384]{1,0:T(8,128)(2,1)S(1)} %get-tuple-element.35.calls_ref.rest_0_, ...), custom_call_target="tpu_custom_call" | custom-call | flops 301989888 | bytes 524288 | tf_op jit(solution)/shard_map/pallas_call | solution.py:40
  44.1 0.4 shard_map.32
  44.6 0.1 collective-permute-start.16
  44.7 0.0 collective-permute-done.8.rest_1_
  44.7 0.0 collective-permute-done.7.rest_0_.rest_2_
  44.7 0.7 shard_map.29
  45.4 1.4 %shard_map.33 = (f32[512,256]{1,0:T(8,128)S(1)}, f32[512,256]{1,0:T(8,128)S(1)}, f32[512,256]{1,0:T(8,128)S(1)}, f32[512,256]{1,0:T(8,128)S(1)}) custom-call(bf16[512,384]{1,0:T(8,128)(2,1)S(1)} %get-tuple-element.37.left_ref, f32[2,384]{1,0:T(2,128)S(1)} %get-tuple-element.38.factors_ref, bf16[512,384]{1,0:T(8,128)(2,1)S(1)} %get-tuple-element.35.calls_ref.rest_0_, ...), custom_call_target="tpu_custom_call" | custom-call | flops 402653184 | bytes 524288 | tf_op jit(solution)/shard_map/pallas_call | solution.py:40
  46.8 0.0 collective-permute-done.5.rest_0_
  46.8 0.7 shard_map.30
  47.5 0.6 collective-permute-start.9
  48.1 0.0 collective-permute-done.12.rest_0_
  48.1 0.4 shard_map.34
  48.6 0.1 collective-permute-start.14
  48.7 0.2 pad_maximum_fusion
  48.9 0.5 collective-permute-start.13
  49.4 0.0 collective-permute-done.16
  49.4 0.1 add_convert_fusion
  49.5 1.6 %collective-permute-start.17 = (f16[512,256]{1,0:T(8,128)(2,1)S(1)}, f16[512,256]{1,0:T(8,128)(2,1)S(1)}, u32[]{:S(2)}, u32[]{:S(2)}) collective-permute-start(f16[512,256]{1,0:T(8,128)(2,1)S(1)} %add_convert_fusion), channel_id=1, source_target_pairs={{0,2},{1,3},{2,0},{3,1},{4,6},{5,7},{6,4},{7,5},{8,10},{9,11},{10,... | collective-permute-start | bytes 786440 | tf_op jit(solution)/shard_map/ppermute | solution.py:15
  51.1 0.0 collective-permute-done.14
  51.1 0.1 add_convert_fusion.1
  51.2 0.7 collective-permute-start.15
  51.9 0.0 collective-permute-done.9
  51.9 1.5 %collective-permute-start.10 = (f16[512,128]{1,0:T(8,128)(2,1)S(1)}, f16[512,128]{1,0:T(8,128)(2,1)S(1)}, u32[]{:S(2)}, u32[]{:S(2)}) collective-permute-start(f16[512,128]{1,0:T(8,128)(2,1)S(1)} %add_convert_fusion.2), channel_id=1, source_target_pairs={{0,2},{1,3},{2,0},{3,1},{4,6},{5,7},{6,4},{7,5},{8,10},{9,11},{10,... | collective-permute-start | bytes 393224 | tf_op jit(solution)/shard_map/ppermute | solution.py:15
  53.4 12.9 %collective-permute-done.10 = f16[512,128]{1,0:T(8,128)(2,1)S(1)} collective-permute-done((f16[512,128]{1,0:T(8,128)(2,1)S(1)}, f16[512,128]{1,0:T(8,128)(2,1)S(1)}, u32[]{:S(2)}, u32[]{:S(2)}) %collective-permute-start.10) | collective-permute-done | bytes 131104 | tf_op jit(solution)/shard_map/ppermute | solution.py:15
  66.3 0.0 collective-permute-done.17
  66.3 0.0 collective-permute-done.15
  66.4 0.0 collective-permute-done.13
  66.4 0.1 convert_element_type.55.other_ref
  66.5 0.9 %shard_map.35.rest_0_ = f32[512,640]{1,0:T(8,128)} custom-call(f32[512,256]{1,0:T(8,128)S(1)} %get-tuple-element.62.ours_ref, f32[512,256]{1,0:T(8,128)S(1)} %convert_element_type.63.got_ref, f32[512,640]{1,0:T(8,128)S(1)} %convert_element_type.55.other_ref), custom_call_target="tpu_custom_call" | custom-call | flops 131072 | bytes 524288 | tf_op jit(solution)/shard_map/pallas_call | solution.py:40
  67.4 0.9 %shard_map.36.rest_0_ = f32[512,640]{1,0:T(8,128)} custom-call(f32[512,256]{1,0:T(8,128)S(1)} %get-tuple-element.59.ours_ref, f32[512,256]{1,0:T(8,128)S(1)} %convert_element_type.59.got_ref, f32[512,640]{1,0:T(8,128)S(1)} %convert_element_type.55.other_ref, f32[512,640]{1,0:T(8,128)} %shard_map.35.rest_0_), custom_call_target="tpu_custom_call", output_to_operand_aliasing={{}: (3, {})} | custom-call | flops 131072 | bytes 524288 | tf_op jit(solution)/shard_map/pallas_call | solution.py:40
  68.3 0.8 %shard_map.37 = f32[512,640]{1,0:T(8,128)} custom-call(f32[512,128]{1,0:T(8,128)S(1)} %get-tuple-element.45.ours_ref, f32[512,128]{1,0:T(8,128)S(1)} %convert_element_type.51.got_ref, f32[512,640]{1,0:T(8,128)S(1)} %convert_element_type.55.other_ref, f32[512,640]{1,0:T(8,128)} %shard_map.36.rest_0_), custom_call_target="tpu_custom_call", output_to_operand_aliasing={{}: (3, {})} | custom-call | flops 65536 | bytes 262144 | tf_op jit(solution)/shard_map/pallas_call | solution.py:40
  (14 shorter events, 0.4 us)
Async XLA Ops:
  1.5 10.4 %collective-permute-start.3 = (bf16[256,384]{1,0:T(8,128)(2,1)S(1)}, bf16[256,384]{1,0:T(8,128)(2,1)S(1)}, u32[]{:S(2)}, u32[]{:S(2)}) collective-permute-start(bf16[256,384]{1,0:T(8,128)(2,1)S(1)} %get-tuple-element.39), channel_id=1, source_target_pairs={{0,24},{4,28},{8,0},{12,4},{16,8},{20,12},{24,16},{28,20},{1,25},{... | collective-permute-start | bytes 589832 | tf_op jit(solution)/shard_map/ppermute | solution.py:15
  6.6 11.1 %collective-permute-start.6 = (bf16[256,384]{1,0:T(8,128)(2,1)S(1)}, bf16[256,384]{1,0:T(8,128)(2,1)S(1)}, u32[]{:S(2)}, u32[]{:S(2)}) collective-permute-start(bf16[256,384]{1,0:T(8,128)(2,1)S(1)} %get-tuple-element.40), channel_id=1, source_target_pairs={{0,24},{4,28},{8,0},{12,4},{16,8},{20,12},{24,16},{28,20},{1,25},{... | collective-permute-start | bytes 589832 | tf_op jit(solution)/shard_map/ppermute | solution.py:15
  11.9 9.7 %collective-permute-start.4 = (bf16[256,384]{1,0:T(8,128)(2,1)S(1)}, bf16[256,384]{1,0:T(8,128)(2,1)S(1)}, u32[]{:S(2)}, u32[]{:S(2)}) collective-permute-start(bf16[256,384]{1,0:T(8,128)(2,1)S(1)} %collective-permute-done.3.rest_2_), channel_id=1, source_target_pairs={{0,24},{4,28},{8,0},{12,4},{16,8},{20,12},{24,16},{28,20},{1,25},{... | collective-permute-start | bytes 589832 | tf_op jit(solution)/shard_map/ppermute | solution.py:15
  16.2 28.5 %collective-permute-start.8 = (bf16[256,384]{1,0:T(8,128)(2,1)S(1)}, bf16[256,384]{1,0:T(8,128)(2,1)S(1)}, u32[]{:S(2)}, u32[]{:S(2)}) collective-permute-start(bf16[256,384]{1,0:T(8,128)(2,1)S(1)} %collective-permute-done.3.rest_2_), channel_id=1, source_target_pairs={{0,4},{4,0},{8,12},{12,8},{16,20},{20,16},{24,28},{28,24},{1,5},{5... | collective-permute-start | bytes 589832 | tf_op jit(solution)/shard_map/ppermute | solution.py:15
  17.7 5.9 %collective-permute-start.11 = (bf16[256,384]{1,0:T(8,128)(2,1)S(1)}, bf16[256,384]{1,0:T(8,128)(2,1)S(1)}, u32[]{:S(2)}, u32[]{:S(2)}) collective-permute-start(bf16[256,384]{1,0:T(8,128)(2,1)S(1)} %collective-permute-done.6.rest_1_), channel_id=1, source_target_pairs={{0,24},{4,28},{8,0},{12,4},{16,8},{20,12},{24,16},{28,20},{1,25},{... | collective-permute-start | bytes 589832 | tf_op jit(solution)/shard_map/ppermute | solution.py:15
  20.1 24.6 %collective-permute-start.7 = (bf16[256,384]{1,0:T(8,128)(2,1)S(1)}, bf16[256,384]{1,0:T(8,128)(2,1)S(1)}, u32[]{:S(2)}, u32[]{:S(2)}) collective-permute-start(bf16[256,384]{1,0:T(8,128)(2,1)S(1)} %collective-permute-done.6.rest_1_), channel_id=1, source_target_pairs={{0,4},{4,0},{8,12},{12,8},{16,20},{20,16},{24,28},{28,24},{1,5},{5... | collective-permute-start | bytes 589832 | tf_op jit(solution)/shard_map/ppermute | solution.py:15
  21.7 25.1 %collective-permute-start.5 = (bf16[256,384]{1,0:T(8,128)(2,1)S(1)}, bf16[256,384]{1,0:T(8,128)(2,1)S(1)}, u32[]{:S(2)}, u32[]{:S(2)}) collective-permute-start(bf16[256,384]{1,0:T(8,128)(2,1)S(1)} %broadcast_select_fusion.1), channel_id=1, source_target_pairs={{0,4},{4,0},{8,12},{12,8},{16,20},{20,16},{24,28},{28,24},{1,5},{5... | collective-permute-start | bytes 589832 | tf_op jit(solution)/shard_map/ppermute | solution.py:15
  23.6 24.4 %collective-permute-start.12 = (bf16[256,384]{1,0:T(8,128)(2,1)S(1)}, bf16[256,384]{1,0:T(8,128)(2,1)S(1)}, u32[]{:S(2)}, u32[]{:S(2)}) collective-permute-start(bf16[256,384]{1,0:T(8,128)(2,1)S(1)} %broadcast_select_fusion), channel_id=1, source_target_pairs={{0,4},{4,0},{8,12},{12,8},{16,20},{20,16},{24,28},{28,24},{1,5},{5... | collective-permute-start | bytes 589832 | tf_op jit(solution)/shard_map/ppermute | solution.py:15
  25.2 9.4 %collective-permute-start = (f32[2,384]{1,0:T(2,128)S(1)}, f32[2,384]{1,0:T(2,128)S(1)}, u32[]{:S(2)}, u32[]{:S(2)}) collective-permute-start(f32[2,384]{1,0:T(2,128)S(1)} %get-tuple-element.36), channel_id=1, source_target_pairs={{0,4},{4,0},{8,12},{12,8},{16,20},{20,16},{24,28},{28,24},{1,5},{5... | collective-permute-start | bytes 9224 | tf_op jit(solution)/shard_map/ppermute | solution.py:15
  34.6 3.6 %collective-permute-start.1 = (f32[2,384]{1,0:T(2,128)S(1)}, f32[2,384]{1,0:T(2,128)S(1)}, u32[]{:S(2)}, u32[]{:S(2)}) collective-permute-start(f32[2,384]{1,0:T(2,128)S(1)} %add.19), channel_id=1, source_target_pairs={{0,8},{4,12},{8,0},{12,4},{16,24},{20,28},{24,16},{28,20},{1,9},{5... | collective-permute-start | bytes 9224 | tf_op jit(solution)/shard_map/ppermute | solution.py:15
  38.2 4.5 %collective-permute-start.2 = (f32[2,384]{1,0:T(2,128)S(1)}, f32[2,384]{1,0:T(2,128)S(1)}, u32[]{:S(2)}, u32[]{:S(2)}) collective-permute-start(f32[2,384]{1,0:T(2,128)S(1)} %add.20.sums_ref), channel_id=1, source_target_pairs={{0,16},{4,20},{8,24},{12,28},{16,0},{20,4},{24,8},{28,12},{1,17},{... | collective-permute-start | bytes 9224 | tf_op jit(solution)/shard_map/ppermute | solution.py:15
  44.6 4.9 %collective-permute-start.16 = (f16[512,256]{1,0:T(8,128)(2,1)S(1)}, f16[512,256]{1,0:T(8,128)(2,1)S(1)}, u32[]{:S(2)}, u32[]{:S(2)}) collective-permute-start(f16[512,256]{1,0:T(8,128)(2,1)S(1)} %convert_element_type.60), channel_id=1, source_target_pairs={{0,1},{1,0},{2,3},{3,2},{4,5},{5,4},{6,7},{7,6},{8,9},{9,8},{10,11... | collective-permute-start | bytes 786440 | tf_op jit(solution)/shard_map/ppermute | solution.py:15
  47.5 4.3 %collective-permute-start.9 = (f16[512,128]{1,0:T(8,128)(2,1)S(1)}, f16[512,128]{1,0:T(8,128)(2,1)S(1)}, u32[]{:S(2)}, u32[]{:S(2)}) collective-permute-start(f16[512,128]{1,0:T(8,128)(2,1)S(1)} %convert_element_type.48), channel_id=1, source_target_pairs={{0,1},{1,0},{2,3},{3,2},{4,5},{5,4},{6,7},{7,6},{8,9},{9,8},{10,11... | collective-permute-start | bytes 393224 | tf_op jit(solution)/shard_map/ppermute | solution.py:15
  48.6 2.5 %collective-permute-start.14 = (f16[512,256]{1,0:T(8,128)(2,1)S(1)}, f16[512,256]{1,0:T(8,128)(2,1)S(1)}, u32[]{:S(2)}, u32[]{:S(2)}) collective-permute-start(f16[512,256]{1,0:T(8,128)(2,1)S(1)} %convert_element_type.56), channel_id=1, source_target_pairs={{0,1},{1,0},{2,3},{3,2},{4,5},{5,4},{6,7},{7,6},{8,9},{9,8},{10,11... | collective-permute-start | bytes 786440 | tf_op jit(solution)/shard_map/ppermute | solution.py:15
  48.9 17.5 %collective-permute-start.13 = (f16[512,640]{1,0:T(8,128)(2,1)S(1)}, f16[512,640]{1,0:T(8,128)(2,1)S(1)}, u32[]{:S(2)}, u32[]{:S(2)}) collective-permute-start(f16[512,640]{1,0:T(8,128)(2,1)S(1)} %pad_maximum_fusion), channel_id=1, source_target_pairs={{0,1},{1,0},{2,3},{3,2},{4,5},{5,4},{6,7},{7,6},{8,9},{9,8},{10,11... | collective-permute-start | bytes 1966088 | tf_op jit(solution)/shard_map/ppermute | solution.py:15
  49.5 16.8 %collective-permute-start.17 = (f16[512,256]{1,0:T(8,128)(2,1)S(1)}, f16[512,256]{1,0:T(8,128)(2,1)S(1)}, u32[]{:S(2)}, u32[]{:S(2)}) collective-permute-start(f16[512,256]{1,0:T(8,128)(2,1)S(1)} %add_convert_fusion), channel_id=1, source_target_pairs={{0,2},{1,3},{2,0},{3,1},{4,6},{5,7},{6,4},{7,5},{8,10},{9,11},{10,... | collective-permute-start | bytes 786440 | tf_op jit(solution)/shard_map/ppermute | solution.py:15
  51.2 15.2 %collective-permute-start.15 = (f16[512,256]{1,0:T(8,128)(2,1)S(1)}, f16[512,256]{1,0:T(8,128)(2,1)S(1)}, u32[]{:S(2)}, u32[]{:S(2)}) collective-permute-start(f16[512,256]{1,0:T(8,128)(2,1)S(1)} %add_convert_fusion.1), channel_id=1, source_target_pairs={{0,2},{1,3},{2,0},{3,1},{4,6},{5,7},{6,4},{7,5},{8,10},{9,11},{10,... | collective-permute-start | bytes 786440 | tf_op jit(solution)/shard_map/ppermute | solution.py:15
  51.9 14.4 %collective-permute-start.10 = (f16[512,128]{1,0:T(8,128)(2,1)S(1)}, f16[512,128]{1,0:T(8,128)(2,1)S(1)}, u32[]{:S(2)}, u32[]{:S(2)}) collective-permute-start(f16[512,128]{1,0:T(8,128)(2,1)S(1)} %add_convert_fusion.2), channel_id=1, source_target_pairs={{0,2},{1,3},{2,0},{3,1},{4,6},{5,7},{6,4},{7,5},{8,10},{9,11},{10,... | collective-permute-start | bytes 393224 | tf_op jit(solution)/shard_map/ppermute | solution.py:15

commit v8 on v7

--- a/solution.py
+++ b/solution.py
@@ -109,11 +109,11 @@
     return jnp.where(wide > 0.0, (wide - shift) * scale, 0.0).astype(jnp.bfloat16)
 
 
-def left_body(calls_ref, sums_ref, more_ref, left_ref, factors_ref):
+def left_body(down, calls_ref, sums_ref, more_ref, left_ref, factors_ref):
     shift, scale = factors(sums_ref[...] + more_ref[...])
     factors_ref[0:1, :] = shift
     factors_ref[1:2, :] = scale
-    left_ref[...] = standardized(calls_ref[...], shift, scale)
+    left_ref[...] = standardized(calls_ref[...], shift, scale) * down
 
 
 def multiply(left, right):
@@ -122,31 +122,31 @@
     )
 
 
-def products_body(cases, down, left_ref, factors_ref, *rest):
+def products_body(cases, left_ref, factors_ref, *rest):
     refs, target_refs, right_ref = rest[:-5], rest[-5:-1], rest[-1]
     shift, scale = factors_ref[0:1, :], factors_ref[1:2, :]
-    device = lax.axis_index("snps")
     parity = lax.axis_index("samples") % 2
-    for strip, at, begin, only in cases:
-
-        def work(strip=strip, at=at, begin=begin):
-            rows = refs[at][pl.ds(begin, right_ref.shape[0]), :]
-            right_ref[...] = standardized(rows, shift, scale)
-            place = device ^ strip
-            for index, target_ref in enumerate(target_refs):
-
-                @pl.when(place == index)
-                def _(target_ref=target_ref):
-                    target_ref[...] = multiply(left_ref[...], right_ref[...]) * down
-
-        if only is None:
-            work()
-        else:
-            pl.when(parity == only)(work)
-
-
-def products_more_body(cases, down, left_ref, factors_ref, *rest):
-    products_body(cases, down, left_ref, factors_ref, *rest[:-9], *rest[-5:])
+    columns = right_ref.shape[1]
+
+    def work(device, only):
+        for n, (strip, at, begin, wanted) in enumerate(cases):
+            if wanted == only:
+                right_ref[n] = standardized(refs[at][pl.ds(begin, columns), :], shift, scale)
+                target_refs[device ^ strip][...] = multiply(left_ref[...], right_ref[n])
+
+    for device in range(len(target_refs)):
+
+        @pl.when(lax.axis_index("snps") == device)
+        def _(device=device):
+            kinds = {wanted for *_, wanted in cases}
+            if None in kinds:
+                work(device, None)
+            for odd in sorted(kinds - {None}):
+                pl.when(parity == odd)(functools.partial(work, device, odd))
+
+
+def products_more_body(cases, left_ref, factors_ref, *rest):
+    products_body(cases, left_ref, factors_ref, *rest[:-9], *rest[-5:])
 
 
 def add_body(places, at, up, ours_ref, got_ref, other_ref, *rest):
@@ -181,7 +181,10 @@
     line = [[first, second]]
     for _ in range(1, turns + 1):
         line.append([send(line[-1][h], "samples", along) for h in range(2)])
-    side = [None] + [[send(line[t][h], "samples", lambda s: s ^ 1) for h in range(2)] for t in range(1, turns)]
+    side = [None] + [
+        [send(line[t][h], "samples", lambda s: s ^ 1) for h in range(2)]
+        for t in range(1, turns)
+    ]
     side.append([])
     for h in range(2):
         chosen = jnp.where(even, line[turns][h], line[0][1 - h])
@@ -201,14 +204,14 @@
             return side[turns][1 - h], 0
         return side[(k + odd) // 2][h], 0
 
+    table = strips(samples)
+    bound = snp_total / 2 * 4 * (samples * rows + 1) / 3
+    down = 2.0 ** -math.ceil(math.log2(bound / 32768.0))
     left, pair = call_kernel(
-        left_body,
+        functools.partial(left_body, down),
         (jax.ShapeDtypeStruct((rows, snp_part), jnp.bfloat16), jax.ShapeDtypeStruct((2, snp_part), jnp.float32)),
         (calls, sums, more), [VMEM] * 3, 5 * rows * snp_part, 4 * rows * snp_part, out_specs=(VMEM, VMEM),
     )
-    table = strips(samples)
-    bound = snp_total / 2 * 4 * (samples * rows + 1) / 3
-    down = 2.0 ** -math.ceil(math.log2(bound / 32768.0))
     count = len(table[0][0])
     quarter = half_rows // 2
 
@@ -235,11 +238,11 @@
         shape = jax.ShapeDtypeStruct((rows, columns), jnp.float32)
         operands = (left, pair, *arrays, *so_far)
         return call_kernel(
-            functools.partial(products_body if not so_far else products_more_body, tuple(cases), down),
+            functools.partial(products_body if not so_far else products_more_body, tuple(cases)),
             (shape,) * 4, operands, [VMEM] * len(operands),
             2 * rows * snp_part * columns * len(chosen), 4 * rows * columns,
             out_specs=(VMEM,) * 4,
-            scratch_shapes=[pltpu.VMEM((columns, snp_part), jnp.bfloat16)],
+            scratch_shapes=[pltpu.VMEM((len(cases), columns, snp_part), jnp.bfloat16)],
             input_output_aliases={len(operands) - 4 + i: i for i in range(len(so_far))},
         )
 

time: 69.3 us -> 67.9 us (0.980)
  Pallas kernels: 8.95 us -> 7.53 us
    pallas_call x10, Pallas kernels: 7.46 us -> 6.04 us  [call_kernel(): pl.pallas_call(body, out_shape=shapes, in_specs=specs, compiler_params=pl...]
  transfers between devices with their start and end apart: 18 -> 18, of which waited for: 6 -> 6; matrix products, arithmetic and copies ran while one was open for 1% -> 1% of each run, Pallas kernels for 7% -> 5%
where the time goes in v8:
time: 67.9 us; the launch traced here: 67.8 us
  waiting for transfers between devices  36 us (53%)
  starting transfers between devices  22.9 us (34%)
  Pallas kernels  7.53 us (11%)
  other arithmetic  0.84 us (1%)
    ppermute x18, waiting for transfers between devices, send(): lax.ppermute(value, axis, [pair for pair in pairs if pair[1] is not None])  36 us
    ppermute x18, starting transfers between devices, send(): lax.ppermute(value, axis, [pair for pair in pairs if pair[1] is not None])  22.9 us
    pallas_call x10, Pallas kernels, call_kernel(): pl.pallas_call(body, out_shape=shapes, in_specs=specs, compiler_params=pl...  6.04 us
    pallas_call x1, Pallas kernels, encode(): pl.pallas_call(encode_body, name='encode', out_shape=(calls(rows), calls(...  1.49 us
  transfers between devices with their start and end apart: 18, of which 6 were waited for; matrix products, arithmetic and copies ran while one was open for 1% of the time, Pallas kernels for 5%

profile of v8, /device:TPU:0, one launch (start us, length us, event | category | flops | bytes accessed | tf_op | source)
XLA Modules:
  0.0 67.8 jit_solution(15850924699962857630)
XLA Ops:
  0.0 1.5 %encode.1 = (bf16[512,384]{1,0:T(8,128)(2,1)S(1)}, bf16[256,384]{1,0:T(8,128)(2,1)S(1)}, bf16[256,384]{1,0:T(8,128)(2,1)S(1)}, f32[2,384]{1,0:T(2,128)S(1)}) custom-call(s32[512,384]{1,0:T(8,128)} %genotype_ref.1, s32[512,384]{1,0:T(8,128)} %mask_ref.1), custom_call_target="tpu_custom_call" | custom-call | tf_op jit(solution)/shard_map/encode/pallas_call | solution.py:87
  1.5 5.1 %collective-permute-start.3 = (bf16[256,384]{1,0:T(8,128)(2,1)S(1)}, bf16[256,384]{1,0:T(8,128)(2,1)S(1)}, u32[]{:S(2)}, u32[]{:S(2)}) collective-permute-start(bf16[256,384]{1,0:T(8,128)(2,1)S(1)} %get-tuple-element.39), channel_id=1, source_target_pairs={{0,24},{4,28},{8,0},{12,4},{16,8},{20,12},{24,16},{28,20},{1,25},{... | collective-permute-start | bytes 589832 | tf_op jit(solution)/shard_map/ppermute | solution.py:15
  6.6 0.4 collective-permute-start.6
  7.1 4.8 %collective-permute-done.3.rest_2_ = bf16[256,384]{1,0:T(8,128)(2,1)S(1)} collective-permute-done((bf16[256,384]{1,0:T(8,128)(2,1)S(1)}, bf16[256,384]{1,0:T(8,128)(2,1)S(1)}, u32[]{:S(2)}, u32[]{:S(2)}) %collective-permute-start.3) | collective-permute-done | bytes 196640 | tf_op jit(solution)/shard_map/ppermute | solution.py:15
  11.9 4.3 %collective-permute-start.4 = (bf16[256,384]{1,0:T(8,128)(2,1)S(1)}, bf16[256,384]{1,0:T(8,128)(2,1)S(1)}, u32[]{:S(2)}, u32[]{:S(2)}) collective-permute-start(bf16[256,384]{1,0:T(8,128)(2,1)S(1)} %collective-permute-done.3.rest_2_), channel_id=1, source_target_pairs={{0,24},{4,28},{8,0},{12,4},{16,8},{20,12},{24,16},{28,20},{1,25},{... | collective-permute-start | bytes 589832 | tf_op jit(solution)/shard_map/ppermute | solution.py:15
  16.2 1.5 %collective-permute-start.8 = (bf16[256,384]{1,0:T(8,128)(2,1)S(1)}, bf16[256,384]{1,0:T(8,128)(2,1)S(1)}, u32[]{:S(2)}, u32[]{:S(2)}) collective-permute-start(bf16[256,384]{1,0:T(8,128)(2,1)S(1)} %collective-permute-done.3.rest_2_), channel_id=1, source_target_pairs={{0,4},{4,0},{8,12},{12,8},{16,20},{20,16},{24,28},{28,24},{1,5},{5... | collective-permute-start | bytes 589832 | tf_op jit(solution)/shard_map/ppermute | solution.py:15
  17.7 0.0 collective-permute-done.6.rest_1_
  17.7 2.4 %collective-permute-start.11 = (bf16[256,384]{1,0:T(8,128)(2,1)S(1)}, bf16[256,384]{1,0:T(8,128)(2,1)S(1)}, u32[]{:S(2)}, u32[]{:S(2)}) collective-permute-start(bf16[256,384]{1,0:T(8,128)(2,1)S(1)} %collective-permute-done.6.rest_1_), channel_id=1, source_target_pairs={{0,24},{4,28},{8,0},{12,4},{16,8},{20,12},{24,16},{28,20},{1,25},{... | collective-permute-start | bytes 589832 | tf_op jit(solution)/shard_map/ppermute | solution.py:15
  20.1 1.5 %collective-permute-start.7 = (bf16[256,384]{1,0:T(8,128)(2,1)S(1)}, bf16[256,384]{1,0:T(8,128)(2,1)S(1)}, u32[]{:S(2)}, u32[]{:S(2)}) collective-permute-start(bf16[256,384]{1,0:T(8,128)(2,1)S(1)} %collective-permute-done.6.rest_1_), channel_id=1, source_target_pairs={{0,4},{4,0},{8,12},{12,8},{16,20},{20,16},{24,28},{28,24},{1,5},{5... | collective-permute-start | bytes 589832 | tf_op jit(solution)/shard_map/ppermute | solution.py:15
  21.6 0.0 collective-permute-done.4.rest_3_
  21.7 0.6 collective-permute-start.5
  22.2 1.4 %collective-permute-done.11.rest_0_ = bf16[256,384]{1,0:T(8,128)(2,1)S(1)} collective-permute-done((bf16[256,384]{1,0:T(8,128)(2,1)S(1)}, bf16[256,384]{1,0:T(8,128)(2,1)S(1)}, u32[]{:S(2)}, u32[]{:S(2)}) %collective-permute-start.11) | collective-permute-done | bytes 196640 | tf_op jit(solution)/shard_map/ppermute | solution.py:15
  23.6 1.6 %collective-permute-start.12 = (bf16[256,384]{1,0:T(8,128)(2,1)S(1)}, bf16[256,384]{1,0:T(8,128)(2,1)S(1)}, u32[]{:S(2)}, u32[]{:S(2)}) collective-permute-start(bf16[256,384]{1,0:T(8,128)(2,1)S(1)} %broadcast_select_fusion), channel_id=1, source_target_pairs={{0,4},{4,0},{8,12},{12,8},{16,20},{20,16},{24,28},{28,24},{1,5},{5... | collective-permute-start | bytes 589832 | tf_op jit(solution)/shard_map/ppermute | solution.py:15
  25.2 0.5 collective-permute-start
  25.7 8.9 %collective-permute-done = f32[2,384]{1,0:T(2,128)S(1)} collective-permute-done((f32[2,384]{1,0:T(2,128)S(1)}, f32[2,384]{1,0:T(2,128)S(1)}, u32[]{:S(2)}, u32[]{:S(2)}) %collective-permute-start) | collective-permute-done | bytes 3104 | tf_op jit(solution)/shard_map/ppermute | solution.py:15
  34.6 0.0 collective-permute-start.1
  34.6 3.6 %collective-permute-done.1 = f32[2,384]{1,0:T(2,128)S(1)} collective-permute-done((f32[2,384]{1,0:T(2,128)S(1)}, f32[2,384]{1,0:T(2,128)S(1)}, u32[]{:S(2)}, u32[]{:S(2)}) %collective-permute-start.1) | collective-permute-done | bytes 3104 | tf_op jit(solution)/shard_map/ppermute | solution.py:15
  38.2 0.0 collective-permute-start.2
  38.2 4.5 %collective-permute-done.2.more_ref = f32[2,384]{1,0:T(2,128)S(1)} collective-permute-done((f32[2,384]{1,0:T(2,128)S(1)}, f32[2,384]{1,0:T(2,128)S(1)}, u32[]{:S(2)}, u32[]{:S(2)}) %collective-permute-start.2) | collective-permute-done | bytes 3104 | tf_op jit(solution)/shard_map/ppermute | solution.py:15
  42.7 0.2 shard_map.28
  42.9 0.7 %shard_map.31 = (f32[512,256]{1,0:T(8,128)S(1)}, f32[512,256]{1,0:T(8,128)S(1)}, f32[512,256]{1,0:T(8,128)S(1)}, f32[512,256]{1,0:T(8,128)S(1)}) custom-call(bf16[512,384]{1,0:T(8,128)(2,1)S(1)} %get-tuple-element.37.left_ref, f32[2,384]{1,0:T(2,128)S(1)} %get-tuple-element.38.factors_ref, bf16[512,384]{1,0:T(8,128)(2,1)S(1)} %get-tuple-element.35.calls_ref.rest_0_, ...), custom_call_target="tpu_custom_call" | custom-call | flops 301989888 | bytes 524288 | tf_op jit(solution)/shard_map/pallas_call | solution.py:40
  43.6 0.4 shard_map.32
  44.0 0.1 collective-permute-start.16
  44.1 0.0 collective-permute-done.8.rest_1_
  44.1 0.0 collective-permute-done.7.rest_0_.rest_2_
  44.1 0.4 shard_map.29
  44.6 0.9 %shard_map.33 = (f32[512,256]{1,0:T(8,128)S(1)}, f32[512,256]{1,0:T(8,128)S(1)}, f32[512,256]{1,0:T(8,128)S(1)}, f32[512,256]{1,0:T(8,128)S(1)}) custom-call(bf16[512,384]{1,0:T(8,128)(2,1)S(1)} %get-tuple-element.37.left_ref, f32[2,384]{1,0:T(2,128)S(1)} %get-tuple-element.38.factors_ref, bf16[512,384]{1,0:T(8,128)(2,1)S(1)} %get-tuple-element.35.calls_ref.rest_0_, ...), custom_call_target="tpu_custom_call" | custom-call | flops 402653184 | bytes 524288 | tf_op jit(solution)/shard_map/pallas_call | solution.py:40
  45.5 0.0 collective-permute-done.5.rest_0_
  45.5 0.6 shard_map.30
  46.1 0.5 collective-permute-start.9
  46.7 0.0 collective-permute-done.12.rest_0_
  46.7 0.4 shard_map.34
  47.2 0.1 collective-permute-start.14
  47.3 0.2 pad_maximum_fusion
  47.5 0.5 collective-permute-start.13
  48.0 0.0 collective-permute-done.16
  48.0 0.1 add_convert_fusion
  48.1 1.6 %collective-permute-start.17 = (f16[512,256]{1,0:T(8,128)(2,1)S(1)}, f16[512,256]{1,0:T(8,128)(2,1)S(1)}, u32[]{:S(2)}, u32[]{:S(2)}) collective-permute-start(f16[512,256]{1,0:T(8,128)(2,1)S(1)} %add_convert_fusion), channel_id=1, source_target_pairs={{0,2},{1,3},{2,0},{3,1},{4,6},{5,7},{6,4},{7,5},{8,10},{9,11},{10,... | collective-permute-start | bytes 786440 | tf_op jit(solution)/shard_map/ppermute | solution.py:15
  49.6 0.0 collective-permute-done.14
  49.7 0.1 add_convert_fusion.1
  49.7 0.7 collective-permute-start.15
  50.4 0.0 collective-permute-done.9
  50.5 1.5 %collective-permute-start.10 = (f16[512,128]{1,0:T(8,128)(2,1)S(1)}, f16[512,128]{1,0:T(8,128)(2,1)S(1)}, u32[]{:S(2)}, u32[]{:S(2)}) collective-permute-start(f16[512,128]{1,0:T(8,128)(2,1)S(1)} %add_convert_fusion.2), channel_id=1, source_target_pairs={{0,2},{1,3},{2,0},{3,1},{4,6},{5,7},{6,4},{7,5},{8,10},{9,11},{10,... | collective-permute-start | bytes 393224 | tf_op jit(solution)/shard_map/ppermute | solution.py:15
  51.9 12.9 %collective-permute-done.10 = f16[512,128]{1,0:T(8,128)(2,1)S(1)} collective-permute-done((f16[512,128]{1,0:T(8,128)(2,1)S(1)}, f16[512,128]{1,0:T(8,128)(2,1)S(1)}, u32[]{:S(2)}, u32[]{:S(2)}) %collective-permute-start.10) | collective-permute-done | bytes 131104 | tf_op jit(solution)/shard_map/ppermute | solution.py:15
  64.8 0.0 collective-permute-done.17
  64.9 0.0 collective-permute-done.15
  65.0 0.0 collective-permute-done.13
  65.0 0.1 convert_element_type.55.other_ref
  65.1 0.9 %shard_map.35.rest_0_ = f32[512,640]{1,0:T(8,128)} custom-call(f32[512,256]{1,0:T(8,128)S(1)} %get-tuple-element.62.ours_ref, f32[512,256]{1,0:T(8,128)S(1)} %convert_element_type.63.got_ref, f32[512,640]{1,0:T(8,128)S(1)} %convert_element_type.55.other_ref), custom_call_target="tpu_custom_call" | custom-call | flops 131072 | bytes 524288 | tf_op jit(solution)/shard_map/pallas_call | solution.py:40
  66.0 0.9 %shard_map.36.rest_0_ = f32[512,640]{1,0:T(8,128)} custom-call(f32[512,256]{1,0:T(8,128)S(1)} %get-tuple-element.59.ours_ref, f32[512,256]{1,0:T(8,128)S(1)} %convert_element_type.59.got_ref, f32[512,640]{1,0:T(8,128)S(1)} %convert_element_type.55.other_ref, f32[512,640]{1,0:T(8,128)} %shard_map.35.rest_0_), custom_call_target="tpu_custom_call", output_to_operand_aliasing={{}: (3, {})} | custom-call | flops 131072 | bytes 524288 | tf_op jit(solution)/shard_map/pallas_call | solution.py:40
  66.8 0.8 %shard_map.37 = f32[512,640]{1,0:T(8,128)} custom-call(f32[512,128]{1,0:T(8,128)S(1)} %get-tuple-element.45.ours_ref, f32[512,128]{1,0:T(8,128)S(1)} %convert_element_type.51.got_ref, f32[512,640]{1,0:T(8,128)S(1)} %convert_element_type.55.other_ref, f32[512,640]{1,0:T(8,128)} %shard_map.36.rest_0_), custom_call_target="tpu_custom_call", output_to_operand_aliasing={{}: (3, {})} | custom-call | flops 65536 | bytes 262144 | tf_op jit(solution)/shard_map/pallas_call | solution.py:40
  (14 shorter events, 0.4 us)
Async XLA Ops:
  1.5 10.4 %collective-permute-start.3 = (bf16[256,384]{1,0:T(8,128)(2,1)S(1)}, bf16[256,384]{1,0:T(8,128)(2,1)S(1)}, u32[]{:S(2)}, u32[]{:S(2)}) collective-permute-start(bf16[256,384]{1,0:T(8,128)(2,1)S(1)} %get-tuple-element.39), channel_id=1, source_target_pairs={{0,24},{4,28},{8,0},{12,4},{16,8},{20,12},{24,16},{28,20},{1,25},{... | collective-permute-start | bytes 589832 | tf_op jit(solution)/shard_map/ppermute | solution.py:15
  6.6 11.1 %collective-permute-start.6 = (bf16[256,384]{1,0:T(8,128)(2,1)S(1)}, bf16[256,384]{1,0:T(8,128)(2,1)S(1)}, u32[]{:S(2)}, u32[]{:S(2)}) collective-permute-start(bf16[256,384]{1,0:T(8,128)(2,1)S(1)} %get-tuple-element.40), channel_id=1, source_target_pairs={{0,24},{4,28},{8,0},{12,4},{16,8},{20,12},{24,16},{28,20},{1,25},{... | collective-permute-start | bytes 589832 | tf_op jit(solution)/shard_map/ppermute | solution.py:15
  11.9 9.7 %collective-permute-start.4 = (bf16[256,384]{1,0:T(8,128)(2,1)S(1)}, bf16[256,384]{1,0:T(8,128)(2,1)S(1)}, u32[]{:S(2)}, u32[]{:S(2)}) collective-permute-start(bf16[256,384]{1,0:T(8,128)(2,1)S(1)} %collective-permute-done.3.rest_2_), channel_id=1, source_target_pairs={{0,24},{4,28},{8,0},{12,4},{16,8},{20,12},{24,16},{28,20},{1,25},{... | collective-permute-start | bytes 589832 | tf_op jit(solution)/shard_map/ppermute | solution.py:15
  16.2 27.9 %collective-permute-start.8 = (bf16[256,384]{1,0:T(8,128)(2,1)S(1)}, bf16[256,384]{1,0:T(8,128)(2,1)S(1)}, u32[]{:S(2)}, u32[]{:S(2)}) collective-permute-start(bf16[256,384]{1,0:T(8,128)(2,1)S(1)} %collective-permute-done.3.rest_2_), channel_id=1, source_target_pairs={{0,4},{4,0},{8,12},{12,8},{16,20},{20,16},{24,28},{28,24},{1,5},{5... | collective-permute-start | bytes 589832 | tf_op jit(solution)/shard_map/ppermute | solution.py:15
  17.7 5.9 %collective-permute-start.11 = (bf16[256,384]{1,0:T(8,128)(2,1)S(1)}, bf16[256,384]{1,0:T(8,128)(2,1)S(1)}, u32[]{:S(2)}, u32[]{:S(2)}) collective-permute-start(bf16[256,384]{1,0:T(8,128)(2,1)S(1)} %collective-permute-done.6.rest_1_), channel_id=1, source_target_pairs={{0,24},{4,28},{8,0},{12,4},{16,8},{20,12},{24,16},{28,20},{1,25},{... | collective-permute-start | bytes 589832 | tf_op jit(solution)/shard_map/ppermute | solution.py:15
  20.1 24.0 %collective-permute-start.7 = (bf16[256,384]{1,0:T(8,128)(2,1)S(1)}, bf16[256,384]{1,0:T(8,128)(2,1)S(1)}, u32[]{:S(2)}, u32[]{:S(2)}) collective-permute-start(bf16[256,384]{1,0:T(8,128)(2,1)S(1)} %collective-permute-done.6.rest_1_), channel_id=1, source_target_pairs={{0,4},{4,0},{8,12},{12,8},{16,20},{20,16},{24,28},{28,24},{1,5},{5... | collective-permute-start | bytes 589832 | tf_op jit(solution)/shard_map/ppermute | solution.py:15
  21.7 23.8 %collective-permute-start.5 = (bf16[256,384]{1,0:T(8,128)(2,1)S(1)}, bf16[256,384]{1,0:T(8,128)(2,1)S(1)}, u32[]{:S(2)}, u32[]{:S(2)}) collective-permute-start(bf16[256,384]{1,0:T(8,128)(2,1)S(1)} %broadcast_select_fusion.1), channel_id=1, source_target_pairs={{0,4},{4,0},{8,12},{12,8},{16,20},{20,16},{24,28},{28,24},{1,5},{5... | collective-permute-start | bytes 589832 | tf_op jit(solution)/shard_map/ppermute | solution.py:15
  23.6 23.1 %collective-permute-start.12 = (bf16[256,384]{1,0:T(8,128)(2,1)S(1)}, bf16[256,384]{1,0:T(8,128)(2,1)S(1)}, u32[]{:S(2)}, u32[]{:S(2)}) collective-permute-start(bf16[256,384]{1,0:T(8,128)(2,1)S(1)} %broadcast_select_fusion), channel_id=1, source_target_pairs={{0,4},{4,0},{8,12},{12,8},{16,20},{20,16},{24,28},{28,24},{1,5},{5... | collective-permute-start | bytes 589832 | tf_op jit(solution)/shard_map/ppermute | solution.py:15
  25.2 9.4 %collective-permute-start = (f32[2,384]{1,0:T(2,128)S(1)}, f32[2,384]{1,0:T(2,128)S(1)}, u32[]{:S(2)}, u32[]{:S(2)}) collective-permute-start(f32[2,384]{1,0:T(2,128)S(1)} %get-tuple-element.36), channel_id=1, source_target_pairs={{0,4},{4,0},{8,12},{12,8},{16,20},{20,16},{24,28},{28,24},{1,5},{5... | collective-permute-start | bytes 9224 | tf_op jit(solution)/shard_map/ppermute | solution.py:15
  34.6 3.6 %collective-permute-start.1 = (f32[2,384]{1,0:T(2,128)S(1)}, f32[2,384]{1,0:T(2,128)S(1)}, u32[]{:S(2)}, u32[]{:S(2)}) collective-permute-start(f32[2,384]{1,0:T(2,128)S(1)} %add.19), channel_id=1, source_target_pairs={{0,8},{4,12},{8,0},{12,4},{16,24},{20,28},{24,16},{28,20},{1,9},{5... | collective-permute-start | bytes 9224 | tf_op jit(solution)/shard_map/ppermute | solution.py:15
  38.2 4.5 %collective-permute-start.2 = (f32[2,384]{1,0:T(2,128)S(1)}, f32[2,384]{1,0:T(2,128)S(1)}, u32[]{:S(2)}, u32[]{:S(2)}) collective-permute-start(f32[2,384]{1,0:T(2,128)S(1)} %add.20.sums_ref), channel_id=1, source_target_pairs={{0,16},{4,20},{8,24},{12,28},{16,0},{20,4},{24,8},{28,12},{1,17},{... | collective-permute-start | bytes 9224 | tf_op jit(solution)/shard_map/ppermute | solution.py:15
  44.0 4.0 %collective-permute-start.16 = (f16[512,256]{1,0:T(8,128)(2,1)S(1)}, f16[512,256]{1,0:T(8,128)(2,1)S(1)}, u32[]{:S(2)}, u32[]{:S(2)}) collective-permute-start(f16[512,256]{1,0:T(8,128)(2,1)S(1)} %convert_element_type.60), channel_id=1, source_target_pairs={{0,1},{1,0},{2,3},{3,2},{4,5},{5,4},{6,7},{7,6},{8,9},{9,8},{10,11... | collective-permute-start | bytes 786440 | tf_op jit(solution)/shard_map/ppermute | solution.py:15
  46.1 4.3 %collective-permute-start.9 = (f16[512,128]{1,0:T(8,128)(2,1)S(1)}, f16[512,128]{1,0:T(8,128)(2,1)S(1)}, u32[]{:S(2)}, u32[]{:S(2)}) collective-permute-start(f16[512,128]{1,0:T(8,128)(2,1)S(1)} %convert_element_type.48), channel_id=1, source_target_pairs={{0,1},{1,0},{2,3},{3,2},{4,5},{5,4},{6,7},{7,6},{8,9},{9,8},{10,11... | collective-permute-start | bytes 393224 | tf_op jit(solution)/shard_map/ppermute | solution.py:15
  47.2 2.5 %collective-permute-start.14 = (f16[512,256]{1,0:T(8,128)(2,1)S(1)}, f16[512,256]{1,0:T(8,128)(2,1)S(1)}, u32[]{:S(2)}, u32[]{:S(2)}) collective-permute-start(f16[512,256]{1,0:T(8,128)(2,1)S(1)} %convert_element_type.56), channel_id=1, source_target_pairs={{0,1},{1,0},{2,3},{3,2},{4,5},{5,4},{6,7},{7,6},{8,9},{9,8},{10,11... | collective-permute-start | bytes 786440 | tf_op jit(solution)/shard_map/ppermute | solution.py:15
  47.5 17.5 %collective-permute-start.13 = (f16[512,640]{1,0:T(8,128)(2,1)S(1)}, f16[512,640]{1,0:T(8,128)(2,1)S(1)}, u32[]{:S(2)}, u32[]{:S(2)}) collective-permute-start(f16[512,640]{1,0:T(8,128)(2,1)S(1)} %pad_maximum_fusion), channel_id=1, source_target_pairs={{0,1},{1,0},{2,3},{3,2},{4,5},{5,4},{6,7},{7,6},{8,9},{9,8},{10,11... | collective-permute-start | bytes 1966088 | tf_op jit(solution)/shard_map/ppermute | solution.py:15
  48.1 16.8 %collective-permute-start.17 = (f16[512,256]{1,0:T(8,128)(2,1)S(1)}, f16[512,256]{1,0:T(8,128)(2,1)S(1)}, u32[]{:S(2)}, u32[]{:S(2)}) collective-permute-start(f16[512,256]{1,0:T(8,128)(2,1)S(1)} %add_convert_fusion), channel_id=1, source_target_pairs={{0,2},{1,3},{2,0},{3,1},{4,6},{5,7},{6,4},{7,5},{8,10},{9,11},{10,... | collective-permute-start | bytes 786440 | tf_op jit(solution)/shard_map/ppermute | solution.py:15
  49.7 15.2 %collective-permute-start.15 = (f16[512,256]{1,0:T(8,128)(2,1)S(1)}, f16[512,256]{1,0:T(8,128)(2,1)S(1)}, u32[]{:S(2)}, u32[]{:S(2)}) collective-permute-start(f16[512,256]{1,0:T(8,128)(2,1)S(1)} %add_convert_fusion.1), channel_id=1, source_target_pairs={{0,2},{1,3},{2,0},{3,1},{4,6},{5,7},{6,4},{7,5},{8,10},{9,11},{10,... | collective-permute-start | bytes 786440 | tf_op jit(solution)/shard_map/ppermute | solution.py:15
  50.5 14.4 %collective-permute-start.10 = (f16[512,128]{1,0:T(8,128)(2,1)S(1)}, f16[512,128]{1,0:T(8,128)(2,1)S(1)}, u32[]{:S(2)}, u32[]{:S(2)}) collective-permute-start(f16[512,128]{1,0:T(8,128)(2,1)S(1)} %add_convert_fusion.2), channel_id=1, source_target_pairs={{0,2},{1,3},{2,0},{3,1},{4,6},{5,7},{6,4},{7,5},{8,10},{9,11},{10,... | collective-permute-start | bytes 393224 | tf_op jit(solution)/shard_map/ppermute | solution.py:15

commit v9 on v8

--- a/solution.py
+++ b/solution.py
@@ -51,7 +51,7 @@
 ANY = pl.BlockSpec(memory_space=pl.ANY)
 
 
-def encode_body(genotype_ref, mask_ref, whole_ref, first_ref, second_ref, sums_ref,
+def encode_body(genotype_ref, mask_ref, first_ref, second_ref, sums_ref,
                 dosage_in, mask_in, sems):
     rows = first_ref.shape[0]
     copies = []
@@ -71,7 +71,6 @@
         mask = mask_in[at, :]
         dosage = mask * dosage_in[at, :]
         calls = (dosage + mask).astype(jnp.float32).astype(jnp.bfloat16)
-        whole_ref[at, :] = calls
         part_ref[...] = calls
         totals.append([
             jnp.sum(value.astype(jnp.float32), axis=0, keepdims=True) for value in (dosage, mask)
@@ -87,9 +86,9 @@
     return pl.pallas_call(
         encode_body,
         name="encode",
-        out_shape=(calls(rows), calls(half), calls(half), jax.ShapeDtypeStruct((2, columns), jnp.float32)),
+        out_shape=(calls(half), calls(half), jax.ShapeDtypeStruct((2, columns), jnp.float32)),
         in_specs=[ANY, ANY],
-        out_specs=(VMEM,) * 4,
+        out_specs=(VMEM,) * 3,
         scratch_shapes=[
             pltpu.VMEM((rows, columns), jnp.int32),
             pltpu.VMEM((rows, columns), jnp.int32),
@@ -109,11 +108,13 @@
     return jnp.where(wide > 0.0, (wide - shift) * scale, 0.0).astype(jnp.bfloat16)
 
 
-def left_body(down, calls_ref, sums_ref, more_ref, left_ref, factors_ref):
+def left_body(down, first_ref, second_ref, sums_ref, more_ref, left_ref, factors_ref):
     shift, scale = factors(sums_ref[...] + more_ref[...])
     factors_ref[0:1, :] = shift
     factors_ref[1:2, :] = scale
-    left_ref[...] = standardized(calls_ref[...], shift, scale) * down
+    half = first_ref.shape[0]
+    for n, calls_ref in enumerate((first_ref, second_ref)):
+        left_ref[pl.ds(n * half, half), :] = standardized(calls_ref[...], shift, scale) * down
 
 
 def multiply(left, right):
@@ -150,18 +151,24 @@
 
 
 def add_body(places, at, up, ours_ref, got_ref, other_ref, *rest):
-    out_ref, total_ref, sem = rest[-3:]
-    other = other_ref[:, pl.ds(at, total_ref.shape[1])]
-    total_ref[...] = (ours_ref[...] + other + got_ref[...]) * up
+    out_ref, total_ref, sems = rest[-3:]
+    height, width = total_ref.shape[0] // 2, total_ref.shape[1]
     device = lax.axis_index("snps")
-    width = total_ref.shape[1]
     for strip, begin in enumerate(places):
 
         @pl.when(device == strip)
         def _(begin=begin):
-            copy = pltpu.make_async_copy(total_ref, out_ref.at[:, pl.ds(begin, width)], sem)
-            copy.start()
-            copy.wait()
+            copies = []
+            for half in range(2):
+                rows = pl.ds(half * height, height)
+                other = other_ref[rows, pl.ds(at, width)]
+                total_ref[rows, :] = (ours_ref[rows, :] + other + got_ref[rows, :]) * up
+                copies.append(pltpu.make_async_copy(
+                    total_ref.at[rows], out_ref.at[rows, pl.ds(begin, width)], sems.at[half]
+                ))
+                copies[half].start()
+            for copy in copies:
+                copy.wait()
 
 
 def per_device(genotype, mask):
@@ -174,7 +181,7 @@
     half_rows = rows // 2
     width = rows * (samples // 2 + 1) // parts
 
-    calls, first, second, sums = encode(genotype, mask)
+    first, second, sums = encode(genotype, mask)
 
     along = lambda s: (s - 2) % samples
     even = lax.axis_index("samples") % 2 == 0
@@ -197,7 +204,7 @@
 
     def source(k, h, odd):
         if k == 0:
-            return calls, h * half_rows
+            return line[0][h], 0
         if k % 2 == 0:
             return line[k // 2][h], 0
         if k == 1 and not odd:
@@ -210,7 +217,7 @@
     left, pair = call_kernel(
         functools.partial(left_body, down),
         (jax.ShapeDtypeStruct((rows, snp_part), jnp.bfloat16), jax.ShapeDtypeStruct((2, snp_part), jnp.float32)),
-        (calls, sums, more), [VMEM] * 3, 5 * rows * snp_part, 4 * rows * snp_part, out_specs=(VMEM, VMEM),
+        (first, second, sums, more), [VMEM] * 4, 5 * rows * snp_part, 4 * rows * snp_part, out_specs=(VMEM, VMEM),
     )
     count = len(table[0][0])
     quarter = half_rows // 2
@@ -277,7 +284,7 @@
             jax.ShapeDtypeStruct((rows, width), jnp.float32), operands,
             [VMEM] * 3 + [ANY] * len(last), rows * columns, 4 * rows * columns,
             out_specs=ANY,
-            scratch_shapes=[pltpu.VMEM((rows, columns), jnp.float32), pltpu.SemaphoreType.DMA],
+            scratch_shapes=[pltpu.VMEM((rows, columns), jnp.float32), pltpu.SemaphoreType.DMA((2,))],
             input_output_aliases={len(operands) - 1: 0} if last else {},
         )
     return out

time: 67.9 us -> 70.8 us (1.043)
  starting transfers between devices: 22.9 us -> 24.4 us
  waiting for transfers between devices: 36 us -> 37.5 us
    ppermute x18, starting transfers between devices: 22.9 us -> 24.4 us  [send(): lax.ppermute(value, axis, [pair for pair in pairs if pair[1] is not None])]
    ppermute x18, waiting for transfers between devices: 36 us -> 37.5 us  [send(): lax.ppermute(value, axis, [pair for pair in pairs if pair[1] is not None])]
  transfers between devices with their start and end apart: 18 -> 18, of which waited for: 6 -> 5; matrix products, arithmetic and copies ran while one was open for 1% -> 1% of each run, Pallas kernels for 5% -> 5%
where the time goes in v9:
time: 70.8 us; the launch traced here: 70.6 us
  waiting for transfers between devices  37.5 us (53%)
  starting transfers between devices  24.4 us (34%)
  Pallas kernels  7.48 us (11%)
  other arithmetic  0.83 us (1%)
    ppermute x18, waiting for transfers between devices, send(): lax.ppermute(value, axis, [pair for pair in pairs if pair[1] is not None])  37.5 us
    ppermute x18, starting transfers between devices, send(): lax.ppermute(value, axis, [pair for pair in pairs if pair[1] is not None])  24.4 us
    pallas_call x10, Pallas kernels, call_kernel(): pl.pallas_call(body, out_shape=shapes, in_specs=specs, compiler_params=pl...  5.98 us
    pallas_call x1, Pallas kernels, encode(): pl.pallas_call(encode_body, name='encode', out_shape=(calls(half), calls(...  1.49 us
  transfers between devices with their start and end apart: 18, of which 5 were waited for; matrix products, arithmetic and copies ran while one was open for 1% of the time, Pallas kernels for 5%

profile of v9, /device:TPU:0, one launch (start us, length us, event | category | flops | bytes accessed | tf_op | source)
XLA Modules:
  0.0 70.6 jit_solution(17109301665916723394)
XLA Ops:
  0.0 1.5 %encode.1 = (bf16[256,384]{1,0:T(8,128)(2,1)S(1)}, bf16[256,384]{1,0:T(8,128)(2,1)S(1)}, f32[2,384]{1,0:T(2,128)S(1)}) custom-call(s32[512,384]{1,0:T(8,128)} %genotype_ref.1, s32[512,384]{1,0:T(8,128)} %mask_ref.1), custom_call_target="tpu_custom_call" | custom-call | tf_op jit(solution)/shard_map/encode/pallas_call | solution.py:86
  1.5 5.1 %collective-permute-start.3 = (bf16[256,384]{1,0:T(8,128)(2,1)S(1)}, bf16[256,384]{1,0:T(8,128)(2,1)S(1)}, u32[]{:S(2)}, u32[]{:S(2)}) collective-permute-start(bf16[256,384]{1,0:T(8,128)(2,1)S(1)} %get-tuple-element.35.second_ref.rest_0_), channel_id=1, source_target_pairs={{0,24},{4,28},{8,0},{12,4},{16,8},{20,12},{24,16},{28,20},{1,25},{... | collective-permute-start | bytes 589832 | tf_op jit(solution)/shard_map/ppermute | solution.py:15
  6.6 0.4 collective-permute-start.6
  7.1 4.8 %collective-permute-done.3.rest_2_ = bf16[256,384]{1,0:T(8,128)(2,1)S(1)} collective-permute-done((bf16[256,384]{1,0:T(8,128)(2,1)S(1)}, bf16[256,384]{1,0:T(8,128)(2,1)S(1)}, u32[]{:S(2)}, u32[]{:S(2)}) %collective-permute-start.3) | collective-permute-done | bytes 196640 | tf_op jit(solution)/shard_map/ppermute | solution.py:15
  11.9 4.3 %collective-permute-start.4 = (bf16[256,384]{1,0:T(8,128)(2,1)S(1)}, bf16[256,384]{1,0:T(8,128)(2,1)S(1)}, u32[]{:S(2)}, u32[]{:S(2)}) collective-permute-start(bf16[256,384]{1,0:T(8,128)(2,1)S(1)} %collective-permute-done.3.rest_2_), channel_id=1, source_target_pairs={{0,24},{4,28},{8,0},{12,4},{16,8},{20,12},{24,16},{28,20},{1,25},{... | collective-permute-start | bytes 589832 | tf_op jit(solution)/shard_map/ppermute | solution.py:15
  16.2 0.0 collective-permute-done.6.rest_1_
  16.2 3.9 %collective-permute-start.11 = (bf16[256,384]{1,0:T(8,128)(2,1)S(1)}, bf16[256,384]{1,0:T(8,128)(2,1)S(1)}, u32[]{:S(2)}, u32[]{:S(2)}) collective-permute-start(bf16[256,384]{1,0:T(8,128)(2,1)S(1)} %collective-permute-done.6.rest_1_), channel_id=1, source_target_pairs={{0,24},{4,28},{8,0},{12,4},{16,8},{20,12},{24,16},{28,20},{1,25},{... | collective-permute-start | bytes 589832 | tf_op jit(solution)/shard_map/ppermute | solution.py:15
  20.1 1.5 %collective-permute-start.7 = (bf16[256,384]{1,0:T(8,128)(2,1)S(1)}, bf16[256,384]{1,0:T(8,128)(2,1)S(1)}, u32[]{:S(2)}, u32[]{:S(2)}) collective-permute-start(bf16[256,384]{1,0:T(8,128)(2,1)S(1)} %collective-permute-done.6.rest_1_), channel_id=1, source_target_pairs={{0,4},{4,0},{8,12},{12,8},{16,20},{20,16},{24,28},{28,24},{1,5},{5... | collective-permute-start | bytes 589832 | tf_op jit(solution)/shard_map/ppermute | solution.py:15
  21.6 0.5 collective-permute-start.8
  22.2 0.0 collective-permute-done.4.rest_3_
  22.2 1.6 %collective-permute-start.5 = (bf16[256,384]{1,0:T(8,128)(2,1)S(1)}, bf16[256,384]{1,0:T(8,128)(2,1)S(1)}, u32[]{:S(2)}, u32[]{:S(2)}) collective-permute-start(bf16[256,384]{1,0:T(8,128)(2,1)S(1)} %broadcast_select_fusion.1), channel_id=1, source_target_pairs={{0,4},{4,0},{8,12},{12,8},{16,20},{20,16},{24,28},{28,24},{1,5},{5... | collective-permute-start | bytes 589832 | tf_op jit(solution)/shard_map/ppermute | solution.py:15
  23.8 0.0 collective-permute-done.11.rest_0_
  23.8 1.4 %collective-permute-start.12 = (bf16[256,384]{1,0:T(8,128)(2,1)S(1)}, bf16[256,384]{1,0:T(8,128)(2,1)S(1)}, u32[]{:S(2)}, u32[]{:S(2)}) collective-permute-start(bf16[256,384]{1,0:T(8,128)(2,1)S(1)} %broadcast_select_fusion), channel_id=1, source_target_pairs={{0,4},{4,0},{8,12},{12,8},{16,20},{20,16},{24,28},{28,24},{1,5},{5... | collective-permute-start | bytes 589832 | tf_op jit(solution)/shard_map/ppermute | solution.py:15
  25.2 0.7 collective-permute-start
  25.9 11.6 %collective-permute-done = f32[2,384]{1,0:T(2,128)S(1)} collective-permute-done((f32[2,384]{1,0:T(2,128)S(1)}, f32[2,384]{1,0:T(2,128)S(1)}, u32[]{:S(2)}, u32[]{:S(2)}) %collective-permute-start) | collective-permute-done | bytes 3104 | tf_op jit(solution)/shard_map/ppermute | solution.py:15
  37.5 0.0 collective-permute-start.1
  37.5 3.6 %collective-permute-done.1 = f32[2,384]{1,0:T(2,128)S(1)} collective-permute-done((f32[2,384]{1,0:T(2,128)S(1)}, f32[2,384]{1,0:T(2,128)S(1)}, u32[]{:S(2)}, u32[]{:S(2)}) %collective-permute-start.1) | collective-permute-done | bytes 3104 | tf_op jit(solution)/shard_map/ppermute | solution.py:15
  41.1 0.0 collective-permute-start.2
  41.1 4.5 %collective-permute-done.2.more_ref = f32[2,384]{1,0:T(2,128)S(1)} collective-permute-done((f32[2,384]{1,0:T(2,128)S(1)}, f32[2,384]{1,0:T(2,128)S(1)}, u32[]{:S(2)}, u32[]{:S(2)}) %collective-permute-start.2) | collective-permute-done | bytes 3104 | tf_op jit(solution)/shard_map/ppermute | solution.py:15
  45.6 0.2 shard_map.28
  45.8 0.7 shard_map.31
  46.5 0.4 shard_map.32
  46.9 0.1 collective-permute-start.16
  47.0 0.0 collective-permute-done.7.rest_0_.rest_2_
  47.1 0.0 collective-permute-done.8.rest_1_
  47.1 0.4 shard_map.29
  47.5 0.9 %shard_map.33 = (f32[512,256]{1,0:T(8,128)S(1)}, f32[512,256]{1,0:T(8,128)S(1)}, f32[512,256]{1,0:T(8,128)S(1)}, f32[512,256]{1,0:T(8,128)S(1)}) custom-call(bf16[512,384]{1,0:T(8,128)(2,1)S(1)} %get-tuple-element.37.left_ref, f32[2,384]{1,0:T(2,128)S(1)} %get-tuple-element.38.factors_ref, bf16[256,384]{1,0:T(8,128)(2,1)S(1)} %get-tuple-element.35.second_ref.rest_0_, ...), custom_call_target="tpu_custom_call" | custom-call | flops 402653184 | bytes 524288 | tf_op jit(solution)/shard_map/pallas_call | solution.py:40
  48.4 0.0 collective-permute-done.5.rest_0_
  48.4 0.6 shard_map.30
  49.1 0.5 collective-permute-start.9
  49.6 0.0 collective-permute-done.12.rest_0_
  49.6 0.4 shard_map.34
  50.1 0.1 collective-permute-start.14
  50.2 0.2 pad_maximum_fusion
  50.4 0.5 collective-permute-start.13
  50.9 0.0 collective-permute-done.16
  50.9 0.1 add_convert_fusion
  51.0 1.5 %collective-permute-start.17 = (f16[512,256]{1,0:T(8,128)(2,1)S(1)}, f16[512,256]{1,0:T(8,128)(2,1)S(1)}, u32[]{:S(2)}, u32[]{:S(2)}) collective-permute-start(f16[512,256]{1,0:T(8,128)(2,1)S(1)} %add_convert_fusion), channel_id=1, source_target_pairs={{0,2},{1,3},{2,0},{3,1},{4,6},{5,7},{6,4},{7,5},{8,10},{9,11},{10,... | collective-permute-start | bytes 786440 | tf_op jit(solution)/shard_map/ppermute | solution.py:15
  52.5 0.0 collective-permute-done.14
  52.5 0.1 add_convert_fusion.1
  52.6 0.7 collective-permute-start.15
  53.3 0.0 collective-permute-done.9
  53.4 1.5 %collective-permute-start.10 = (f16[512,128]{1,0:T(8,128)(2,1)S(1)}, f16[512,128]{1,0:T(8,128)(2,1)S(1)}, u32[]{:S(2)}, u32[]{:S(2)}) collective-permute-start(f16[512,128]{1,0:T(8,128)(2,1)S(1)} %add_convert_fusion.2), channel_id=1, source_target_pairs={{0,2},{1,3},{2,0},{3,1},{4,6},{5,7},{6,4},{7,5},{8,10},{9,11},{10,... | collective-permute-start | bytes 393224 | tf_op jit(solution)/shard_map/ppermute | solution.py:15
  54.8 12.9 %collective-permute-done.10 = f16[512,128]{1,0:T(8,128)(2,1)S(1)} collective-permute-done((f16[512,128]{1,0:T(8,128)(2,1)S(1)}, f16[512,128]{1,0:T(8,128)(2,1)S(1)}, u32[]{:S(2)}, u32[]{:S(2)}) %collective-permute-start.10) | collective-permute-done | bytes 131104 | tf_op jit(solution)/shard_map/ppermute | solution.py:15
  67.8 0.0 collective-permute-done.17
  67.8 0.0 collective-permute-done.15
  67.9 0.0 collective-permute-done.13
  67.9 0.1 convert_element_type.55.other_ref
  68.0 0.9 %shard_map.35.rest_0_ = f32[512,640]{1,0:T(8,128)} custom-call(f32[512,256]{1,0:T(8,128)S(1)} %get-tuple-element.60.ours_ref, f32[512,256]{1,0:T(8,128)S(1)} %convert_element_type.63.got_ref, f32[512,640]{1,0:T(8,128)S(1)} %convert_element_type.55.other_ref), custom_call_target="tpu_custom_call" | custom-call | flops 131072 | bytes 524288 | tf_op jit(solution)/shard_map/pallas_call | solution.py:40
  68.8 0.9 %shard_map.36.rest_0_ = f32[512,640]{1,0:T(8,128)} custom-call(f32[512,256]{1,0:T(8,128)S(1)} %get-tuple-element.57.ours_ref, f32[512,256]{1,0:T(8,128)S(1)} %convert_element_type.59.got_ref, f32[512,640]{1,0:T(8,128)S(1)} %convert_element_type.55.other_ref, f32[512,640]{1,0:T(8,128)} %shard_map.35.rest_0_), custom_call_target="tpu_custom_call", output_to_operand_aliasing={{}: (3, {})} | custom-call | flops 131072 | bytes 524288 | tf_op jit(solution)/shard_map/pallas_call | solution.py:40
  69.7 0.8 %shard_map.37 = f32[512,640]{1,0:T(8,128)} custom-call(f32[512,128]{1,0:T(8,128)S(1)} %get-tuple-element.43.ours_ref, f32[512,128]{1,0:T(8,128)S(1)} %convert_element_type.51.got_ref, f32[512,640]{1,0:T(8,128)S(1)} %convert_element_type.55.other_ref, f32[512,640]{1,0:T(8,128)} %shard_map.36.rest_0_), custom_call_target="tpu_custom_call", output_to_operand_aliasing={{}: (3, {})} | custom-call | flops 65536 | bytes 262144 | tf_op jit(solution)/shard_map/pallas_call | solution.py:40
  (14 shorter events, 0.4 us)
Async XLA Ops:
  1.5 10.4 %collective-permute-start.3 = (bf16[256,384]{1,0:T(8,128)(2,1)S(1)}, bf16[256,384]{1,0:T(8,128)(2,1)S(1)}, u32[]{:S(2)}, u32[]{:S(2)}) collective-permute-start(bf16[256,384]{1,0:T(8,128)(2,1)S(1)} %get-tuple-element.35.second_ref.rest_0_), channel_id=1, source_target_pairs={{0,24},{4,28},{8,0},{12,4},{16,8},{20,12},{24,16},{28,20},{1,25},{... | collective-permute-start | bytes 589832 | tf_op jit(solution)/shard_map/ppermute | solution.py:15
  6.6 9.6 %collective-permute-start.6 = (bf16[256,384]{1,0:T(8,128)(2,1)S(1)}, bf16[256,384]{1,0:T(8,128)(2,1)S(1)}, u32[]{:S(2)}, u32[]{:S(2)}) collective-permute-start(bf16[256,384]{1,0:T(8,128)(2,1)S(1)} %get-tuple-element.34.first_ref.rest_0_), channel_id=1, source_target_pairs={{0,24},{4,28},{8,0},{12,4},{16,8},{20,12},{24,16},{28,20},{1,25},{... | collective-permute-start | bytes 589832 | tf_op jit(solution)/shard_map/ppermute | solution.py:15
  11.9 10.2 %collective-permute-start.4 = (bf16[256,384]{1,0:T(8,128)(2,1)S(1)}, bf16[256,384]{1,0:T(8,128)(2,1)S(1)}, u32[]{:S(2)}, u32[]{:S(2)}) collective-permute-start(bf16[256,384]{1,0:T(8,128)(2,1)S(1)} %collective-permute-done.3.rest_2_), channel_id=1, source_target_pairs={{0,24},{4,28},{8,0},{12,4},{16,8},{20,12},{24,16},{28,20},{1,25},{... | collective-permute-start | bytes 589832 | tf_op jit(solution)/shard_map/ppermute | solution.py:15
  16.2 7.6 %collective-permute-start.11 = (bf16[256,384]{1,0:T(8,128)(2,1)S(1)}, bf16[256,384]{1,0:T(8,128)(2,1)S(1)}, u32[]{:S(2)}, u32[]{:S(2)}) collective-permute-start(bf16[256,384]{1,0:T(8,128)(2,1)S(1)} %collective-permute-done.6.rest_1_), channel_id=1, source_target_pairs={{0,24},{4,28},{8,0},{12,4},{16,8},{20,12},{24,16},{28,20},{1,25},{... | collective-permute-start | bytes 589832 | tf_op jit(solution)/shard_map/ppermute | solution.py:15
  20.1 26.9 %collective-permute-start.7 = (bf16[256,384]{1,0:T(8,128)(2,1)S(1)}, bf16[256,384]{1,0:T(8,128)(2,1)S(1)}, u32[]{:S(2)}, u32[]{:S(2)}) collective-permute-start(bf16[256,384]{1,0:T(8,128)(2,1)S(1)} %collective-permute-done.6.rest_1_), channel_id=1, source_target_pairs={{0,4},{4,0},{8,12},{12,8},{16,20},{20,16},{24,28},{28,24},{1,5},{5... | collective-permute-start | bytes 589832 | tf_op jit(solution)/shard_map/ppermute | solution.py:15
  21.6 25.4 %collective-permute-start.8 = (bf16[256,384]{1,0:T(8,128)(2,1)S(1)}, bf16[256,384]{1,0:T(8,128)(2,1)S(1)}, u32[]{:S(2)}, u32[]{:S(2)}) collective-permute-start(bf16[256,384]{1,0:T(8,128)(2,1)S(1)} %collective-permute-done.3.rest_2_), channel_id=1, source_target_pairs={{0,4},{4,0},{8,12},{12,8},{16,20},{20,16},{24,28},{28,24},{1,5},{5... | collective-permute-start | bytes 589832 | tf_op jit(solution)/shard_map/ppermute | solution.py:15
  22.2 26.2 %collective-permute-start.5 = (bf16[256,384]{1,0:T(8,128)(2,1)S(1)}, bf16[256,384]{1,0:T(8,128)(2,1)S(1)}, u32[]{:S(2)}, u32[]{:S(2)}) collective-permute-start(bf16[256,384]{1,0:T(8,128)(2,1)S(1)} %broadcast_select_fusion.1), channel_id=1, source_target_pairs={{0,4},{4,0},{8,12},{12,8},{16,20},{20,16},{24,28},{28,24},{1,5},{5... | collective-permute-start | bytes 589832 | tf_op jit(solution)/shard_map/ppermute | solution.py:15
  23.8 25.8 %collective-permute-start.12 = (bf16[256,384]{1,0:T(8,128)(2,1)S(1)}, bf16[256,384]{1,0:T(8,128)(2,1)S(1)}, u32[]{:S(2)}, u32[]{:S(2)}) collective-permute-start(bf16[256,384]{1,0:T(8,128)(2,1)S(1)} %broadcast_select_fusion), channel_id=1, source_target_pairs={{0,4},{4,0},{8,12},{12,8},{16,20},{20,16},{24,28},{28,24},{1,5},{5... | collective-permute-start | bytes 589832 | tf_op jit(solution)/shard_map/ppermute | solution.py:15
  25.2 12.3 %collective-permute-start = (f32[2,384]{1,0:T(2,128)S(1)}, f32[2,384]{1,0:T(2,128)S(1)}, u32[]{:S(2)}, u32[]{:S(2)}) collective-permute-start(f32[2,384]{1,0:T(2,128)S(1)} %get-tuple-element.36), channel_id=1, source_target_pairs={{0,4},{4,0},{8,12},{12,8},{16,20},{20,16},{24,28},{28,24},{1,5},{5... | collective-permute-start | bytes 9224 | tf_op jit(solution)/shard_map/ppermute | solution.py:15
  37.5 3.6 %collective-permute-start.1 = (f32[2,384]{1,0:T(2,128)S(1)}, f32[2,384]{1,0:T(2,128)S(1)}, u32[]{:S(2)}, u32[]{:S(2)}) collective-permute-start(f32[2,384]{1,0:T(2,128)S(1)} %add.19), channel_id=1, source_target_pairs={{0,8},{4,12},{8,0},{12,4},{16,24},{20,28},{24,16},{28,20},{1,9},{5... | collective-permute-start | bytes 9224 | tf_op jit(solution)/shard_map/ppermute | solution.py:15
  41.1 4.5 %collective-permute-start.2 = (f32[2,384]{1,0:T(2,128)S(1)}, f32[2,384]{1,0:T(2,128)S(1)}, u32[]{:S(2)}, u32[]{:S(2)}) collective-permute-start(f32[2,384]{1,0:T(2,128)S(1)} %add.20.sums_ref), channel_id=1, source_target_pairs={{0,16},{4,20},{8,24},{12,28},{16,0},{20,4},{24,8},{28,12},{1,17},{... | collective-permute-start | bytes 9224 | tf_op jit(solution)/shard_map/ppermute | solution.py:15
  46.9 4.0 %collective-permute-start.16 = (f16[512,256]{1,0:T(8,128)(2,1)S(1)}, f16[512,256]{1,0:T(8,128)(2,1)S(1)}, u32[]{:S(2)}, u32[]{:S(2)}) collective-permute-start(f16[512,256]{1,0:T(8,128)(2,1)S(1)} %convert_element_type.60), channel_id=1, source_target_pairs={{0,1},{1,0},{2,3},{3,2},{4,5},{5,4},{6,7},{7,6},{8,9},{9,8},{10,11... | collective-permute-start | bytes 786440 | tf_op jit(solution)/shard_map/ppermute | solution.py:15
  49.1 4.3 %collective-permute-start.9 = (f16[512,128]{1,0:T(8,128)(2,1)S(1)}, f16[512,128]{1,0:T(8,128)(2,1)S(1)}, u32[]{:S(2)}, u32[]{:S(2)}) collective-permute-start(f16[512,128]{1,0:T(8,128)(2,1)S(1)} %convert_element_type.48), channel_id=1, source_target_pairs={{0,1},{1,0},{2,3},{3,2},{4,5},{5,4},{6,7},{7,6},{8,9},{9,8},{10,11... | collective-permute-start | bytes 393224 | tf_op jit(solution)/shard_map/ppermute | solution.py:15
  50.1 2.5 %collective-permute-start.14 = (f16[512,256]{1,0:T(8,128)(2,1)S(1)}, f16[512,256]{1,0:T(8,128)(2,1)S(1)}, u32[]{:S(2)}, u32[]{:S(2)}) collective-permute-start(f16[512,256]{1,0:T(8,128)(2,1)S(1)} %convert_element_type.56), channel_id=1, source_target_pairs={{0,1},{1,0},{2,3},{3,2},{4,5},{5,4},{6,7},{7,6},{8,9},{9,8},{10,11... | collective-permute-start | bytes 786440 | tf_op jit(solution)/shard_map/ppermute | solution.py:15
  50.4 17.5 %collective-permute-start.13 = (f16[512,640]{1,0:T(8,128)(2,1)S(1)}, f16[512,640]{1,0:T(8,128)(2,1)S(1)}, u32[]{:S(2)}, u32[]{:S(2)}) collective-permute-start(f16[512,640]{1,0:T(8,128)(2,1)S(1)} %pad_maximum_fusion), channel_id=1, source_target_pairs={{0,1},{1,0},{2,3},{3,2},{4,5},{5,4},{6,7},{7,6},{8,9},{9,8},{10,11... | collective-permute-start | bytes 1966088 | tf_op jit(solution)/shard_map/ppermute | solution.py:15
  51.0 16.8 %collective-permute-start.17 = (f16[512,256]{1,0:T(8,128)(2,1)S(1)}, f16[512,256]{1,0:T(8,128)(2,1)S(1)}, u32[]{:S(2)}, u32[]{:S(2)}) collective-permute-start(f16[512,256]{1,0:T(8,128)(2,1)S(1)} %add_convert_fusion), channel_id=1, source_target_pairs={{0,2},{1,3},{2,0},{3,1},{4,6},{5,7},{6,4},{7,5},{8,10},{9,11},{10,... | collective-permute-start | bytes 786440 | tf_op jit(solution)/shard_map/ppermute | solution.py:15
  52.6 15.2 %collective-permute-start.15 = (f16[512,256]{1,0:T(8,128)(2,1)S(1)}, f16[512,256]{1,0:T(8,128)(2,1)S(1)}, u32[]{:S(2)}, u32[]{:S(2)}) collective-permute-start(f16[512,256]{1,0:T(8,128)(2,1)S(1)} %add_convert_fusion.1), channel_id=1, source_target_pairs={{0,2},{1,3},{2,0},{3,1},{4,6},{5,7},{6,4},{7,5},{8,10},{9,11},{10,... | collective-permute-start | bytes 786440 | tf_op jit(solution)/shard_map/ppermute | solution.py:15
  53.4 14.4 %collective-permute-start.10 = (f16[512,128]{1,0:T(8,128)(2,1)S(1)}, f16[512,128]{1,0:T(8,128)(2,1)S(1)}, u32[]{:S(2)}, u32[]{:S(2)}) collective-permute-start(f16[512,128]{1,0:T(8,128)(2,1)S(1)} %add_convert_fusion.2), channel_id=1, source_target_pairs={{0,2},{1,3},{2,0},{3,1},{4,6},{5,7},{6,4},{7,5},{8,10},{9,11},{10,... | collective-permute-start | bytes 393224 | tf_op jit(solution)/shard_map/ppermute | solution.py:15

commit v10 on v8

--- a/solution.py
+++ b/solution.py
@@ -51,7 +51,7 @@
 ANY = pl.BlockSpec(memory_space=pl.ANY)
 
 
-def encode_body(genotype_ref, mask_ref, whole_ref, first_ref, second_ref, sums_ref,
+def encode_body(genotype_ref, mask_ref, first_ref, second_ref, sums_ref,
                 dosage_in, mask_in, sems):
     rows = first_ref.shape[0]
     copies = []
@@ -71,7 +71,6 @@
         mask = mask_in[at, :]
         dosage = mask * dosage_in[at, :]
         calls = (dosage + mask).astype(jnp.float32).astype(jnp.bfloat16)
-        whole_ref[at, :] = calls
         part_ref[...] = calls
         totals.append([
             jnp.sum(value.astype(jnp.float32), axis=0, keepdims=True) for value in (dosage, mask)
@@ -87,9 +86,9 @@
     return pl.pallas_call(
         encode_body,
         name="encode",
-        out_shape=(calls(rows), calls(half), calls(half), jax.ShapeDtypeStruct((2, columns), jnp.float32)),
+        out_shape=(calls(half), calls(half), jax.ShapeDtypeStruct((2, columns), jnp.float32)),
         in_specs=[ANY, ANY],
-        out_specs=(VMEM,) * 4,
+        out_specs=(VMEM,) * 3,
         scratch_shapes=[
             pltpu.VMEM((rows, columns), jnp.int32),
             pltpu.VMEM((rows, columns), jnp.int32),
@@ -109,11 +108,13 @@
     return jnp.where(wide > 0.0, (wide - shift) * scale, 0.0).astype(jnp.bfloat16)
 
 
-def left_body(down, calls_ref, sums_ref, more_ref, left_ref, factors_ref):
+def left_body(down, first_ref, second_ref, sums_ref, more_ref, left_ref, factors_ref):
     shift, scale = factors(sums_ref[...] + more_ref[...])
     factors_ref[0:1, :] = shift
     factors_ref[1:2, :] = scale
-    left_ref[...] = standardized(calls_ref[...], shift, scale) * down
+    half = first_ref.shape[0]
+    for n, calls_ref in enumerate((first_ref, second_ref)):
+        left_ref[pl.ds(n * half, half), :] = standardized(calls_ref[...], shift, scale) * down
 
 
 def multiply(left, right):
@@ -174,7 +175,7 @@
     half_rows = rows // 2
     width = rows * (samples // 2 + 1) // parts
 
-    calls, first, second, sums = encode(genotype, mask)
+    first, second, sums = encode(genotype, mask)
 
     along = lambda s: (s - 2) % samples
     even = lax.axis_index("samples") % 2 == 0
@@ -197,7 +198,7 @@
 
     def source(k, h, odd):
         if k == 0:
-            return calls, h * half_rows
+            return line[0][h], 0
         if k % 2 == 0:
             return line[k // 2][h], 0
         if k == 1 and not odd:
@@ -210,7 +211,7 @@
     left, pair = call_kernel(
         functools.partial(left_body, down),
         (jax.ShapeDtypeStruct((rows, snp_part), jnp.bfloat16), jax.ShapeDtypeStruct((2, snp_part), jnp.float32)),
-        (calls, sums, more), [VMEM] * 3, 5 * rows * snp_part, 4 * rows * snp_part, out_specs=(VMEM, VMEM),
+        (first, second, sums, more), [VMEM] * 4, 5 * rows * snp_part, 4 * rows * snp_part, out_specs=(VMEM, VMEM),
     )
     count = len(table[0][0])
     quarter = half_rows // 2

time: 67.9 us -> 70.8 us (1.043)
  starting transfers between devices: 22.9 us -> 24.4 us
  waiting for transfers between devices: 36 us -> 37.5 us
    ppermute x18, starting transfers between devices: 22.9 us -> 24.4 us  [send(): lax.ppermute(value, axis, [pair for pair in pairs if pair[1] is not None])]
    ppermute x18, waiting for transfers between devices: 36 us -> 37.5 us  [send(): lax.ppermute(value, axis, [pair for pair in pairs if pair[1] is not None])]
  transfers between devices with their start and end apart: 18 -> 18, of which waited for: 6 -> 5; matrix products, arithmetic and copies ran while one was open for 1% -> 1% of each run, Pallas kernels for 5% -> 5%
where the time goes in v10:
time: 70.8 us; the launch traced here: 70.7 us
  waiting for transfers between devices  37.5 us (53%)
  starting transfers between devices  24.4 us (34%)
  Pallas kernels  7.53 us (11%)
  other arithmetic  0.83 us (1%)
    ppermute x18, waiting for transfers between devices, send(): lax.ppermute(value, axis, [pair for pair in pairs if pair[1] is not None])  37.5 us
    ppermute x18, starting transfers between devices, send(): lax.ppermute(value, axis, [pair for pair in pairs if pair[1] is not None])  24.4 us
    pallas_call x10, Pallas kernels, call_kernel(): pl.pallas_call(body, out_shape=shapes, in_specs=specs, compiler_params=pl...  6.04 us
    pallas_call x1, Pallas kernels, encode(): pl.pallas_call(encode_body, name='encode', out_shape=(calls(half), calls(...  1.49 us
  transfers between devices with their start and end apart: 18, of which 5 were waited for; matrix products, arithmetic and copies ran while one was open for 1% of the time, Pallas kernels for 5%

profile of v10, /device:TPU:0, one launch (start us, length us, event | category | flops | bytes accessed | tf_op | source)
XLA Modules:
  0.0 70.7 jit_solution(1825899812448364584)
XLA Ops:
  0.0 1.5 %encode.1 = (bf16[256,384]{1,0:T(8,128)(2,1)S(1)}, bf16[256,384]{1,0:T(8,128)(2,1)S(1)}, f32[2,384]{1,0:T(2,128)S(1)}) custom-call(s32[512,384]{1,0:T(8,128)} %genotype_ref.1, s32[512,384]{1,0:T(8,128)} %mask_ref.1), custom_call_target="tpu_custom_call" | custom-call | tf_op jit(solution)/shard_map/encode/pallas_call | solution.py:86
  1.5 5.1 %collective-permute-start.3 = (bf16[256,384]{1,0:T(8,128)(2,1)S(1)}, bf16[256,384]{1,0:T(8,128)(2,1)S(1)}, u32[]{:S(2)}, u32[]{:S(2)}) collective-permute-start(bf16[256,384]{1,0:T(8,128)(2,1)S(1)} %get-tuple-element.35.second_ref.rest_0_), channel_id=1, source_target_pairs={{0,24},{4,28},{8,0},{12,4},{16,8},{20,12},{24,16},{28,20},{1,25},{... | collective-permute-start | bytes 589832 | tf_op jit(solution)/shard_map/ppermute | solution.py:15
  6.6 0.4 collective-permute-start.6
  7.1 4.8 %collective-permute-done.3.rest_2_ = bf16[256,384]{1,0:T(8,128)(2,1)S(1)} collective-permute-done((bf16[256,384]{1,0:T(8,128)(2,1)S(1)}, bf16[256,384]{1,0:T(8,128)(2,1)S(1)}, u32[]{:S(2)}, u32[]{:S(2)}) %collective-permute-start.3) | collective-permute-done | bytes 196640 | tf_op jit(solution)/shard_map/ppermute | solution.py:15
  11.9 4.3 %collective-permute-start.4 = (bf16[256,384]{1,0:T(8,128)(2,1)S(1)}, bf16[256,384]{1,0:T(8,128)(2,1)S(1)}, u32[]{:S(2)}, u32[]{:S(2)}) collective-permute-start(bf16[256,384]{1,0:T(8,128)(2,1)S(1)} %collective-permute-done.3.rest_2_), channel_id=1, source_target_pairs={{0,24},{4,28},{8,0},{12,4},{16,8},{20,12},{24,16},{28,20},{1,25},{... | collective-permute-start | bytes 589832 | tf_op jit(solution)/shard_map/ppermute | solution.py:15
  16.2 0.0 collective-permute-done.6.rest_1_
  16.2 3.9 %collective-permute-start.11 = (bf16[256,384]{1,0:T(8,128)(2,1)S(1)}, bf16[256,384]{1,0:T(8,128)(2,1)S(1)}, u32[]{:S(2)}, u32[]{:S(2)}) collective-permute-start(bf16[256,384]{1,0:T(8,128)(2,1)S(1)} %collective-permute-done.6.rest_1_), channel_id=1, source_target_pairs={{0,24},{4,28},{8,0},{12,4},{16,8},{20,12},{24,16},{28,20},{1,25},{... | collective-permute-start | bytes 589832 | tf_op jit(solution)/shard_map/ppermute | solution.py:15
  20.1 1.5 %collective-permute-start.7 = (bf16[256,384]{1,0:T(8,128)(2,1)S(1)}, bf16[256,384]{1,0:T(8,128)(2,1)S(1)}, u32[]{:S(2)}, u32[]{:S(2)}) collective-permute-start(bf16[256,384]{1,0:T(8,128)(2,1)S(1)} %collective-permute-done.6.rest_1_), channel_id=1, source_target_pairs={{0,4},{4,0},{8,12},{12,8},{16,20},{20,16},{24,28},{28,24},{1,5},{5... | collective-permute-start | bytes 589832 | tf_op jit(solution)/shard_map/ppermute | solution.py:15
  21.6 0.5 collective-permute-start.8
  22.2 0.0 collective-permute-done.4.rest_3_
  22.2 1.6 %collective-permute-start.5 = (bf16[256,384]{1,0:T(8,128)(2,1)S(1)}, bf16[256,384]{1,0:T(8,128)(2,1)S(1)}, u32[]{:S(2)}, u32[]{:S(2)}) collective-permute-start(bf16[256,384]{1,0:T(8,128)(2,1)S(1)} %broadcast_select_fusion.1), channel_id=1, source_target_pairs={{0,4},{4,0},{8,12},{12,8},{16,20},{20,16},{24,28},{28,24},{1,5},{5... | collective-permute-start | bytes 589832 | tf_op jit(solution)/shard_map/ppermute | solution.py:15
  23.8 0.0 collective-permute-done.11.rest_0_
  23.8 1.4 %collective-permute-start.12 = (bf16[256,384]{1,0:T(8,128)(2,1)S(1)}, bf16[256,384]{1,0:T(8,128)(2,1)S(1)}, u32[]{:S(2)}, u32[]{:S(2)}) collective-permute-start(bf16[256,384]{1,0:T(8,128)(2,1)S(1)} %broadcast_select_fusion), channel_id=1, source_target_pairs={{0,4},{4,0},{8,12},{12,8},{16,20},{20,16},{24,28},{28,24},{1,5},{5... | collective-permute-start | bytes 589832 | tf_op jit(solution)/shard_map/ppermute | solution.py:15
  25.2 0.7 collective-permute-start
  25.9 11.6 %collective-permute-done = f32[2,384]{1,0:T(2,128)S(1)} collective-permute-done((f32[2,384]{1,0:T(2,128)S(1)}, f32[2,384]{1,0:T(2,128)S(1)}, u32[]{:S(2)}, u32[]{:S(2)}) %collective-permute-start) | collective-permute-done | bytes 3104 | tf_op jit(solution)/shard_map/ppermute | solution.py:15
  37.5 0.0 collective-permute-start.1
  37.5 3.6 %collective-permute-done.1 = f32[2,384]{1,0:T(2,128)S(1)} collective-permute-done((f32[2,384]{1,0:T(2,128)S(1)}, f32[2,384]{1,0:T(2,128)S(1)}, u32[]{:S(2)}, u32[]{:S(2)}) %collective-permute-start.1) | collective-permute-done | bytes 3104 | tf_op jit(solution)/shard_map/ppermute | solution.py:15
  41.1 0.0 collective-permute-start.2
  41.1 4.5 %collective-permute-done.2.more_ref = f32[2,384]{1,0:T(2,128)S(1)} collective-permute-done((f32[2,384]{1,0:T(2,128)S(1)}, f32[2,384]{1,0:T(2,128)S(1)}, u32[]{:S(2)}, u32[]{:S(2)}) %collective-permute-start.2) | collective-permute-done | bytes 3104 | tf_op jit(solution)/shard_map/ppermute | solution.py:15
  45.6 0.2 shard_map.28
  45.8 0.7 shard_map.31
  46.5 0.4 shard_map.32
  46.9 0.1 collective-permute-start.16
  47.0 0.0 collective-permute-done.7.rest_0_.rest_2_
  47.1 0.0 collective-permute-done.8.rest_1_
  47.1 0.4 shard_map.29
  47.5 0.9 %shard_map.33 = (f32[512,256]{1,0:T(8,128)S(1)}, f32[512,256]{1,0:T(8,128)S(1)}, f32[512,256]{1,0:T(8,128)S(1)}, f32[512,256]{1,0:T(8,128)S(1)}) custom-call(bf16[512,384]{1,0:T(8,128)(2,1)S(1)} %get-tuple-element.37.left_ref, f32[2,384]{1,0:T(2,128)S(1)} %get-tuple-element.38.factors_ref, bf16[256,384]{1,0:T(8,128)(2,1)S(1)} %get-tuple-element.35.second_ref.rest_0_, ...), custom_call_target="tpu_custom_call" | custom-call | flops 402653184 | bytes 524288 | tf_op jit(solution)/shard_map/pallas_call | solution.py:40
  48.4 0.0 collective-permute-done.5.rest_0_
  48.4 0.6 shard_map.30
  49.1 0.5 collective-permute-start.9
  49.6 0.0 collective-permute-done.12.rest_0_
  49.6 0.4 shard_map.34
  50.1 0.1 collective-permute-start.14
  50.2 0.2 pad_maximum_fusion
  50.4 0.5 collective-permute-start.13
  50.9 0.0 collective-permute-done.16
  50.9 0.1 add_convert_fusion
  51.0 1.5 %collective-permute-start.17 = (f16[512,256]{1,0:T(8,128)(2,1)S(1)}, f16[512,256]{1,0:T(8,128)(2,1)S(1)}, u32[]{:S(2)}, u32[]{:S(2)}) collective-permute-start(f16[512,256]{1,0:T(8,128)(2,1)S(1)} %add_convert_fusion), channel_id=1, source_target_pairs={{0,2},{1,3},{2,0},{3,1},{4,6},{5,7},{6,4},{7,5},{8,10},{9,11},{10,... | collective-permute-start | bytes 786440 | tf_op jit(solution)/shard_map/ppermute | solution.py:15
  52.5 0.0 collective-permute-done.14
  52.5 0.1 add_convert_fusion.1
  52.6 0.7 collective-permute-start.15
  53.3 0.0 collective-permute-done.9
  53.4 1.5 %collective-permute-start.10 = (f16[512,128]{1,0:T(8,128)(2,1)S(1)}, f16[512,128]{1,0:T(8,128)(2,1)S(1)}, u32[]{:S(2)}, u32[]{:S(2)}) collective-permute-start(f16[512,128]{1,0:T(8,128)(2,1)S(1)} %add_convert_fusion.2), channel_id=1, source_target_pairs={{0,2},{1,3},{2,0},{3,1},{4,6},{5,7},{6,4},{7,5},{8,10},{9,11},{10,... | collective-permute-start | bytes 393224 | tf_op jit(solution)/shard_map/ppermute | solution.py:15
  54.8 12.9 %collective-permute-done.10 = f16[512,128]{1,0:T(8,128)(2,1)S(1)} collective-permute-done((f16[512,128]{1,0:T(8,128)(2,1)S(1)}, f16[512,128]{1,0:T(8,128)(2,1)S(1)}, u32[]{:S(2)}, u32[]{:S(2)}) %collective-permute-start.10) | collective-permute-done | bytes 131104 | tf_op jit(solution)/shard_map/ppermute | solution.py:15
  67.8 0.0 collective-permute-done.17
  67.8 0.0 collective-permute-done.15
  67.9 0.0 collective-permute-done.13
  67.9 0.1 convert_element_type.55.other_ref
  68.0 0.9 %shard_map.35.rest_0_ = f32[512,640]{1,0:T(8,128)} custom-call(f32[512,256]{1,0:T(8,128)S(1)} %get-tuple-element.60.ours_ref, f32[512,256]{1,0:T(8,128)S(1)} %convert_element_type.63.got_ref, f32[512,640]{1,0:T(8,128)S(1)} %convert_element_type.55.other_ref), custom_call_target="tpu_custom_call" | custom-call | flops 131072 | bytes 524288 | tf_op jit(solution)/shard_map/pallas_call | solution.py:40
  68.9 0.9 %shard_map.36.rest_0_ = f32[512,640]{1,0:T(8,128)} custom-call(f32[512,256]{1,0:T(8,128)S(1)} %get-tuple-element.57.ours_ref, f32[512,256]{1,0:T(8,128)S(1)} %convert_element_type.59.got_ref, f32[512,640]{1,0:T(8,128)S(1)} %convert_element_type.55.other_ref, f32[512,640]{1,0:T(8,128)} %shard_map.35.rest_0_), custom_call_target="tpu_custom_call", output_to_operand_aliasing={{}: (3, {})} | custom-call | flops 131072 | bytes 524288 | tf_op jit(solution)/shard_map/pallas_call | solution.py:40
  69.8 0.8 %shard_map.37 = f32[512,640]{1,0:T(8,128)} custom-call(f32[512,128]{1,0:T(8,128)S(1)} %get-tuple-element.43.ours_ref, f32[512,128]{1,0:T(8,128)S(1)} %convert_element_type.51.got_ref, f32[512,640]{1,0:T(8,128)S(1)} %convert_element_type.55.other_ref, f32[512,640]{1,0:T(8,128)} %shard_map.36.rest_0_), custom_call_target="tpu_custom_call", output_to_operand_aliasing={{}: (3, {})} | custom-call | flops 65536 | bytes 262144 | tf_op jit(solution)/shard_map/pallas_call | solution.py:40
  (14 shorter events, 0.4 us)
Async XLA Ops:
  1.5 10.4 %collective-permute-start.3 = (bf16[256,384]{1,0:T(8,128)(2,1)S(1)}, bf16[256,384]{1,0:T(8,128)(2,1)S(1)}, u32[]{:S(2)}, u32[]{:S(2)}) collective-permute-start(bf16[256,384]{1,0:T(8,128)(2,1)S(1)} %get-tuple-element.35.second_ref.rest_0_), channel_id=1, source_target_pairs={{0,24},{4,28},{8,0},{12,4},{16,8},{20,12},{24,16},{28,20},{1,25},{... | collective-permute-start | bytes 589832 | tf_op jit(solution)/shard_map/ppermute | solution.py:15
  6.6 9.6 %collective-permute-start.6 = (bf16[256,384]{1,0:T(8,128)(2,1)S(1)}, bf16[256,384]{1,0:T(8,128)(2,1)S(1)}, u32[]{:S(2)}, u32[]{:S(2)}) collective-permute-start(bf16[256,384]{1,0:T(8,128)(2,1)S(1)} %get-tuple-element.34.first_ref.rest_0_), channel_id=1, source_target_pairs={{0,24},{4,28},{8,0},{12,4},{16,8},{20,12},{24,16},{28,20},{1,25},{... | collective-permute-start | bytes 589832 | tf_op jit(solution)/shard_map/ppermute | solution.py:15
  11.9 10.2 %collective-permute-start.4 = (bf16[256,384]{1,0:T(8,128)(2,1)S(1)}, bf16[256,384]{1,0:T(8,128)(2,1)S(1)}, u32[]{:S(2)}, u32[]{:S(2)}) collective-permute-start(bf16[256,384]{1,0:T(8,128)(2,1)S(1)} %collective-permute-done.3.rest_2_), channel_id=1, source_target_pairs={{0,24},{4,28},{8,0},{12,4},{16,8},{20,12},{24,16},{28,20},{1,25},{... | collective-permute-start | bytes 589832 | tf_op jit(solution)/shard_map/ppermute | solution.py:15
  16.2 7.6 %collective-permute-start.11 = (bf16[256,384]{1,0:T(8,128)(2,1)S(1)}, bf16[256,384]{1,0:T(8,128)(2,1)S(1)}, u32[]{:S(2)}, u32[]{:S(2)}) collective-permute-start(bf16[256,384]{1,0:T(8,128)(2,1)S(1)} %collective-permute-done.6.rest_1_), channel_id=1, source_target_pairs={{0,24},{4,28},{8,0},{12,4},{16,8},{20,12},{24,16},{28,20},{1,25},{... | collective-permute-start | bytes 589832 | tf_op jit(solution)/shard_map/ppermute | solution.py:15
  20.1 26.9 %collective-permute-start.7 = (bf16[256,384]{1,0:T(8,128)(2,1)S(1)}, bf16[256,384]{1,0:T(8,128)(2,1)S(1)}, u32[]{:S(2)}, u32[]{:S(2)}) collective-permute-start(bf16[256,384]{1,0:T(8,128)(2,1)S(1)} %collective-permute-done.6.rest_1_), channel_id=1, source_target_pairs={{0,4},{4,0},{8,12},{12,8},{16,20},{20,16},{24,28},{28,24},{1,5},{5... | collective-permute-start | bytes 589832 | tf_op jit(solution)/shard_map/ppermute | solution.py:15
  21.6 25.4 %collective-permute-start.8 = (bf16[256,384]{1,0:T(8,128)(2,1)S(1)}, bf16[256,384]{1,0:T(8,128)(2,1)S(1)}, u32[]{:S(2)}, u32[]{:S(2)}) collective-permute-start(bf16[256,384]{1,0:T(8,128)(2,1)S(1)} %collective-permute-done.3.rest_2_), channel_id=1, source_target_pairs={{0,4},{4,0},{8,12},{12,8},{16,20},{20,16},{24,28},{28,24},{1,5},{5... | collective-permute-start | bytes 589832 | tf_op jit(solution)/shard_map/ppermute | solution.py:15
  22.2 26.2 %collective-permute-start.5 = (bf16[256,384]{1,0:T(8,128)(2,1)S(1)}, bf16[256,384]{1,0:T(8,128)(2,1)S(1)}, u32[]{:S(2)}, u32[]{:S(2)}) collective-permute-start(bf16[256,384]{1,0:T(8,128)(2,1)S(1)} %broadcast_select_fusion.1), channel_id=1, source_target_pairs={{0,4},{4,0},{8,12},{12,8},{16,20},{20,16},{24,28},{28,24},{1,5},{5... | collective-permute-start | bytes 589832 | tf_op jit(solution)/shard_map/ppermute | solution.py:15
  23.8 25.8 %collective-permute-start.12 = (bf16[256,384]{1,0:T(8,128)(2,1)S(1)}, bf16[256,384]{1,0:T(8,128)(2,1)S(1)}, u32[]{:S(2)}, u32[]{:S(2)}) collective-permute-start(bf16[256,384]{1,0:T(8,128)(2,1)S(1)} %broadcast_select_fusion), channel_id=1, source_target_pairs={{0,4},{4,0},{8,12},{12,8},{16,20},{20,16},{24,28},{28,24},{1,5},{5... | collective-permute-start | bytes 589832 | tf_op jit(solution)/shard_map/ppermute | solution.py:15
  25.2 12.3 %collective-permute-start = (f32[2,384]{1,0:T(2,128)S(1)}, f32[2,384]{1,0:T(2,128)S(1)}, u32[]{:S(2)}, u32[]{:S(2)}) collective-permute-start(f32[2,384]{1,0:T(2,128)S(1)} %get-tuple-element.36), channel_id=1, source_target_pairs={{0,4},{4,0},{8,12},{12,8},{16,20},{20,16},{24,28},{28,24},{1,5},{5... | collective-permute-start | bytes 9224 | tf_op jit(solution)/shard_map/ppermute | solution.py:15
  37.5 3.6 %collective-permute-start.1 = (f32[2,384]{1,0:T(2,128)S(1)}, f32[2,384]{1,0:T(2,128)S(1)}, u32[]{:S(2)}, u32[]{:S(2)}) collective-permute-start(f32[2,384]{1,0:T(2,128)S(1)} %add.19), channel_id=1, source_target_pairs={{0,8},{4,12},{8,0},{12,4},{16,24},{20,28},{24,16},{28,20},{1,9},{5... | collective-permute-start | bytes 9224 | tf_op jit(solution)/shard_map/ppermute | solution.py:15
  41.1 4.5 %collective-permute-start.2 = (f32[2,384]{1,0:T(2,128)S(1)}, f32[2,384]{1,0:T(2,128)S(1)}, u32[]{:S(2)}, u32[]{:S(2)}) collective-permute-start(f32[2,384]{1,0:T(2,128)S(1)} %add.20.sums_ref), channel_id=1, source_target_pairs={{0,16},{4,20},{8,24},{12,28},{16,0},{20,4},{24,8},{28,12},{1,17},{... | collective-permute-start | bytes 9224 | tf_op jit(solution)/shard_map/ppermute | solution.py:15
  46.9 4.0 %collective-permute-start.16 = (f16[512,256]{1,0:T(8,128)(2,1)S(1)}, f16[512,256]{1,0:T(8,128)(2,1)S(1)}, u32[]{:S(2)}, u32[]{:S(2)}) collective-permute-start(f16[512,256]{1,0:T(8,128)(2,1)S(1)} %convert_element_type.60), channel_id=1, source_target_pairs={{0,1},{1,0},{2,3},{3,2},{4,5},{5,4},{6,7},{7,6},{8,9},{9,8},{10,11... | collective-permute-start | bytes 786440 | tf_op jit(solution)/shard_map/ppermute | solution.py:15
  49.1 4.3 %collective-permute-start.9 = (f16[512,128]{1,0:T(8,128)(2,1)S(1)}, f16[512,128]{1,0:T(8,128)(2,1)S(1)}, u32[]{:S(2)}, u32[]{:S(2)}) collective-permute-start(f16[512,128]{1,0:T(8,128)(2,1)S(1)} %convert_element_type.48), channel_id=1, source_target_pairs={{0,1},{1,0},{2,3},{3,2},{4,5},{5,4},{6,7},{7,6},{8,9},{9,8},{10,11... | collective-permute-start | bytes 393224 | tf_op jit(solution)/shard_map/ppermute | solution.py:15
  50.1 2.5 %collective-permute-start.14 = (f16[512,256]{1,0:T(8,128)(2,1)S(1)}, f16[512,256]{1,0:T(8,128)(2,1)S(1)}, u32[]{:S(2)}, u32[]{:S(2)}) collective-permute-start(f16[512,256]{1,0:T(8,128)(2,1)S(1)} %convert_element_type.56), channel_id=1, source_target_pairs={{0,1},{1,0},{2,3},{3,2},{4,5},{5,4},{6,7},{7,6},{8,9},{9,8},{10,11... | collective-permute-start | bytes 786440 | tf_op jit(solution)/shard_map/ppermute | solution.py:15
  50.4 17.5 %collective-permute-start.13 = (f16[512,640]{1,0:T(8,128)(2,1)S(1)}, f16[512,640]{1,0:T(8,128)(2,1)S(1)}, u32[]{:S(2)}, u32[]{:S(2)}) collective-permute-start(f16[512,640]{1,0:T(8,128)(2,1)S(1)} %pad_maximum_fusion), channel_id=1, source_target_pairs={{0,1},{1,0},{2,3},{3,2},{4,5},{5,4},{6,7},{7,6},{8,9},{9,8},{10,11... | collective-permute-start | bytes 1966088 | tf_op jit(solution)/shard_map/ppermute | solution.py:15
  51.0 16.8 %collective-permute-start.17 = (f16[512,256]{1,0:T(8,128)(2,1)S(1)}, f16[512,256]{1,0:T(8,128)(2,1)S(1)}, u32[]{:S(2)}, u32[]{:S(2)}) collective-permute-start(f16[512,256]{1,0:T(8,128)(2,1)S(1)} %add_convert_fusion), channel_id=1, source_target_pairs={{0,2},{1,3},{2,0},{3,1},{4,6},{5,7},{6,4},{7,5},{8,10},{9,11},{10,... | collective-permute-start | bytes 786440 | tf_op jit(solution)/shard_map/ppermute | solution.py:15
  52.6 15.2 %collective-permute-start.15 = (f16[512,256]{1,0:T(8,128)(2,1)S(1)}, f16[512,256]{1,0:T(8,128)(2,1)S(1)}, u32[]{:S(2)}, u32[]{:S(2)}) collective-permute-start(f16[512,256]{1,0:T(8,128)(2,1)S(1)} %add_convert_fusion.1), channel_id=1, source_target_pairs={{0,2},{1,3},{2,0},{3,1},{4,6},{5,7},{6,4},{7,5},{8,10},{9,11},{10,... | collective-permute-start | bytes 786440 | tf_op jit(solution)/shard_map/ppermute | solution.py:15
  53.4 14.4 %collective-permute-start.10 = (f16[512,128]{1,0:T(8,128)(2,1)S(1)}, f16[512,128]{1,0:T(8,128)(2,1)S(1)}, u32[]{:S(2)}, u32[]{:S(2)}) collective-permute-start(f16[512,128]{1,0:T(8,128)(2,1)S(1)} %add_convert_fusion.2), channel_id=1, source_target_pairs={{0,2},{1,3},{2,0},{3,1},{4,6},{5,7},{6,4},{7,5},{8,10},{9,11},{10,... | collective-permute-start | bytes 393224 | tf_op jit(solution)/shard_map/ppermute | solution.py:15
